TPU v7x, 256 devices: a 2x2x32 block of a 4x8x32 slice. The times are simulated.
256 devices in a mesh: groups: 4 (over x, y), head: 64 (over z, core).
Axes of the slice: x: 2, y: 2, z: 32, core: 2. Of those that a mesh axis runs over, the one named last changes fastest.
The devices are a block of a 4x8x32 slice.
Arguments:
- hidden_in: bfloat16 [2048, 3072], P(('groups', 'head')), parts along dimension 0, may hold values from -3 to 3
- queries: bfloat16 [2048, 6144], P(('groups', 'head')), parts along dimension 0, may hold values from -120 to 120, as said below
- keys: bfloat16 [2048, 512, 128], P(('groups', 'head')), parts along dimension 0, may hold values from -6 to 6
- values: bfloat16 [2048, 512, 128], P(('groups', 'head')), parts along dimension 0, may hold values from -6 to 6
- lengths: int32 [2048], P(('groups', 'head')), parts along dimension 0, may hold values from 1 to 64
- expert_ids: int32 [2048, 2], P('groups'), parts along dimension 0, may hold values from 0 to 3, all different within a row; in each aligned block of 8 rows (0 to 7, 8 to 15, ...) at most 6 rows name the same one
- w_out: bfloat16 [6144, 3072], P('head'), may hold values from -0.3125 to 0.3125
- norm_gain: bfloat16 [3072], replicated, may hold values from 0.5 to 1.5
- w_router: bfloat16 [3072, 4], replicated, may hold values from -0.21875 to 0.21875
- w_gate: bfloat16 [3072, 32768], P(None, 'head'), may hold values from -0.109375 to 0.109375
- w_up: bfloat16 [3072, 32768], P(None, 'head'), may hold values from -0.109375 to 0.109375
- w_down: bfloat16 [32768, 3072], P('head'), may hold values from -0.0625 to 0.0625
Outputs:
- layer_out: bfloat16 [2048, 3072], P(('groups', 'head')), parts along dimension 0
There are 4 independent parts, one for each index of `groups`. A program takes and returns all parts, laid end to end along the dimension named above; an argument that names none is the same for every part. Nothing has to cross between parts.
Inputs may be any that keep to these rules, and one draw needn't show every extreme that they name: queries and keys are within -120 and 120. `expert_ids`: each row names 2 different experts; among the rows owned by one device no expert is named more than 6 times.
All inputs are finite; a program needn't handle non-finite values.
Results may differ from a plain program's by a relative error of at most 0.0057.
Values may be sent and summed in bfloat16 or wider, within the bound.
No kernel may reach another device: no remote copies, remote signals or barrier semaphores. Data moves between devices by JAX's collectives and lax.ppermute only.
A program may use at most 64 MiB of HBM per device.

v0:
```python
import jax
import jax.numpy as jnp
from jax import lax
from jax.sharding import Mesh
from jax.sharding import PartitionSpec as P

H = 48
KV = 8
HD = 128
EXPERTS = 4
HEAD = ("head_0", "head_1")
GROUPS_HEAD = ("groups", "head_0", "head_1")


EPSILON = 1e-05


def reduced_to_own(pieces, axes, sequence):
    inside = pieces.shape[1:]
    pieces = pieces.reshape(*(lax.axis_size(a) for a in axes), *inside)
    pieces = jnp.moveaxis(pieces, sequence, range(len(axes))).reshape(-1, *inside)
    for k in sequence:
        pieces = lax.psum_scatter(pieces, axes[k], scatter_dimension=0, tiled=True)
    return pieces[0]


def in_blocks(x, dim, length):
    lengths = x.shape
    pieces = x.reshape(*lengths[:dim], length, lengths[dim] // length, *lengths[dim + 1 :])
    return jnp.moveaxis(pieces, dim, 0)


def summed_rows(x, axes, sequence, dim):
    length = lax.axis_size(axes)
    return reduced_to_own(in_blocks(x, dim, length), axes, sequence)


def rms_scale(residual, norm_gain):
    mean_square = jnp.mean(residual * residual, axis=-1, keepdims=True)
    return (residual * lax.rsqrt(mean_square + EPSILON) * norm_gain.astype(jnp.float32)).astype(
        jnp.bfloat16
    )


def gate_pair(logits, chosen_ids):
    marks = (chosen_ids[:, :, None] == jnp.arange(EXPERTS, dtype=jnp.int32)[None, None, :]).astype(
        jnp.float32
    )
    chosen = jnp.sum(logits[:, None, :] * marks, axis=-1)
    first = jax.nn.sigmoid(chosen[:, 0] - chosen[:, 1])
    return jnp.stack([first, 1.0 - first], axis=1)


def on_device(
    hidden_in,
    queries,
    keys,
    values,
    lengths,
    expert_ids,
    w_out,
    norm_gain,
    w_router,
    w_gate,
    w_up,
    w_down,
):
    members = lax.axis_size(HEAD)
    myself = lax.axis_index(HEAD)
    tok_rows, width = hidden_in.shape
    ratio = H // KV
    span = keys.shape[1] // KV
    my_queries = queries.reshape(tok_rows, KV, ratio, HD)
    my_keys = keys.reshape(tok_rows, KV, span, HD)
    my_values = values.reshape(tok_rows, KV, span, HD)
    scores = jnp.einsum(
        "bgrd,bgld->bgrl", my_queries, my_keys, preferred_element_type=jnp.float32
    ) * HD ** (-0.5)
    live = (jnp.arange(span, dtype=jnp.int32)[None, :] < lengths[:, None])[:, None, None, :]
    scores = jnp.where(live, scores, -1e30)
    peak = jnp.max(scores, axis=-1, keepdims=True)
    weights = jnp.where(live, jnp.exp(scores - peak), 0.0)
    denominator = jnp.sum(weights, axis=-1)
    numerator = jnp.einsum(
        "bgrl,bgld->bgrd",
        weights.astype(jnp.bfloat16),
        my_values,
        preferred_element_type=jnp.float32,
    )
    attended = (numerator / denominator[..., None]).reshape(tok_rows, H * HD).astype(jnp.bfloat16)
    column_block = lax.all_to_all(attended, HEAD, split_axis=1, concat_axis=0, tiled=True)
    attn_rows = summed_rows(
        jnp.dot(column_block, w_out, preferred_element_type=jnp.float32), HEAD, (1, 0), 0
    )
    residual = hidden_in.astype(jnp.float32) + attn_rows
    normed = rms_scale(residual, norm_gain)
    shards = members // EXPERTS
    my_expert = myself // shards
    piece = lax.all_gather(normed, HEAD, axis=0, tiled=True)
    gates = gate_pair(jnp.dot(piece, w_router, preferred_element_type=jnp.float32), expert_ids)
    factor = jnp.sum(gates * (expert_ids == my_expert).astype(jnp.float32), axis=1)
    gate_val = jnp.dot(piece, w_gate, preferred_element_type=jnp.float32)
    up_val = jnp.dot(piece, w_up, preferred_element_type=jnp.float32)
    hidden = (jax.nn.silu(gate_val) * up_val).astype(jnp.bfloat16)
    terms = (
        jnp.dot(hidden, w_down, preferred_element_type=jnp.float32)
        .astype(jnp.bfloat16)
        .astype(jnp.float32)
        * factor[:, None]
    )
    mixture = summed_rows(terms, HEAD, (1, 0), 0)
    return (residual + mixture).astype(jnp.bfloat16)


def solution(mesh):
    finer = Mesh(mesh.devices.reshape(mesh.shape["groups"], 32, 2), ("groups", "head_0", "head_1"))
    return jax.shard_map(
        on_device,
        mesh=finer,
        in_specs=(
            P(GROUPS_HEAD, None),
            P(GROUPS_HEAD, None),
            P(GROUPS_HEAD, None, None),
            P(GROUPS_HEAD, None, None),
            P(GROUPS_HEAD),
            P("groups", None),
            P(HEAD, None),
            P(),
            P(),
            P(None, HEAD),
            P(None, HEAD),
            P(HEAD, None),
        ),
        out_specs=P(GROUPS_HEAD, None),
        check_vma=False,
    )
```

profile of v0, /device:TPU:38, one launch (start us, length us, event | category | flops | bytes accessed | tf_op | source)
XLA Modules:
  0.0 563.9 jit_solution(2835706032654039321)
XLA Ops:
  6.5 0.0 copy-start
  6.6 0.0 reduce-scatter.5.cloned.1.call-start
  6.6 0.9 iota_compare_fusion.1
  7.4 2.0 fusion.5
  9.4 0.9 fusion.15
  10.3 1.7 fusion.6
  12.0 0.1 convert_element_type.36
  12.1 0.1 copy.31
  12.2 64.5 %all_to_all.13 = bf16[8,64,96]{2,0,1:T(8,128)(2,1)S(1)} all-to-all(bf16[8,64,96]{2,0,1:T(8,128)(2,1)S(1)} %copy.31), channel_id=1, replica_groups=mesh['groups'=4,'head_0'=32,'head_1'=2] {'head_0','head_1'}, dimensions={1} | all-to-all | bytes 196608 | tf_op jit(solution)/shard_map/all_to_all | solution.py:91
  76.7 2.0 convolution_bitcast_fusion
  78.7 3.1 copy.32
  81.8 0.1 reduce-scatter.5.cloned.1.call-update
  81.9 0.0 copy-start.6
  81.9 0.0 copy-start.3
  81.9 0.0 copy-start.4
  81.9 0.1 reduce-scatter.7.cloned.1.call-start
  82.0 13.9 %reduce-scatter.5.cloned.1.call-done = f32[32,8,3072]{2,1,0:T(8,128)} async-done(((f32[64,8,3072]{2,1,0:T(8,128)}), f32[32,8,3072]{2,1,0:T(8,128)}) %reduce-scatter.5.cloned.1.call-update) | async-done | bytes 3145744 | tf_op jit(solution)/shard_map/reduce_scatter | solution.py:23
  95.9 0.1 reduce-scatter.7.cloned.1.call-update
  95.9 0.0 copy-start.5
  96.0 0.1 all-gather.2.cloned.1.call-start
  96.0 0.0 copy-done.6
  96.0 140.1 %reduce-scatter.7.cloned.1.call-done = f32[1,8,3072]{2,1,0:T(8,128)} async-done(((f32[32,8,3072]{2,1,0:T(8,128)}), f32[1,8,3072]{2,1,0:T(8,128)}) %reduce-scatter.7.cloned.1.call-update) | async-done | bytes 98320 | tf_op jit(solution)/shard_map/reduce_scatter | solution.py:23
  236.2 0.0 copy-done.3
  236.2 1.0 multiply_reduce_fusion
  237.2 1.6 multiply_convert_fusion
  238.8 0.1 all-gather.2.cloned.1.call-update
  238.9 0.1 reduce-scatter.9.cloned.1.call-start
  239.0 129.7 %all-gather.2.cloned.1.call-done = bf16[512,3072]{1,0:T(8,128)(2,1)} async-done(((bf16[8,3072]{1,0:T(8,128)(2,1)}), bf16[512,3072]{1,0:T(8,128)(2,1)}) %all-gather.2.cloned.1.call-update) | async-done | bytes 3145744 | tf_op jit(solution)/shard_map/all_gather | solution.py:99
  368.6 0.0 copy-done.4
  368.6 0.0 copy-start.1
  368.6 2.9 fusion.17
  371.6 0.0 copy-done.5
  371.7 0.0 copy-done.1
  371.7 4.7 fusion.16
  376.4 0.0 copy-done
  376.4 9.3 %convert_multiply_fusion = f32[512,3072]{1,0:T(8,128)} fusion(bf16[512,3072]{1,0:T(8,128)(2,1)S(1)} %copy-done, f32[512]{0:T(512)S(1)} %fusion.12, bf16[512,3072]{1,0:T(8,128)(2,1)} %all-gather.2.cloned.1.call-done, bf16[3072,512]{1,0:T(8,128)(2,1)} %param.22, f32[512,512]{1,0:T(8,128)} %fusion.16), kind=kOutput, calls=%fused_computation.1 | convolution fusion | flops 3227516928 | bytes 16779264 | tf_op jit(solution)/shard_map/dot_general | solution.py:106
  385.6 6.2 %copy.33 = f32[2,32,8,3072]{3,2,1,0:T(8,128)} copy(f32[2,32,8,3072]{3,2,0,1:T(8,128)} %bitcast.44) | data formatting | bytes 12582912 | tf_op jit(solution)/shard_map/transpose | solution.py:21
  391.8 0.1 reduce-scatter.9.cloned.1.call-update
  391.9 0.0 copy-start.2
  391.9 0.1 reduce-scatter.11.cloned.1.call-start
  392.0 23.8 %reduce-scatter.9.cloned.1.call-done = f32[32,8,3072]{2,1,0:T(8,128)} async-done(((f32[64,8,3072]{2,1,0:T(8,128)}), f32[32,8,3072]{2,1,0:T(8,128)}) %reduce-scatter.9.cloned.1.call-update) | async-done | bytes 3145744 | tf_op jit(solution)/shard_map/reduce_scatter | solution.py:23
  415.8 0.1 reduce-scatter.11.cloned.1.call-update
  415.8 140.0 %reduce-scatter.11.cloned.1.call-done = f32[1,8,3072]{2,1,0:T(8,128)} async-done(((f32[32,8,3072]{2,1,0:T(8,128)}), f32[1,8,3072]{2,1,0:T(8,128)}) %reduce-scatter.11.cloned.1.call-update) | async-done | bytes 98320 | tf_op jit(solution)/shard_map/reduce_scatter | solution.py:23
  555.8 0.0 copy-done.2
  555.8 1.5 fusion.11
  (5 shorter events, 0.1 us)
Async XLA Ops:
  6.5 369.8 %copy-start = (bf16[512,3072]{1,0:T(8,128)(2,1)S(1)}, bf16[512,3072]{1,0:T(8,128)(2,1)}, u32[]{:S(2)}) copy-start(bf16[512,3072]{1,0:T(8,128)(2,1)} %param.23) | copy-start | bytes 9437188
  6.6 89.3 %reduce-scatter.5.cloned.1.call-start = ((), (), s32[]{:S(2)}) async-start(), calls=%async_computation.5 | async-start | bytes 9437184 | tf_op jit(solution)/shard_map/reduce_scatter | solution.py:23
  81.9 14.2 %copy-start.6 = (bf16[3072]{0:T(1024)(128)(2,1)S(1)}, bf16[3072]{0:T(1024)(128)(2,1)}, u32[]{:S(2)}) copy-start(bf16[3072]{0:T(1024)(128)(2,1)} %param.19) | copy-start | bytes 18436
  81.9 154.3 %copy-start.3 = (bf16[8,3072]{1,0:T(8,128)(2,1)S(1)}, bf16[8,3072]{1,0:T(8,128)(2,1)}, u32[]{:S(2)}) copy-start(bf16[8,3072]{1,0:T(8,128)(2,1)} %param.12) | copy-start | bytes 147460
  81.9 286.8 %copy-start.4 = (bf16[3072,4]{0,1:T(4,128)(2,1)S(1)}, bf16[3072,4]{0,1:T(4,128)(2,1)}, u32[]{:S(2)}) copy-start(bf16[3072,4]{0,1:T(4,128)(2,1)} %param.20) | copy-start | bytes 73732
  81.9 154.3 %reduce-scatter.7.cloned.1.call-start = ((), (), s32[]{:S(2)}) async-start(), calls=%async_computation.6 | async-start | bytes 3244032 | tf_op jit(solution)/shard_map/reduce_scatter | solution.py:23
  95.9 275.7 %copy-start.5 = (s32[512,2]{0,1:T(2,128)S(1)}, s32[512,2]{0,1:T(2,128)}, u32[]{:S(2)}) copy-start(s32[512,2]{0,1:T(2,128)} %param.17) | copy-start | bytes 12292
  96.0 272.7 %all-gather.2.cloned.1.call-start = ((), (), s32[]{:S(2)}) async-start(), calls=%async_computation.7 | async-start | bytes 3194880 | tf_op jit(solution)/shard_map/all_gather | solution.py:99
  238.9 176.9 %reduce-scatter.9.cloned.1.call-start = ((), (), s32[]{:S(2)}) async-start(), calls=%async_computation.8 | async-start | bytes 9437184 | tf_op jit(solution)/shard_map/reduce_scatter | solution.py:23
  368.6 3.0 copy-start.1
  391.9 163.9 %copy-start.2 = (f32[1,8,3072]{2,1,0:T(8,128)S(1)}, f32[1,8,3072]{2,1,0:T(8,128)}, u32[]{:S(2)}) copy-start(f32[1,8,3072]{2,1,0:T(8,128)} %reduce-scatter.7.cloned.1.call-done) | copy-start | bytes 294916
  391.9 163.9 %reduce-scatter.11.cloned.1.call-start = ((), (), s32[]{:S(2)}) async-start(), calls=%async_computation.9 | async-start | bytes 3244032 | tf_op jit(solution)/shard_map/reduce_scatter | solution.py:23
Sparse Core Ops, SparseCore 0:
  82.0 13.8 reduce-scatter.4
  98.4 137.7 reduce-scatter.6
  239.0 129.5 all-gather.1
  392.0 23.7 reduce-scatter.8
  418.2 137.5 reduce-scatter.10
where the time goes:
time: 564 us
  waiting for transfers between devices  448 us (79%)
  blocking collectives  64.5 us (11%)
  matrix products  22.6 us (4%)
  between operations  13.3 us (2%)
  local copies, waits for them, and re-layouts  9.53 us (2%)
  other arithmetic  5.98 us (1%)
    reduce_scatter x4, waiting for transfers between devices, reduced_to_own(): pieces = lax.psum_scatter(pieces, axes[k], scatter_dimension=0, tiled=True)  318 us
    all_gather x1, waiting for transfers between devices, on_device(): piece = lax.all_gather(normed, HEAD, axis=0, tiled=True)  130 us
    all_to_all x1, blocking collectives, on_device(): lax.all_to_all(attended, HEAD, split_axis=1, concat_axis=0, tiled=True)  64.5 us
  transfers between devices with their start and end apart: 5, of which 5 were waited for; matrix products, arithmetic and copies ran while one was open for 0% of the time, Pallas kernels for 0%

commit v1 on v0

v1 whole, which is shorter than its diff:
```python
import functools

import jax
import jax.numpy as jnp
from jax import lax
from jax.experimental import pallas as pl
from jax.experimental.pallas import tpu as pltpu
from jax.sharding import Mesh
from jax.sharding import PartitionSpec as P

H = 48
KV = 8
HD = 128
EXPERTS = 4
RING = "head_0"
CORE = "head_1"
HEAD = (RING, CORE)
GROUPS_HEAD = ("groups", "head_0", "head_1")


EPSILON = 1e-05


def rms_scale(residual, norm_gain):
    mean_square = jnp.mean(residual * residual, axis=-1, keepdims=True)
    return (residual * lax.rsqrt(mean_square + EPSILON) * norm_gain.astype(jnp.float32)).astype(
        jnp.bfloat16
    )


def gate_pair(logits, chosen_ids):
    marks = (chosen_ids[:, :, None] == jnp.arange(EXPERTS, dtype=jnp.int32)[None, None, :]).astype(
        jnp.float32
    )
    chosen = jnp.sum(logits[:, None, :] * marks, axis=-1)
    first = jax.nn.sigmoid(chosen[:, 0] - chosen[:, 1])
    return jnp.stack([first, 1.0 - first], axis=1)


def moved(x, distance):
    length = lax.axis_size(RING)
    return lax.ppermute(x, RING, [(i, (i + distance) % length) for i in range(length)])


def plan():
    length = lax.axis_size(RING)
    reach = (-(-length // 3)) // 2
    window = 2 * reach + 1
    assert 0 <= 3 * window - length <= 1
    return reach, window, 3 * window > length


def bundles():
    reach, window, doubled = plan()
    keys = [0] + [k for s in range(1, reach + 1) for k in (-s, s)]
    return {
        k: (k, k - window, k + window)[: 2 if doubled and k == reach else 3] for k in keys
    }


def gathered(own):
    reach, window, doubled = plan()
    rows = own.shape[0]
    behind, ahead = moved(own, window), moved(own, -window)
    right = left = jnp.concatenate([own, behind, ahead], axis=0)
    found = [right]
    for s in range(1, reach + 1):
        right = moved(right, 1)
        if doubled and s == reach:
            left = left[: 2 * rows]
        left = moved(left, -1)
        found += [right, left]
    return jnp.concatenate(found, axis=0)


def scattered(terms, rows):
    reach, window, _ = plan()
    start, at = {}, 0
    for k, offsets in bundles().items():
        start[k] = (at, at + len(offsets) * rows)
        at = start[k][1]

    def term(k):
        return lax.slice_in_dim(terms, *start[k], axis=0)

    def joined(received, own):
        rows = received.shape[0]
        if rows == own.shape[0]:
            return received.astype(jnp.float32) + own
        return jnp.concatenate([received.astype(jnp.float32) + own[:rows], own[rows:]], axis=0)

    right, left = term(reach), term(-reach)
    for s in range(reach, 0, -1):
        right_in = moved(right.astype(jnp.bfloat16), 1)
        left_in = moved(left.astype(jnp.bfloat16), -1)
        if s > 1:
            right = joined(right_in, term(s - 1))
            left = joined(left_in, term(1 - s))
    near = joined(right_in, term(0)) + left_in.astype(jnp.float32)
    from_ahead = moved(near[rows : 2 * rows].astype(jnp.bfloat16), -window)
    from_behind = moved(near[2 * rows :].astype(jnp.bfloat16), window)
    return near[:rows] + (from_ahead.astype(jnp.float32) + from_behind.astype(jnp.float32))


def experts_kernel(half, x, factor, gate, up, down, gate_too, up_too, down_too, out):
    step = pl.program_id(0)

    def add(gate_ref, up_ref, down_ref, first):
        gate_val = jnp.dot(x[...], gate_ref[...], preferred_element_type=jnp.float32)
        up_val = jnp.dot(x[...], up_ref[...], preferred_element_type=jnp.float32)
        hidden = (gate_val * jax.nn.sigmoid(gate_val) * up_val).astype(jnp.bfloat16)
        down_val = jnp.dot(hidden, down_ref[...], preferred_element_type=jnp.float32)
        out[...] = down_val if first else out[...] + down_val

    @pl.when(step == 0)
    def _():
        add(gate, up, down, True)

    @pl.when((step > 0) & (step < half))
    def _():
        add(gate, up, down, False)

    @pl.when(step >= half)
    def _():
        add(gate_too, up_too, down_too, False)

    @pl.when(step == 2 * half - 1)
    def _():
        out[...] = out[...] * factor[...]


def expert_terms(x, factor, own, partner):
    rows, width = x.shape
    units = own[0].shape[1]
    chunk = 256
    half = units // chunk
    early = lambda i: jnp.minimum(i, half - 1)
    late = lambda i: jnp.maximum(i - half, 0)

    def specs(which):
        return [
            pl.BlockSpec((width, chunk), lambda i: (0, which(i))),
            pl.BlockSpec((width, chunk), lambda i: (0, which(i))),
            pl.BlockSpec((chunk, width), lambda i: (which(i), 0)),
        ]

    return pl.pallas_call(
        functools.partial(experts_kernel, half),
        grid=(2 * half,),
        in_specs=[
            pl.BlockSpec((rows, width), lambda i: (0, 0)),
            pl.BlockSpec((rows, 1), lambda i: (0, 0)),
            *specs(early),
            *specs(late),
        ],
        out_specs=pl.BlockSpec((rows, width), lambda i: (0, 0)),
        out_shape=jax.ShapeDtypeStruct((rows, width), jnp.float32),
        compiler_params=pltpu.CompilerParams(
            dimension_semantics=("arbitrary",), vmem_limit_bytes=48 << 20
        ),
        cost_estimate=pl.CostEstimate(
            flops=12 * rows * width * units, bytes_accessed=12 * width * units, transcendentals=0
        ),
        name="experts",
    )(x, factor, *own, *partner)


def on_device(
    hidden_in,
    queries,
    keys,
    values,
    lengths,
    expert_ids,
    w_out,
    norm_gain,
    w_router,
    w_gate,
    w_up,
    w_down,
):
    length = lax.axis_size(RING)
    place = lax.axis_index(RING)
    core = lax.axis_index(CORE)
    cores = lax.axis_size(CORE)
    assert cores == 2

    def partners(x):
        return lax.ppermute(x, CORE, [(0, 1), (1, 0)])

    w_out_too = partners(w_out)
    w_gate_too, w_up_too, w_down_too = partners(w_gate), partners(w_up), partners(w_down)
    tok_rows, width = hidden_in.shape
    ratio = H // KV
    span = keys.shape[1] // KV
    my_queries = queries.reshape(tok_rows, KV, ratio, HD)
    my_keys = keys.reshape(tok_rows, KV, span, HD)
    my_values = values.reshape(tok_rows, KV, span, HD)
    scores = jnp.einsum(
        "bgrd,bgld->bgrl", my_queries, my_keys, preferred_element_type=jnp.float32
    ) * HD ** (-0.5)
    live = (jnp.arange(span, dtype=jnp.int32)[None, :] < lengths[:, None])[:, None, None, :]
    scores = jnp.where(live, scores, -1e30)
    peak = jnp.max(scores, axis=-1, keepdims=True)
    weights = jnp.where(live, jnp.exp(scores - peak), 0.0)
    denominator = jnp.sum(weights, axis=-1)
    numerator = jnp.einsum(
        "bgrl,bgld->bgrd",
        weights.astype(jnp.bfloat16),
        my_values,
        preferred_element_type=jnp.float32,
    )
    attended = (numerator / denominator[..., None]).reshape(tok_rows, H * HD).astype(jnp.bfloat16)
    column_block = lax.all_to_all(attended, RING, split_axis=1, concat_axis=0, tiled=True)

    order = [offset % length for offsets in bundles().values() for offset in offsets]
    assert sorted(order) == list(range(length))

    def in_order(x):
        x = jnp.roll(x, -place, axis=0)
        return jnp.concatenate([x[k : k + 1] for k in order], axis=0)

    column_block = in_order(column_block.reshape(length, tok_rows, -1)).reshape(
        length * tok_rows, -1
    )
    depth = w_out.shape[0]
    low, high = column_block[:, :depth], column_block[:, depth:]
    first = core == 0
    attn_terms = jnp.dot(
        jnp.where(first, low, high), w_out, preferred_element_type=jnp.float32
    ) + jnp.dot(jnp.where(first, high, low), w_out_too, preferred_element_type=jnp.float32)

    residual = hidden_in.astype(jnp.float32) + scattered(attn_terms, tok_rows)
    normed = rms_scale(residual, norm_gain)
    my_expert = place // (length // EXPERTS)
    piece = gathered(normed)
    ids = lax.dynamic_index_in_dim(
        expert_ids.reshape(length, cores, tok_rows, -1), core, axis=1, keepdims=False
    )
    ids = in_order(ids).reshape(length * tok_rows, -1)
    gates = gate_pair(jnp.dot(piece, w_router, preferred_element_type=jnp.float32), ids)
    factor = jnp.sum(gates * (ids == my_expert).astype(jnp.float32), axis=1)
    terms = expert_terms(
        piece, factor[:, None], (w_gate, w_up, w_down), (w_gate_too, w_up_too, w_down_too)
    )
    return (residual + scattered(terms, tok_rows)).astype(jnp.bfloat16)


def solution(mesh):
    cores = 2
    finer = Mesh(
        mesh.devices.reshape(mesh.shape["groups"], mesh.shape["head"] // cores, cores),
        GROUPS_HEAD,
    )
    return jax.shard_map(
        on_device,
        mesh=finer,
        in_specs=(
            P(GROUPS_HEAD, None),
            P(GROUPS_HEAD, None),
            P(GROUPS_HEAD, None, None),
            P(GROUPS_HEAD, None, None),
            P(GROUPS_HEAD),
            P("groups", None),
            P(HEAD, None),
            P(),
            P(),
            P(None, HEAD),
            P(None, HEAD),
            P(HEAD, None),
        ),
        out_specs=P(GROUPS_HEAD, None),
        check_vma=False,
    )
```

time: 564 us -> 288 us (0.51)
  waiting for transfers between devices: 448 us -> 123 us
  starting transfers between devices: 0.26 us -> 136 us
  blocking collectives: 64.5 us -> 0 us
  matrix products: 22.6 us -> 4.12 us
  between operations: 13.3 us -> 1.06 us
  Pallas kernels: 0 us -> 11 us
  local copies, waits for them, and re-layouts: 9.53 us -> 2.96 us
    reduce_scatter x4 -> x0, waiting for transfers between devices: 318 us -> none  [reduced_to_own(): pieces = lax.psum_scatter(pieces, axes[k], scatter_dimension=0, tiled=True)]
    all_gather x1 -> x0, waiting for transfers between devices: 130 us -> none  [on_device(): piece = lax.all_gather(normed, HEAD, axis=0, tiled=True)]
    ppermute x0 -> x40, starting transfers between devices: none -> 104 us  [the longest x36 103 us: moved(): lax.ppermute(x, RING, [(i, (i + distance) % length) for i in range(length)])]
    ppermute x0 -> x40, waiting for transfers between devices: none -> 92.5 us  [the longest x36 92.5 us: moved(): lax.ppermute(x, RING, [(i, (i + distance) % length) for i in range(length)])]
    all_to_all x1 -> x0, blocking collectives: 64.5 us -> none  [on_device(): lax.all_to_all(attended, HEAD, split_axis=1, concat_axis=0, tiled=True)]
    all_to_all x0 -> x1, starting transfers between devices: none -> 32.7 us  [on_device(): lax.all_to_all(attended, RING, split_axis=1, concat_axis=0, tiled=True)]
    all_to_all x0 -> x1, waiting for transfers between devices: none -> 30.7 us  [on_device(): lax.all_to_all(attended, RING, split_axis=1, concat_axis=0, tiled=True)]
    dot_general x3 -> x2, matrix products: 16 us -> 1.23 us  [the longest x1 0.62 us: on_device(): jnp.dot(jnp.where(first, high, low), w_out_too, preferred_element_type=jn...]
  transfers between devices with their start and end apart: 5 -> 41, of which waited for: 5 -> 26; matrix products, arithmetic and copies ran while one was open for 0% -> 2% of each run, Pallas kernels for 0% -> 0%
where the time goes in v1:
time: 288 us; the launch traced here: 284 us
  starting transfers between devices  136 us (47%)
  waiting for transfers between devices  123 us (43%)
  Pallas kernels  11 us (4%)
  other arithmetic  5.81 us (2%)
  matrix products  4.12 us (1%)
  local copies, waits for them, and re-layouts  2.96 us (1%)
    ppermute x36, starting transfers between devices, moved(): lax.ppermute(x, RING, [(i, (i + distance) % length) for i in range(length)])  103 us
    ppermute x36, waiting for transfers between devices, moved(): lax.ppermute(x, RING, [(i, (i + distance) % length) for i in range(length)])  92.5 us
    all_to_all x1, starting transfers between devices, on_device(): lax.all_to_all(attended, RING, split_axis=1, concat_axis=0, tiled=True)  32.7 us
    all_to_all x1, waiting for transfers between devices, on_device(): lax.all_to_all(attended, RING, split_axis=1, concat_axis=0, tiled=True)  30.7 us
    pallas_call x1, Pallas kernels, expert_terms(): pl.pallas_call(functools.partial(experts_kernel, half), grid=(2 * half,),...  11 us
  transfers between devices with their start and end apart: 41, of which 26 were waited for; matrix products, arithmetic and copies ran while one was open for 2% of the time, Pallas kernels for 0%

profile of v1, /device:TPU:38, one launch (start us, length us, event | category | flops | bytes accessed | tf_op | source)
XLA Modules:
  0.0 284.5 jit_solution(17003229865170206944)
XLA Ops:
  0.0 0.8 iota_compare_fusion.1
  0.8 1.9 fusion.4
  3.0 0.5 fusion.5
  3.6 0.7 copy.48
  4.3 32.7 %all-to-all-start = ((bf16[8,32,192]{2,0,1:T(8,128)(2,1)}), bf16[8,32,192]{2,0,1:T(8,128)(2,1)S(1)}, u32[]{:S(2)}, u32[]{:S(2)}) async-start(bf16[8,32,192]{2,0,1:T(8,128)(2,1)} %copy.48), calls=%async_computation | async-start | bytes 262144 | tf_op jit(solution)/shard_map/all_to_all | solution.py:214
  37.2 30.7 %all-to-all-done = bf16[8,32,192]{2,0,1:T(8,128)(2,1)S(1)} async-done(((bf16[8,32,192]{2,0,1:T(8,128)(2,1)}), bf16[8,32,192]{2,0,1:T(8,128)(2,1)S(1)}, u32[]{:S(2)}, u32[]{:S(2)}) %all-to-all-start) | async-done | bytes 98336 | tf_op jit(solution)/shard_map/all_to_all | solution.py:214
  68.5 0.6 fusion.31
  69.1 0.6 fusion.52
  69.8 0.3 collective-permute-start.1
  70.1 3.2 %collective-permute-start.6 = (bf16[24,3072]{1,0:T(8,128)(2,1)S(1)}, bf16[24,3072]{1,0:T(8,128)(2,1)S(1)}, u32[]{:S(2)}, u32[]{:S(2)}) collective-permute-start(bf16[24,3072]{1,0:T(8,128)(2,1)S(1)} %slice.453), channel_id=1, source_target_pairs={{0,62},{2,0},{4,2},{6,4},{8,6},{10,8},{12,10},{14,12},{16,14},{18,... | collective-permute-start | bytes 442376 | tf_op jit(solution)/shard_map/ppermute | solution.py:42
  73.3 2.5 collective-permute-done.1
  76.0 3.8 %collective-permute-start.7 = (bf16[24,3072]{1,0:T(8,128)(2,1)S(1)}, bf16[24,3072]{1,0:T(8,128)(2,1)S(1)}, u32[]{:S(2)}, u32[]{:S(2)}) collective-permute-start(bf16[24,3072]{1,0:T(8,128)(2,1)S(1)} %fusion.17), channel_id=1, source_target_pairs={{0,62},{2,0},{4,2},{6,4},{8,6},{10,8},{12,10},{14,12},{16,14},{18,... | collective-permute-start | bytes 442376 | tf_op jit(solution)/shard_map/ppermute | solution.py:42
  79.8 2.5 collective-permute-done.2
  82.3 0.9 collective-permute-done.7
  83.4 3.8 %collective-permute-start.8 = (bf16[24,3072]{1,0:T(8,128)(2,1)S(1)}, bf16[24,3072]{1,0:T(8,128)(2,1)S(1)}, u32[]{:S(2)}, u32[]{:S(2)}) collective-permute-start(bf16[24,3072]{1,0:T(8,128)(2,1)S(1)} %get-tuple-element.26), channel_id=1, source_target_pairs={{0,62},{2,0},{4,2},{6,4},{8,6},{10,8},{12,10},{14,12},{16,14},{18,... | collective-permute-start | bytes 442376 | tf_op jit(solution)/shard_map/ppermute | solution.py:42
  87.2 4.5 %collective-permute-done.3 = bf16[24,3072]{1,0:T(8,128)(2,1)S(1)} collective-permute-done((bf16[24,3072]{1,0:T(8,128)(2,1)S(1)}, bf16[24,3072]{1,0:T(8,128)(2,1)S(1)}, u32[]{:S(2)}, u32[]{:S(2)}) %collective-permute-start.3) | collective-permute-done | bytes 147488 | tf_op jit(solution)/shard_map/ppermute | solution.py:42
  92.0 3.3 %collective-permute-start.9 = (bf16[24,3072]{1,0:T(8,128)(2,1)S(1)}, bf16[24,3072]{1,0:T(8,128)(2,1)S(1)}, u32[]{:S(2)}, u32[]{:S(2)}) collective-permute-start(bf16[24,3072]{1,0:T(8,128)(2,1)S(1)} %get-tuple-element.24), channel_id=1, source_target_pairs={{0,62},{2,0},{4,2},{6,4},{8,6},{10,8},{12,10},{14,12},{16,14},{18,... | collective-permute-start | bytes 442376 | tf_op jit(solution)/shard_map/ppermute | solution.py:42
  95.2 0.5 collective-permute-start.26
  95.7 0.3 collective-permute-start.27
  96.2 2.1 collective-permute-done.4
  98.3 1.1 fusion.19
  99.5 3.4 %collective-permute-start.10 = (bf16[24,3072]{1,0:T(8,128)(2,1)S(1)}, bf16[24,3072]{1,0:T(8,128)(2,1)S(1)}, u32[]{:S(2)}, u32[]{:S(2)}) collective-permute-start(bf16[24,3072]{1,0:T(8,128)(2,1)S(1)} %get-tuple-element.22), channel_id=1, source_target_pairs={{0,62},{2,0},{4,2},{6,4},{8,6},{10,8},{12,10},{14,12},{16,14},{18,... | collective-permute-start | bytes 442376 | tf_op jit(solution)/shard_map/ppermute | solution.py:42
  103.1 2.8 collective-permute-done.5
  106.1 1.0 fusion.45
  107.2 2.5 collective-permute-start.11
  109.7 11.0 %collective-permute-start.12 = (bf16[8,3072]{1,0:T(8,128)(2,1)S(1)}, bf16[8,3072]{1,0:T(8,128)(2,1)S(1)}, u32[]{:S(2)}, u32[]{:S(2)}) collective-permute-start(bf16[8,3072]{1,0:T(8,128)(2,1)S(1)} %get-tuple-element.30), channel_id=1, source_target_pairs={{0,22},{2,24},{4,26},{6,28},{8,30},{10,32},{12,34},{14,36},{16,38}... | collective-permute-start | bytes 147464 | tf_op jit(solution)/shard_map/ppermute | solution.py:42
  120.8 7.1 %collective-permute-done.11 = bf16[8,3072]{1,0:T(8,128)(2,1)S(1)} collective-permute-done((bf16[8,3072]{1,0:T(8,128)(2,1)S(1)}, bf16[8,3072]{1,0:T(8,128)(2,1)S(1)}, u32[]{:S(2)}, u32[]{:S(2)}) %collective-permute-start.11) | collective-permute-done | bytes 49184 | tf_op jit(solution)/shard_map/ppermute | solution.py:42
  128.2 6.4 %collective-permute-start.14 = (bf16[8,3072]{1,0:T(8,128)(2,1)S(1)}, bf16[8,3072]{1,0:T(8,128)(2,1)S(1)}, u32[]{:S(2)}, u32[]{:S(2)}) collective-permute-start(bf16[8,3072]{1,0:T(8,128)(2,1)S(1)} %get-tuple-element.10), channel_id=1, source_target_pairs={{0,42},{2,44},{4,46},{6,48},{8,50},{10,52},{12,54},{14,56},{16,58}... | collective-permute-start | bytes 147464 | tf_op jit(solution)/shard_map/ppermute | solution.py:42
  134.5 7.2 %collective-permute-start.13 = (bf16[8,3072]{1,0:T(8,128)(2,1)S(1)}, bf16[8,3072]{1,0:T(8,128)(2,1)S(1)}, u32[]{:S(2)}, u32[]{:S(2)}) collective-permute-start(bf16[8,3072]{1,0:T(8,128)(2,1)S(1)} %get-tuple-element.10), channel_id=1, source_target_pairs={{0,22},{2,24},{4,26},{6,28},{8,30},{10,32},{12,34},{14,36},{16,38}... | collective-permute-start | bytes 147464 | tf_op jit(solution)/shard_map/ppermute | solution.py:42
  142.2 2.6 collective-permute-done.14
  144.8 12.5 %collective-permute-done.13 = bf16[8,3072]{1,0:T(8,128)(2,1)S(1)} collective-permute-done((bf16[8,3072]{1,0:T(8,128)(2,1)S(1)}, bf16[8,3072]{1,0:T(8,128)(2,1)S(1)}, u32[]{:S(2)}, u32[]{:S(2)}) %collective-permute-start.13) | collective-permute-done | bytes 49184 | tf_op jit(solution)/shard_map/ppermute | solution.py:42
  157.5 1.9 collective-permute-start.15
  159.4 3.8 %collective-permute-done.16 = bf16[24,3072]{1,0:T(8,128)(2,1)S(1)} collective-permute-done((bf16[24,3072]{1,0:T(8,128)(2,1)S(1)}, bf16[24,3072]{1,0:T(8,128)(2,1)S(1)}, u32[]{:S(2)}, u32[]{:S(2)}) %collective-permute-start.16) | collective-permute-done | bytes 147488 | tf_op jit(solution)/shard_map/ppermute | solution.py:42
  163.2 0.7 collective-permute-start.18
  163.9 1.7 collective-permute-start.17
  165.6 2.8 collective-permute-done.18
  168.3 3.0 %collective-permute-start.20 = (bf16[24,3072]{1,0:T(8,128)(2,1)S(1)}, bf16[24,3072]{1,0:T(8,128)(2,1)S(1)}, u32[]{:S(2)}, u32[]{:S(2)}) collective-permute-start(bf16[24,3072]{1,0:T(8,128)(2,1)S(1)} %collective-permute-done.18), channel_id=1, source_target_pairs={{0,62},{2,0},{4,2},{6,4},{8,6},{10,8},{12,10},{14,12},{16,14},{18,... | collective-permute-start | bytes 442376 | tf_op jit(solution)/shard_map/ppermute | solution.py:42
  171.3 0.6 collective-permute-start.19
  172.0 2.0 collective-permute-done.20
  174.0 3.7 %collective-permute-start.22 = (bf16[24,3072]{1,0:T(8,128)(2,1)S(1)}, bf16[24,3072]{1,0:T(8,128)(2,1)S(1)}, u32[]{:S(2)}, u32[]{:S(2)}) collective-permute-start(bf16[24,3072]{1,0:T(8,128)(2,1)S(1)} %collective-permute-done.20), channel_id=1, source_target_pairs={{0,62},{2,0},{4,2},{6,4},{8,6},{10,8},{12,10},{14,12},{16,14},{18,... | collective-permute-start | bytes 442376 | tf_op jit(solution)/shard_map/ppermute | solution.py:42
  177.7 2.6 collective-permute-done.22
  180.3 12.7 %collective-permute-start.24 = (bf16[16,3072]{1,0:T(8,128)(2,1)S(1)}, bf16[16,3072]{1,0:T(8,128)(2,1)S(1)}, u32[]{:S(2)}, u32[]{:S(2)}) collective-permute-start(bf16[16,3072]{1,0:T(8,128)(2,1)S(1)} %slice.461), channel_id=1, source_target_pairs={{0,62},{2,0},{4,2},{6,4},{8,6},{10,8},{12,10},{14,12},{16,14},{18,... | collective-permute-start | bytes 294920 | tf_op jit(solution)/shard_map/ppermute | solution.py:42
  193.1 6.3 %collective-permute-done.23 = bf16[24,3072]{1,0:T(8,128)(2,1)S(1)} collective-permute-done((bf16[24,3072]{1,0:T(8,128)(2,1)S(1)}, bf16[24,3072]{1,0:T(8,128)(2,1)S(1)}, u32[]{:S(2)}, u32[]{:S(2)}) %collective-permute-start.23) | collective-permute-done | bytes 147488 | tf_op jit(solution)/shard_map/ppermute | solution.py:42
  199.5 0.5 fusion.53
  200.0 0.5 broadcast.65
  200.5 0.7 fusion.41
  201.7 11.0 %experts.1 = f32[256,3072]{1,0:T(8,128)S(1)} custom-call(bf16[256,3072]{1,0:T(8,128)(2,1)S(1)} %constant_dynamic-update-slice_fusion.32.x, f32[256,1]{1,0:T(8,128)S(1)} %broadcast_in_dim.34.factor, bf16[3072,512]{1,0:T(8,128)(2,1)} %gate.1, bf16[3072,512]{1,0:T(8,128)(2,1)} %up.1, bf16[512,3072]{1,0:T(8,128)(2,1)} %down.1, ...), custom_call_target="tpu_custom_call" | custom-call | flops 4831838208 | bytes 18874368 | tf_op jit(solution)/shard_map/experts/pallas_call | solution.py:147
  213.1 3.3 %collective-permute-start.33 = (bf16[24,3072]{1,0:T(8,128)(2,1)S(1)}, bf16[24,3072]{1,0:T(8,128)(2,1)S(1)}, u32[]{:S(2)}, u32[]{:S(2)}) collective-permute-start(bf16[24,3072]{1,0:T(8,128)(2,1)S(1)} %slice.503), channel_id=1, source_target_pairs={{0,62},{2,0},{4,2},{6,4},{8,6},{10,8},{12,10},{14,12},{16,14},{18,... | collective-permute-start | bytes 442376 | tf_op jit(solution)/shard_map/ppermute | solution.py:42
  216.4 2.5 collective-permute-done.28
  219.4 3.8 %collective-permute-start.34 = (bf16[24,3072]{1,0:T(8,128)(2,1)S(1)}, bf16[24,3072]{1,0:T(8,128)(2,1)S(1)}, u32[]{:S(2)}, u32[]{:S(2)}) collective-permute-start(bf16[24,3072]{1,0:T(8,128)(2,1)S(1)} %fusion.9), channel_id=1, source_target_pairs={{0,62},{2,0},{4,2},{6,4},{8,6},{10,8},{12,10},{14,12},{16,14},{18,... | collective-permute-start | bytes 442376 | tf_op jit(solution)/shard_map/ppermute | solution.py:42
  223.2 2.2 collective-permute-done.29
  225.4 1.5 collective-permute-done.34
  227.1 3.8 %collective-permute-start.35 = (bf16[24,3072]{1,0:T(8,128)(2,1)S(1)}, bf16[24,3072]{1,0:T(8,128)(2,1)S(1)}, u32[]{:S(2)}, u32[]{:S(2)}) collective-permute-start(bf16[24,3072]{1,0:T(8,128)(2,1)S(1)} %get-tuple-element.20), channel_id=1, source_target_pairs={{0,62},{2,0},{4,2},{6,4},{8,6},{10,8},{12,10},{14,12},{16,14},{18,... | collective-permute-start | bytes 442376 | tf_op jit(solution)/shard_map/ppermute | solution.py:42
  230.9 3.0 %collective-permute-done.30 = bf16[24,3072]{1,0:T(8,128)(2,1)S(1)} collective-permute-done((bf16[24,3072]{1,0:T(8,128)(2,1)S(1)}, bf16[24,3072]{1,0:T(8,128)(2,1)S(1)}, u32[]{:S(2)}, u32[]{:S(2)}) %collective-permute-start.30) | collective-permute-done | bytes 147488 | tf_op jit(solution)/shard_map/ppermute | solution.py:42
  234.1 3.5 %collective-permute-start.36 = (bf16[24,3072]{1,0:T(8,128)(2,1)S(1)}, bf16[24,3072]{1,0:T(8,128)(2,1)S(1)}, u32[]{:S(2)}, u32[]{:S(2)}) collective-permute-start(bf16[24,3072]{1,0:T(8,128)(2,1)S(1)} %get-tuple-element.18), channel_id=1, source_target_pairs={{0,62},{2,0},{4,2},{6,4},{8,6},{10,8},{12,10},{14,12},{16,14},{18,... | collective-permute-start | bytes 442376 | tf_op jit(solution)/shard_map/ppermute | solution.py:42
  237.6 3.0 %collective-permute-done.31 = bf16[24,3072]{1,0:T(8,128)(2,1)S(1)} collective-permute-done((bf16[24,3072]{1,0:T(8,128)(2,1)S(1)}, bf16[24,3072]{1,0:T(8,128)(2,1)S(1)}, u32[]{:S(2)}, u32[]{:S(2)}) %collective-permute-start.31) | collective-permute-done | bytes 147488 | tf_op jit(solution)/shard_map/ppermute | solution.py:42
  240.5 4.6 %collective-permute-done.36 = bf16[24,3072]{1,0:T(8,128)(2,1)S(1)} collective-permute-done((bf16[24,3072]{1,0:T(8,128)(2,1)S(1)}, bf16[24,3072]{1,0:T(8,128)(2,1)S(1)}, u32[]{:S(2)}, u32[]{:S(2)}) %collective-permute-start.36) | collective-permute-done | bytes 147488 | tf_op jit(solution)/shard_map/ppermute | solution.py:42
  245.2 1.1 collective-permute-start.32
  246.3 2.4 collective-permute-start.37
  248.8 3.1 %collective-permute-done.32 = bf16[24,3072]{1,0:T(8,128)(2,1)S(1)} collective-permute-done((bf16[24,3072]{1,0:T(8,128)(2,1)S(1)}, bf16[24,3072]{1,0:T(8,128)(2,1)S(1)}, u32[]{:S(2)}, u32[]{:S(2)}) %collective-permute-start.32) | collective-permute-done | bytes 147488 | tf_op jit(solution)/shard_map/ppermute | solution.py:42
  251.9 14.5 %collective-permute-start.38 = (bf16[8,3072]{1,0:T(8,128)(2,1)S(1)}, bf16[8,3072]{1,0:T(8,128)(2,1)S(1)}, u32[]{:S(2)}, u32[]{:S(2)}) collective-permute-start(bf16[8,3072]{1,0:T(8,128)(2,1)S(1)} %get-tuple-element.27), channel_id=1, source_target_pairs={{0,42},{2,44},{4,46},{6,48},{8,50},{10,52},{12,54},{14,56},{16,58}... | collective-permute-start | bytes 147464 | tf_op jit(solution)/shard_map/ppermute | solution.py:42
  266.4 3.2 %collective-permute-done.38 = bf16[8,3072]{1,0:T(8,128)(2,1)S(1)} collective-permute-done((bf16[8,3072]{1,0:T(8,128)(2,1)S(1)}, bf16[8,3072]{1,0:T(8,128)(2,1)S(1)}, u32[]{:S(2)}, u32[]{:S(2)}) %collective-permute-start.38) | collective-permute-done | bytes 49184 | tf_op jit(solution)/shard_map/ppermute | solution.py:42
  269.6 14.0 %collective-permute-done.39 = bf16[8,3072]{1,0:T(8,128)(2,1)S(1)} collective-permute-done((bf16[8,3072]{1,0:T(8,128)(2,1)S(1)}, bf16[8,3072]{1,0:T(8,128)(2,1)S(1)}, u32[]{:S(2)}, u32[]{:S(2)}) %collective-permute-start.39) | collective-permute-done | bytes 49184 | tf_op jit(solution)/shard_map/ppermute | solution.py:42
  283.6 0.6 fusion.28
  (136 shorter events, 5.3 us)
Async XLA Ops:
  0.0 3.0 %copy-start = (bf16[8,512,128]{2,1,0:T(8,128)(2,1)S(1)}, bf16[8,512,128]{2,1,0:T(8,128)(2,1)}, u32[]{:S(2)}) copy-start(bf16[8,512,128]{2,1,0:T(8,128)(2,1)} %param.15) | copy-start | bytes 3145732
  2.7 34.3 %copy-start.2 = (bf16[96,3072]{1,0:T(8,128)(2,1)S(1)}, bf16[96,3072]{1,0:T(8,128)(2,1)}, u32[]{:S(2)}) copy-start(bf16[96,3072]{1,0:T(8,128)(2,1)} %param.18) | copy-start | bytes 1769476
  4.3 63.6 %all-to-all-start = ((bf16[8,32,192]{2,0,1:T(8,128)(2,1)}), bf16[8,32,192]{2,0,1:T(8,128)(2,1)S(1)}, u32[]{:S(2)}, u32[]{:S(2)}) async-start(bf16[8,32,192]{2,0,1:T(8,128)(2,1)} %copy.48), calls=%async_computation | async-start | bytes 262144 | tf_op jit(solution)/shard_map/all_to_all | solution.py:214
  37.0 32.1 %collective-permute-start = (bf16[96,3072]{1,0:T(8,128)(2,1)S(1)}, bf16[96,3072]{1,0:T(8,128)(2,1)S(1)}, u32[]{:S(2)}, u32[]{:S(2)}) collective-permute-start(bf16[96,3072]{1,0:T(8,128)(2,1)S(1)} %copy-done.2), channel_id=1, source_target_pairs={{0,1},{1,0},{2,3},{3,2},{4,5},{5,4},{6,7},{7,6},{8,9},{9,8},{10,11... | collective-permute-start | bytes 1769480 | tf_op jit(solution)/shard_map/ppermute | solution.py:189
  69.8 22.0 %copy-start.1 = (f32[256,3072]{1,0:T(8,128)}, f32[256,3072]{1,0:T(8,128)S(1)}, u32[]{:S(2)}) copy-start(f32[256,3072]{1,0:T(8,128)S(1)} %get-tuple-element.64) | copy-start | bytes 9437188
  69.8 5.9 %collective-permute-start.1 = (bf16[16,3072]{1,0:T(8,128)(2,1)S(1)}, bf16[16,3072]{1,0:T(8,128)(2,1)S(1)}, u32[]{:S(2)}, u32[]{:S(2)}) collective-permute-start(bf16[16,3072]{1,0:T(8,128)(2,1)S(1)} %slice.446), channel_id=1, source_target_pairs={{0,2},{2,4},{4,6},{6,8},{8,10},{10,12},{12,14},{14,16},{16,18},{18... | collective-permute-start | bytes 294920 | tf_op jit(solution)/shard_map/ppermute | solution.py:42
  70.1 5.9 %collective-permute-start.6 = (bf16[24,3072]{1,0:T(8,128)(2,1)S(1)}, bf16[24,3072]{1,0:T(8,128)(2,1)S(1)}, u32[]{:S(2)}, u32[]{:S(2)}) collective-permute-start(bf16[24,3072]{1,0:T(8,128)(2,1)S(1)} %slice.453), channel_id=1, source_target_pairs={{0,62},{2,0},{4,2},{6,4},{8,6},{10,8},{12,10},{14,12},{16,14},{18,... | collective-permute-start | bytes 442376 | tf_op jit(solution)/shard_map/ppermute | solution.py:42
  75.8 20.3 %copy-start.6 = (s32[512,2]{0,1:T(2,128)S(1)}, s32[512,2]{0,1:T(2,128)}, u32[]{:S(2)}) copy-start(s32[512,2]{0,1:T(2,128)} %param.17) | copy-start | bytes 12292
  75.8 6.5 %collective-permute-start.2 = (bf16[24,3072]{1,0:T(8,128)(2,1)S(1)}, bf16[24,3072]{1,0:T(8,128)(2,1)S(1)}, u32[]{:S(2)}, u32[]{:S(2)}) collective-permute-start(bf16[24,3072]{1,0:T(8,128)(2,1)S(1)} %pad_maximum_fusion), channel_id=1, source_target_pairs={{0,2},{2,4},{4,6},{6,8},{8,10},{10,12},{12,14},{14,16},{16,18},{18... | collective-permute-start | bytes 442376 | tf_op jit(solution)/shard_map/ppermute | solution.py:42
  76.0 7.2 %collective-permute-start.7 = (bf16[24,3072]{1,0:T(8,128)(2,1)S(1)}, bf16[24,3072]{1,0:T(8,128)(2,1)S(1)}, u32[]{:S(2)}, u32[]{:S(2)}) collective-permute-start(bf16[24,3072]{1,0:T(8,128)(2,1)S(1)} %fusion.17), channel_id=1, source_target_pairs={{0,62},{2,0},{4,2},{6,4},{8,6},{10,8},{12,10},{14,12},{16,14},{18,... | collective-permute-start | bytes 442376 | tf_op jit(solution)/shard_map/ppermute | solution.py:42
  83.2 8.5 %collective-permute-start.3 = (bf16[24,3072]{1,0:T(8,128)(2,1)S(1)}, bf16[24,3072]{1,0:T(8,128)(2,1)S(1)}, u32[]{:S(2)}, u32[]{:S(2)}) collective-permute-start(bf16[24,3072]{1,0:T(8,128)(2,1)S(1)} %get-tuple-element.25), channel_id=1, source_target_pairs={{0,2},{2,4},{4,6},{6,8},{8,10},{10,12},{12,14},{14,16},{16,18},{18... | collective-permute-start | bytes 442376 | tf_op jit(solution)/shard_map/ppermute | solution.py:42
  83.4 8.3 %collective-permute-start.8 = (bf16[24,3072]{1,0:T(8,128)(2,1)S(1)}, bf16[24,3072]{1,0:T(8,128)(2,1)S(1)}, u32[]{:S(2)}, u32[]{:S(2)}) collective-permute-start(bf16[24,3072]{1,0:T(8,128)(2,1)S(1)} %get-tuple-element.26), channel_id=1, source_target_pairs={{0,62},{2,0},{4,2},{6,4},{8,6},{10,8},{12,10},{14,12},{16,14},{18,... | collective-permute-start | bytes 442376 | tf_op jit(solution)/shard_map/ppermute | solution.py:42
  91.8 29.0 %copy-start.5 = (bf16[3072]{0:T(1024)(128)(2,1)S(1)}, bf16[3072]{0:T(1024)(128)(2,1)}, u32[]{:S(2)}) copy-start(bf16[3072]{0:T(1024)(128)(2,1)} %param.19) | copy-start | bytes 18436
  91.8 36.1 %copy-start.3 = (bf16[8,3072]{1,0:T(8,128)(2,1)S(1)}, bf16[8,3072]{1,0:T(8,128)(2,1)}, u32[]{:S(2)}) copy-start(bf16[8,3072]{1,0:T(8,128)(2,1)} %param.12) | copy-start | bytes 147460
  91.8 6.5 %collective-permute-start.4 = (bf16[24,3072]{1,0:T(8,128)(2,1)S(1)}, bf16[24,3072]{1,0:T(8,128)(2,1)S(1)}, u32[]{:S(2)}, u32[]{:S(2)}) collective-permute-start(bf16[24,3072]{1,0:T(8,128)(2,1)S(1)} %get-tuple-element.23), channel_id=1, source_target_pairs={{0,2},{2,4},{4,6},{6,8},{8,10},{10,12},{12,14},{14,16},{16,18},{18... | collective-permute-start | bytes 442376 | tf_op jit(solution)/shard_map/ppermute | solution.py:42
  92.0 6.3 %collective-permute-start.9 = (bf16[24,3072]{1,0:T(8,128)(2,1)S(1)}, bf16[24,3072]{1,0:T(8,128)(2,1)S(1)}, u32[]{:S(2)}, u32[]{:S(2)}) collective-permute-start(bf16[24,3072]{1,0:T(8,128)(2,1)S(1)} %get-tuple-element.24), channel_id=1, source_target_pairs={{0,62},{2,0},{4,2},{6,4},{8,6},{10,8},{12,10},{14,12},{16,14},{18,... | collective-permute-start | bytes 442376 | tf_op jit(solution)/shard_map/ppermute | solution.py:42
  95.2 106.5 %collective-permute-start.25 = (bf16[3072,512]{1,0:T(8,128)(2,1)}, bf16[3072,512]{1,0:T(8,128)(2,1)}, u32[]{:S(2)}, u32[]{:S(2)}) collective-permute-start(bf16[3072,512]{1,0:T(8,128)(2,1)} %gate.1), channel_id=1, source_target_pairs={{0,1},{1,0},{2,3},{3,2},{4,5},{5,4},{6,7},{7,6},{8,9},{9,8},{10,11... | collective-permute-start | bytes 9437192 | tf_op jit(solution)/shard_map/ppermute | solution.py:189
  95.2 106.5 %collective-permute-start.26 = (bf16[3072,512]{1,0:T(8,128)(2,1)}, bf16[3072,512]{1,0:T(8,128)(2,1)}, u32[]{:S(2)}, u32[]{:S(2)}) collective-permute-start(bf16[3072,512]{1,0:T(8,128)(2,1)} %up.1), channel_id=1, source_target_pairs={{0,1},{1,0},{2,3},{3,2},{4,5},{5,4},{6,7},{7,6},{8,9},{9,8},{10,11... | collective-permute-start | bytes 9437192 | tf_op jit(solution)/shard_map/ppermute | solution.py:189
  95.7 106.0 %collective-permute-start.27 = (bf16[512,3072]{1,0:T(8,128)(2,1)}, bf16[512,3072]{1,0:T(8,128)(2,1)}, u32[]{:S(2)}, u32[]{:S(2)}) collective-permute-start(bf16[512,3072]{1,0:T(8,128)(2,1)} %down.1), channel_id=1, source_target_pairs={{0,1},{1,0},{2,3},{3,2},{4,5},{5,4},{6,7},{7,6},{8,9},{9,8},{10,11... | collective-permute-start | bytes 9437192 | tf_op jit(solution)/shard_map/ppermute | solution.py:189
  99.4 6.5 %collective-permute-start.5 = (bf16[24,3072]{1,0:T(8,128)(2,1)S(1)}, bf16[24,3072]{1,0:T(8,128)(2,1)S(1)}, u32[]{:S(2)}, u32[]{:S(2)}) collective-permute-start(bf16[24,3072]{1,0:T(8,128)(2,1)S(1)} %get-tuple-element.21), channel_id=1, source_target_pairs={{0,2},{2,4},{4,6},{6,8},{8,10},{10,12},{12,14},{14,16},{16,18},{18... | collective-permute-start | bytes 442376 | tf_op jit(solution)/shard_map/ppermute | solution.py:42
  99.5 6.6 %collective-permute-start.10 = (bf16[24,3072]{1,0:T(8,128)(2,1)S(1)}, bf16[24,3072]{1,0:T(8,128)(2,1)S(1)}, u32[]{:S(2)}, u32[]{:S(2)}) collective-permute-start(bf16[24,3072]{1,0:T(8,128)(2,1)S(1)} %get-tuple-element.22), channel_id=1, source_target_pairs={{0,62},{2,0},{4,2},{6,4},{8,6},{10,8},{12,10},{14,12},{16,14},{18,... | collective-permute-start | bytes 442376 | tf_op jit(solution)/shard_map/ppermute | solution.py:42
  107.2 20.8 %collective-permute-start.11 = (bf16[8,3072]{1,0:T(8,128)(2,1)S(1)}, bf16[8,3072]{1,0:T(8,128)(2,1)S(1)}, u32[]{:S(2)}, u32[]{:S(2)}) collective-permute-start(bf16[8,3072]{1,0:T(8,128)(2,1)S(1)} %get-tuple-element.29), channel_id=1, source_target_pairs={{0,42},{2,44},{4,46},{6,48},{8,50},{10,52},{12,54},{14,56},{16,58}... | collective-permute-start | bytes 147464 | tf_op jit(solution)/shard_map/ppermute | solution.py:42
  109.7 18.2 %collective-permute-start.12 = (bf16[8,3072]{1,0:T(8,128)(2,1)S(1)}, bf16[8,3072]{1,0:T(8,128)(2,1)S(1)}, u32[]{:S(2)}, u32[]{:S(2)}) collective-permute-start(bf16[8,3072]{1,0:T(8,128)(2,1)S(1)} %get-tuple-element.30), channel_id=1, source_target_pairs={{0,22},{2,24},{4,26},{6,28},{8,30},{10,32},{12,34},{14,36},{16,38}... | collective-permute-start | bytes 147464 | tf_op jit(solution)/shard_map/ppermute | solution.py:42
  128.2 16.6 %collective-permute-start.14 = (bf16[8,3072]{1,0:T(8,128)(2,1)S(1)}, bf16[8,3072]{1,0:T(8,128)(2,1)S(1)}, u32[]{:S(2)}, u32[]{:S(2)}) collective-permute-start(bf16[8,3072]{1,0:T(8,128)(2,1)S(1)} %get-tuple-element.10), channel_id=1, source_target_pairs={{0,42},{2,44},{4,46},{6,48},{8,50},{10,52},{12,54},{14,56},{16,58}... | collective-permute-start | bytes 147464 | tf_op jit(solution)/shard_map/ppermute | solution.py:42
  134.5 22.7 %collective-permute-start.13 = (bf16[8,3072]{1,0:T(8,128)(2,1)S(1)}, bf16[8,3072]{1,0:T(8,128)(2,1)S(1)}, u32[]{:S(2)}, u32[]{:S(2)}) collective-permute-start(bf16[8,3072]{1,0:T(8,128)(2,1)S(1)} %get-tuple-element.10), channel_id=1, source_target_pairs={{0,22},{2,24},{4,26},{6,28},{8,30},{10,32},{12,34},{14,36},{16,38}... | collective-permute-start | bytes 147464 | tf_op jit(solution)/shard_map/ppermute | solution.py:42
  157.3 5.9 %collective-permute-start.16 = (bf16[24,3072]{1,0:T(8,128)(2,1)S(1)}, bf16[24,3072]{1,0:T(8,128)(2,1)S(1)}, u32[]{:S(2)}, u32[]{:S(2)}) collective-permute-start(bf16[24,3072]{1,0:T(8,128)(2,1)S(1)} %pad_maximum_fusion.1), channel_id=1, source_target_pairs={{0,62},{2,0},{4,2},{6,4},{8,6},{10,8},{12,10},{14,12},{16,14},{18,... | collective-permute-start | bytes 442376 | tf_op jit(solution)/shard_map/ppermute | solution.py:42
  157.5 6.4 %collective-permute-start.15 = (bf16[24,3072]{1,0:T(8,128)(2,1)S(1)}, bf16[24,3072]{1,0:T(8,128)(2,1)S(1)}, u32[]{:S(2)}, u32[]{:S(2)}) collective-permute-start(bf16[24,3072]{1,0:T(8,128)(2,1)S(1)} %pad_maximum_fusion.1), channel_id=1, source_target_pairs={{0,2},{2,4},{4,6},{6,8},{8,10},{10,12},{12,14},{14,16},{16,18},{18... | collective-permute-start | bytes 442376 | tf_op jit(solution)/shard_map/ppermute | solution.py:42
  159.4 40.0 %copy-start.4 = (bf16[3072,4]{0,1:T(4,128)(2,1)S(1)}, bf16[3072,4]{0,1:T(4,128)(2,1)}, u32[]{:S(2)}) copy-start(bf16[3072,4]{0,1:T(4,128)(2,1)} %param.20) | copy-start | bytes 73732
  163.2 5.1 %collective-permute-start.18 = (bf16[24,3072]{1,0:T(8,128)(2,1)S(1)}, bf16[24,3072]{1,0:T(8,128)(2,1)S(1)}, u32[]{:S(2)}, u32[]{:S(2)}) collective-permute-start(bf16[24,3072]{1,0:T(8,128)(2,1)S(1)} %collective-permute-done.16), channel_id=1, source_target_pairs={{0,62},{2,0},{4,2},{6,4},{8,6},{10,8},{12,10},{14,12},{16,14},{18,... | collective-permute-start | bytes 442376 | tf_op jit(solution)/shard_map/ppermute | solution.py:42
  163.9 7.4 %collective-permute-start.17 = (bf16[24,3072]{1,0:T(8,128)(2,1)S(1)}, bf16[24,3072]{1,0:T(8,128)(2,1)S(1)}, u32[]{:S(2)}, u32[]{:S(2)}) collective-permute-start(bf16[24,3072]{1,0:T(8,128)(2,1)S(1)} %collective-permute-done.15), channel_id=1, source_target_pairs={{0,2},{2,4},{4,6},{6,8},{8,10},{10,12},{12,14},{14,16},{16,18},{18... | collective-permute-start | bytes 442376 | tf_op jit(solution)/shard_map/ppermute | solution.py:42
  168.3 5.6 %collective-permute-start.20 = (bf16[24,3072]{1,0:T(8,128)(2,1)S(1)}, bf16[24,3072]{1,0:T(8,128)(2,1)S(1)}, u32[]{:S(2)}, u32[]{:S(2)}) collective-permute-start(bf16[24,3072]{1,0:T(8,128)(2,1)S(1)} %collective-permute-done.18), channel_id=1, source_target_pairs={{0,62},{2,0},{4,2},{6,4},{8,6},{10,8},{12,10},{14,12},{16,14},{18,... | collective-permute-start | bytes 442376 | tf_op jit(solution)/shard_map/ppermute | solution.py:42
  171.3 6.4 %collective-permute-start.19 = (bf16[24,3072]{1,0:T(8,128)(2,1)S(1)}, bf16[24,3072]{1,0:T(8,128)(2,1)S(1)}, u32[]{:S(2)}, u32[]{:S(2)}) collective-permute-start(bf16[24,3072]{1,0:T(8,128)(2,1)S(1)} %collective-permute-done.17), channel_id=1, source_target_pairs={{0,2},{2,4},{4,6},{6,8},{8,10},{10,12},{12,14},{14,16},{16,18},{18... | collective-permute-start | bytes 442376 | tf_op jit(solution)/shard_map/ppermute | solution.py:42
  174.0 6.4 %collective-permute-start.22 = (bf16[24,3072]{1,0:T(8,128)(2,1)S(1)}, bf16[24,3072]{1,0:T(8,128)(2,1)S(1)}, u32[]{:S(2)}, u32[]{:S(2)}) collective-permute-start(bf16[24,3072]{1,0:T(8,128)(2,1)S(1)} %collective-permute-done.20), channel_id=1, source_target_pairs={{0,62},{2,0},{4,2},{6,4},{8,6},{10,8},{12,10},{14,12},{16,14},{18,... | collective-permute-start | bytes 442376 | tf_op jit(solution)/shard_map/ppermute | solution.py:42
  177.6 15.4 %collective-permute-start.21 = (bf16[24,3072]{1,0:T(8,128)(2,1)S(1)}, bf16[24,3072]{1,0:T(8,128)(2,1)S(1)}, u32[]{:S(2)}, u32[]{:S(2)}) collective-permute-start(bf16[24,3072]{1,0:T(8,128)(2,1)S(1)} %collective-permute-done.19), channel_id=1, source_target_pairs={{0,2},{2,4},{4,6},{6,8},{8,10},{10,12},{12,14},{14,16},{16,18},{18... | collective-permute-start | bytes 442376 | tf_op jit(solution)/shard_map/ppermute | solution.py:42
  180.3 19.1 %collective-permute-start.24 = (bf16[16,3072]{1,0:T(8,128)(2,1)S(1)}, bf16[16,3072]{1,0:T(8,128)(2,1)S(1)}, u32[]{:S(2)}, u32[]{:S(2)}) collective-permute-start(bf16[16,3072]{1,0:T(8,128)(2,1)S(1)} %slice.461), channel_id=1, source_target_pairs={{0,62},{2,0},{4,2},{6,4},{8,6},{10,8},{12,10},{14,12},{16,14},{18,... | collective-permute-start | bytes 294920 | tf_op jit(solution)/shard_map/ppermute | solution.py:42
  193.1 6.4 %collective-permute-start.23 = (bf16[24,3072]{1,0:T(8,128)(2,1)S(1)}, bf16[24,3072]{1,0:T(8,128)(2,1)S(1)}, u32[]{:S(2)}, u32[]{:S(2)}) collective-permute-start(bf16[24,3072]{1,0:T(8,128)(2,1)S(1)} %collective-permute-done.21), channel_id=1, source_target_pairs={{0,2},{2,4},{4,6},{6,8},{8,10},{10,12},{12,14},{14,16},{16,18},{18... | collective-permute-start | bytes 442376 | tf_op jit(solution)/shard_map/ppermute | solution.py:42
  213.0 5.9 %collective-permute-start.28 = (bf16[16,3072]{1,0:T(8,128)(2,1)S(1)}, bf16[16,3072]{1,0:T(8,128)(2,1)S(1)}, u32[]{:S(2)}, u32[]{:S(2)}) collective-permute-start(bf16[16,3072]{1,0:T(8,128)(2,1)S(1)} %slice.496), channel_id=1, source_target_pairs={{0,2},{2,4},{4,6},{6,8},{8,10},{10,12},{12,14},{14,16},{16,18},{18... | collective-permute-start | bytes 294920 | tf_op jit(solution)/shard_map/ppermute | solution.py:42
  213.1 6.2 %collective-permute-start.33 = (bf16[24,3072]{1,0:T(8,128)(2,1)S(1)}, bf16[24,3072]{1,0:T(8,128)(2,1)S(1)}, u32[]{:S(2)}, u32[]{:S(2)}) collective-permute-start(bf16[24,3072]{1,0:T(8,128)(2,1)S(1)} %slice.503), channel_id=1, source_target_pairs={{0,62},{2,0},{4,2},{6,4},{8,6},{10,8},{12,10},{14,12},{16,14},{18,... | collective-permute-start | bytes 442376 | tf_op jit(solution)/shard_map/ppermute | solution.py:42
  218.9 6.5 %collective-permute-start.29 = (bf16[24,3072]{1,0:T(8,128)(2,1)S(1)}, bf16[24,3072]{1,0:T(8,128)(2,1)S(1)}, u32[]{:S(2)}, u32[]{:S(2)}) collective-permute-start(bf16[24,3072]{1,0:T(8,128)(2,1)S(1)} %pad_maximum_fusion.2), channel_id=1, source_target_pairs={{0,2},{2,4},{4,6},{6,8},{8,10},{10,12},{12,14},{14,16},{16,18},{18... | collective-permute-start | bytes 442376 | tf_op jit(solution)/shard_map/ppermute | solution.py:42
  219.4 7.5 %collective-permute-start.34 = (bf16[24,3072]{1,0:T(8,128)(2,1)S(1)}, bf16[24,3072]{1,0:T(8,128)(2,1)S(1)}, u32[]{:S(2)}, u32[]{:S(2)}) collective-permute-start(bf16[24,3072]{1,0:T(8,128)(2,1)S(1)} %fusion.9), channel_id=1, source_target_pairs={{0,62},{2,0},{4,2},{6,4},{8,6},{10,8},{12,10},{14,12},{16,14},{18,... | collective-permute-start | bytes 442376 | tf_op jit(solution)/shard_map/ppermute | solution.py:42
  226.9 6.9 %collective-permute-start.30 = (bf16[24,3072]{1,0:T(8,128)(2,1)S(1)}, bf16[24,3072]{1,0:T(8,128)(2,1)S(1)}, u32[]{:S(2)}, u32[]{:S(2)}) collective-permute-start(bf16[24,3072]{1,0:T(8,128)(2,1)S(1)} %get-tuple-element.19), channel_id=1, source_target_pairs={{0,2},{2,4},{4,6},{6,8},{8,10},{10,12},{12,14},{14,16},{16,18},{18... | collective-permute-start | bytes 442376 | tf_op jit(solution)/shard_map/ppermute | solution.py:42
  227.1 6.8 %collective-permute-start.35 = (bf16[24,3072]{1,0:T(8,128)(2,1)S(1)}, bf16[24,3072]{1,0:T(8,128)(2,1)S(1)}, u32[]{:S(2)}, u32[]{:S(2)}) collective-permute-start(bf16[24,3072]{1,0:T(8,128)(2,1)S(1)} %get-tuple-element.20), channel_id=1, source_target_pairs={{0,62},{2,0},{4,2},{6,4},{8,6},{10,8},{12,10},{14,12},{16,14},{18,... | collective-permute-start | bytes 442376 | tf_op jit(solution)/shard_map/ppermute | solution.py:42
  233.9 6.6 %collective-permute-start.31 = (bf16[24,3072]{1,0:T(8,128)(2,1)S(1)}, bf16[24,3072]{1,0:T(8,128)(2,1)S(1)}, u32[]{:S(2)}, u32[]{:S(2)}) collective-permute-start(bf16[24,3072]{1,0:T(8,128)(2,1)S(1)} %get-tuple-element.17), channel_id=1, source_target_pairs={{0,2},{2,4},{4,6},{6,8},{8,10},{10,12},{12,14},{14,16},{16,18},{18... | collective-permute-start | bytes 442376 | tf_op jit(solution)/shard_map/ppermute | solution.py:42
  234.1 11.0 %collective-permute-start.36 = (bf16[24,3072]{1,0:T(8,128)(2,1)S(1)}, bf16[24,3072]{1,0:T(8,128)(2,1)S(1)}, u32[]{:S(2)}, u32[]{:S(2)}) collective-permute-start(bf16[24,3072]{1,0:T(8,128)(2,1)S(1)} %get-tuple-element.18), channel_id=1, source_target_pairs={{0,62},{2,0},{4,2},{6,4},{8,6},{10,8},{12,10},{14,12},{16,14},{18,... | collective-permute-start | bytes 442376 | tf_op jit(solution)/shard_map/ppermute | solution.py:42
  245.2 6.7 %collective-permute-start.32 = (bf16[24,3072]{1,0:T(8,128)(2,1)S(1)}, bf16[24,3072]{1,0:T(8,128)(2,1)S(1)}, u32[]{:S(2)}, u32[]{:S(2)}) collective-permute-start(bf16[24,3072]{1,0:T(8,128)(2,1)S(1)} %get-tuple-element.15), channel_id=1, source_target_pairs={{0,2},{2,4},{4,6},{6,8},{8,10},{10,12},{12,14},{14,16},{16,18},{18... | collective-permute-start | bytes 442376 | tf_op jit(solution)/shard_map/ppermute | solution.py:42
  246.3 5.5 %collective-permute-start.37 = (bf16[24,3072]{1,0:T(8,128)(2,1)S(1)}, bf16[24,3072]{1,0:T(8,128)(2,1)S(1)}, u32[]{:S(2)}, u32[]{:S(2)}) collective-permute-start(bf16[24,3072]{1,0:T(8,128)(2,1)S(1)} %get-tuple-element.16), channel_id=1, source_target_pairs={{0,62},{2,0},{4,2},{6,4},{8,6},{10,8},{12,10},{14,12},{16,14},{18,... | collective-permute-start | bytes 442376 | tf_op jit(solution)/shard_map/ppermute | solution.py:42
  251.9 17.6 %collective-permute-start.38 = (bf16[8,3072]{1,0:T(8,128)(2,1)S(1)}, bf16[8,3072]{1,0:T(8,128)(2,1)S(1)}, u32[]{:S(2)}, u32[]{:S(2)}) collective-permute-start(bf16[8,3072]{1,0:T(8,128)(2,1)S(1)} %get-tuple-element.27), channel_id=1, source_target_pairs={{0,42},{2,44},{4,46},{6,48},{8,50},{10,52},{12,54},{14,56},{16,58}... | collective-permute-start | bytes 147464 | tf_op jit(solution)/shard_map/ppermute | solution.py:42
  266.4 17.2 %collective-permute-start.39 = (bf16[8,3072]{1,0:T(8,128)(2,1)S(1)}, bf16[8,3072]{1,0:T(8,128)(2,1)S(1)}, u32[]{:S(2)}, u32[]{:S(2)}) collective-permute-start(bf16[8,3072]{1,0:T(8,128)(2,1)S(1)} %get-tuple-element.28), channel_id=1, source_target_pairs={{0,22},{2,24},{4,26},{6,28},{8,30},{10,32},{12,34},{14,36},{16,38}... | collective-permute-start | bytes 147464 | tf_op jit(solution)/shard_map/ppermute | solution.py:42

commit v2 on v1

--- a/solution.py
+++ b/solution.py
@@ -19,6 +19,79 @@
 
 
 EPSILON = 1e-05
+WEIGHT_REACH = 2
+
+
+def outward(x):
+    length = lax.axis_size(RING)
+    pairs = [(2 * i, 2 * ((i - 1) % length)) for i in range(length)]
+    pairs += [(2 * i + 1, 2 * ((i + 1) % length) + 1) for i in range(length)]
+    return lax.ppermute(x, HEAD, pairs)
+
+
+def projected(attended, w_out, slab):
+    length = lax.axis_size(RING)
+    place = lax.axis_index(RING)
+    first = lax.axis_index(CORE) == 0
+    rows = attended.shape[0]
+    chip_depth = attended.shape[1] // length
+    stride = 2 * WEIGHT_REACH + 1
+    steps = -(-length // stride) // 2
+    assert stride * (2 * steps + 1) >= length and steps >= WEIGHT_REACH
+
+    doubled = jnp.concatenate([attended, attended], axis=1)
+    turned = lax.dynamic_slice_in_dim(doubled, place * chip_depth, length * chip_depth, axis=1)
+    taken, stretch = set(), {}
+    for k in sorted(range(-steps, steps + 1), key=abs):
+        pieces = []
+        for n in range(-WEIGHT_REACH, WEIGHT_REACH + 1):
+            chip = (k * stride + n) % length
+            part = turned[:, chip * chip_depth : (chip + 1) * chip_depth]
+            pieces.append(jnp.zeros_like(part) if chip in taken else part)
+            taken.add(chip)
+        stretch[k] = jnp.concatenate(pieces, axis=1)
+    assert len(taken) == length
+    right = jnp.concatenate([stretch[k] for k in range(1, steps + 1)], axis=0)
+    left = jnp.concatenate([stretch[-k] for k in range(1, steps + 1)], axis=0)
+    found = {0: stretch[0]}
+    mine, theirs = [outward(slab)], []
+    for k in range(1, steps + 1):
+        right, left = moved(right, stride), moved(left, -stride)
+        found[-k], found[k] = right[:rows], left[:rows]
+        if k < WEIGHT_REACH:
+            ready, _, _ = lax.optimization_barrier((mine[-1], right, left))
+            mine.append(outward(ready))
+            theirs.append(partner_of(ready))
+        elif k == WEIGHT_REACH:
+            theirs.append(partner_of(mine[-1]))
+        right, left = right[rows:], left[rows:]
+    order = range(-steps, steps + 1)
+    block = jnp.concatenate([found[k] for k in order], axis=0)
+
+    def columns(n):
+        n += WEIGHT_REACH
+        return block[:, n * chip_depth : (n + 1) * chip_depth]
+
+    def product(x, w):
+        return jnp.dot(x, w, preferred_element_type=jnp.float32)
+
+    terms = product(columns(0), slab)
+    for n in range(1, WEIGHT_REACH + 1):
+        terms += product(jnp.where(first, columns(n), columns(-n)), mine[n - 1])
+        terms += product(jnp.where(first, columns(-n), columns(n)), theirs[n - 1])
+
+    def term(k):
+        return lax.dynamic_slice_in_dim(terms, (k + steps) * rows, rows, axis=0)
+
+    def step(i, carry):
+        k = steps - 1 - i
+        more = (k > 0).astype(jnp.float32)
+        right = moved(carry[0].astype(jnp.bfloat16), stride).astype(jnp.float32)
+        left = moved(carry[1].astype(jnp.bfloat16), -stride).astype(jnp.float32)
+        return right + more * term(k), left + more * term(-k)
+
+    right, left = lax.fori_loop(0, steps, step, (term(steps), term(-steps)))
+    return term(0) + (right + left)
 
 
 def rms_scale(residual, norm_gain):
@@ -42,6 +115,10 @@
     return lax.ppermute(x, RING, [(i, (i + distance) % length) for i in range(length)])
 
 
+def partner_of(x):
+    return lax.ppermute(x, CORE, [(0, 1), (1, 0)])
+
+
 def plan():
     length = lax.axis_size(RING)
     reach = (-(-length // 3)) // 2
@@ -50,53 +127,49 @@
     return reach, window, 3 * window > length
 
 
-def bundles():
-    reach, window, doubled = plan()
-    keys = [0] + [k for s in range(1, reach + 1) for k in (-s, s)]
-    return {
-        k: (k, k - window, k + window)[: 2 if doubled and k == reach else 3] for k in keys
-    }
+def keys_in_order():
+    reach, _, _ = plan()
+    return [0] + [k for s in range(1, reach + 1) for k in (-s, s)]
+
+
+def offsets_in_order():
+    _, window, _ = plan()
+    return [k + f for k in keys_in_order() for f in (0, -window, window)]
 
 
 def gathered(own):
-    reach, window, doubled = plan()
-    rows = own.shape[0]
+    reach, window, _ = plan()
     behind, ahead = moved(own, window), moved(own, -window)
-    right = left = jnp.concatenate([own, behind, ahead], axis=0)
-    found = [right]
-    for s in range(1, reach + 1):
-        right = moved(right, 1)
-        if doubled and s == reach:
-            left = left[: 2 * rows]
-        left = moved(left, -1)
+    bundle = jnp.concatenate([own, behind, ahead], axis=0)
+    rows = bundle.shape[0]
+    found = [bundle]
+    right = left = bundle
+    for s in range(reach):
+        right, left = moved(right, 1), moved(left, -1)
         found += [right, left]
     return jnp.concatenate(found, axis=0)
 
 
 def scattered(terms, rows):
     reach, window, _ = plan()
-    start, at = {}, 0
-    for k, offsets in bundles().items():
-        start[k] = (at, at + len(offsets) * rows)
-        at = start[k][1]
-
-    def term(k):
-        return lax.slice_in_dim(terms, *start[k], axis=0)
-
-    def joined(received, own):
-        rows = received.shape[0]
-        if rows == own.shape[0]:
-            return received.astype(jnp.float32) + own
-        return jnp.concatenate([received.astype(jnp.float32) + own[:rows], own[rows:]], axis=0)
-
-    right, left = term(reach), term(-reach)
-    for s in range(reach, 0, -1):
-        right_in = moved(right.astype(jnp.bfloat16), 1)
-        left_in = moved(left.astype(jnp.bfloat16), -1)
-        if s > 1:
-            right = joined(right_in, term(s - 1))
-            left = joined(left_in, term(1 - s))
-    near = joined(right_in, term(0)) + left_in.astype(jnp.float32)
+    many = 3 * rows
+
+    def term(at):
+        return lax.dynamic_slice_in_dim(terms, at * many, many, axis=0)
+
+    right, left = term(2 * reach), term(2 * reach - 1)
+    right, left = right.astype(jnp.bfloat16), left.astype(jnp.bfloat16)
+
+    def step(i, carry):
+        s = reach - 1 - i
+        right, left = moved(carry[0], 1), moved(carry[1], -1)
+        right = (right.astype(jnp.float32) + term(2 * s)).astype(jnp.bfloat16)
+        left = (left.astype(jnp.float32) + term(2 * s - 1)).astype(jnp.bfloat16)
+        return right, left
+
+    right, left = lax.fori_loop(0, reach - 1, step, (right, left))
+    right, left = moved(right, 1), moved(left, -1)
+    near = right.astype(jnp.float32) + left.astype(jnp.float32) + terms[:many]
     from_ahead = moved(near[rows : 2 * rows].astype(jnp.bfloat16), -window)
     from_behind = moved(near[2 * rows :].astype(jnp.bfloat16), window)
     return near[:rows] + (from_ahead.astype(jnp.float32) + from_behind.astype(jnp.float32))
@@ -105,24 +178,24 @@
 def experts_kernel(half, x, factor, gate, up, down, gate_too, up_too, down_too, out):
     step = pl.program_id(0)
 
-    def add(gate_ref, up_ref, down_ref, first):
+    def add(gate_ref, up_ref, down_ref):
         gate_val = jnp.dot(x[...], gate_ref[...], preferred_element_type=jnp.float32)
         up_val = jnp.dot(x[...], up_ref[...], preferred_element_type=jnp.float32)
         hidden = (gate_val * jax.nn.sigmoid(gate_val) * up_val).astype(jnp.bfloat16)
         down_val = jnp.dot(hidden, down_ref[...], preferred_element_type=jnp.float32)
-        out[...] = down_val if first else out[...] + down_val
+        out[...] += down_val
 
     @pl.when(step == 0)
     def _():
-        add(gate, up, down, True)
-
-    @pl.when((step > 0) & (step < half))
+        out[...] = jnp.zeros_like(out)
+
+    @pl.when(step < half)
     def _():
-        add(gate, up, down, False)
+        add(gate, up, down)
 
     @pl.when(step >= half)
     def _():
-        add(gate_too, up_too, down_too, False)
+        add(gate_too, up_too, down_too)
 
     @pl.when(step == 2 * half - 1)
     def _():
@@ -185,11 +258,11 @@
     cores = lax.axis_size(CORE)
     assert cores == 2
 
-    def partners(x):
-        return lax.ppermute(x, CORE, [(0, 1), (1, 0)])
-
-    w_out_too = partners(w_out)
-    w_gate_too, w_up_too, w_down_too = partners(w_gate), partners(w_up), partners(w_down)
+    too = tuple(partner_of(w) for w in (w_gate, w_up, w_down))
+    other = partner_of(w_out)
+    first = core == 0
+    slab = jnp.concatenate([jnp.where(first, w_out, other), jnp.where(first, other, w_out)], axis=0)
+    slab, queries = lax.optimization_barrier((slab, queries))
     tok_rows, width = hidden_in.shape
     ratio = H // KV
     span = keys.shape[1] // KV
@@ -211,37 +284,30 @@
         preferred_element_type=jnp.float32,
     )
     attended = (numerator / denominator[..., None]).reshape(tok_rows, H * HD).astype(jnp.bfloat16)
-    column_block = lax.all_to_all(attended, RING, split_axis=1, concat_axis=0, tiled=True)
-
-    order = [offset % length for offsets in bundles().values() for offset in offsets]
-    assert sorted(order) == list(range(length))
-
+    order = offsets_in_order()
+    seen = [offset % length for offset in order]
+    once = [float(k not in seen[:i]) for i, k in enumerate(seen)]
+    assert set(seen) == set(range(length))
+    once = jnp.repeat(jnp.array(once, jnp.float32), tok_rows)[:, None]
     def in_order(x):
         x = jnp.roll(x, -place, axis=0)
-        return jnp.concatenate([x[k : k + 1] for k in order], axis=0)
-
-    column_block = in_order(column_block.reshape(length, tok_rows, -1)).reshape(
-        length * tok_rows, -1
-    )
-    depth = w_out.shape[0]
-    low, high = column_block[:, :depth], column_block[:, depth:]
-    first = core == 0
-    attn_terms = jnp.dot(
-        jnp.where(first, low, high), w_out, preferred_element_type=jnp.float32
-    ) + jnp.dot(jnp.where(first, high, low), w_out_too, preferred_element_type=jnp.float32)
-
-    residual = hidden_in.astype(jnp.float32) + scattered(attn_terms, tok_rows)
+        return jnp.concatenate([x[k : k + 1] for k in seen], axis=0).reshape(
+            len(seen) * tok_rows, -1
+        )
+
+    residual = hidden_in.astype(jnp.float32) + projected(attended, w_out, slab)
     normed = rms_scale(residual, norm_gain)
     my_expert = place // (length // EXPERTS)
     piece = gathered(normed)
     ids = lax.dynamic_index_in_dim(
         expert_ids.reshape(length, cores, tok_rows, -1), core, axis=1, keepdims=False
     )
-    ids = in_order(ids).reshape(length * tok_rows, -1)
+    ids = in_order(ids)
     gates = gate_pair(jnp.dot(piece, w_router, preferred_element_type=jnp.float32), ids)
     factor = jnp.sum(gates * (ids == my_expert).astype(jnp.float32), axis=1)
+    factor = factor * once[:, 0]
     terms = expert_terms(
-        piece, factor[:, None], (w_gate, w_up, w_down), (w_gate_too, w_up_too, w_down_too)
+        piece, factor[:, None], (w_gate, w_up, w_down), too
     )
     return (residual + scattered(terms, tok_rows)).astype(jnp.bfloat16)
 

time: 288 us -> 279 us (0.969)
  waiting for transfers between devices: 123 us -> 96.9 us
  starting transfers between devices: 136 us -> 144 us
  local copies, waits for them, and re-layouts: 2.96 us -> 6.97 us
  other arithmetic: 5.81 us -> 9.56 us
  matrix products: 4.12 us -> 7.18 us
    ppermute x4 -> x8, starting transfers between devices: 0.93 us -> 40 us  [the longest x2 23.2 us: outward(): return lax.ppermute(x, HEAD, pairs)]
    all_to_all x1 -> x0, starting transfers between devices: 32.7 us -> none  [on_device(): lax.all_to_all(attended, RING, split_axis=1, concat_axis=0, tiled=True)]
    all_to_all x1 -> x0, waiting for transfers between devices: 30.7 us -> none  [on_device(): lax.all_to_all(attended, RING, split_axis=1, concat_axis=0, tiled=True)]
    unnamed x56 -> x33, local copies, waits for them, and re-layouts: 0.24 us -> 4.62 us
    dot_general x2 -> x5, matrix products: 1.23 us -> 5.54 us  [product(): return jnp.dot(x, w, preferred_element_type=jnp.float32)]
    convert_element_type x8 -> x10, other arithmetic: 1.48 us -> 4.46 us  [the longest x4 4.41 us: step(): left = (left.astype(jnp.float32) + term(2 * s - 1)).astype(jnp.bfloat16)]
    ppermute x4 -> x8, waiting for transfers between devices: 0.01 us -> 2.89 us  [the longest x2 2.75 us: outward(): return lax.ppermute(x, HEAD, pairs)]
  transfers between devices with their start and end apart: 41 -> 44, of which waited for: 26 -> 28; matrix products, arithmetic and copies ran while one was open for 2% -> 5% of each run, Pallas kernels for 0% -> 0%
where the time goes in v2:
time: 279 us; the launch traced here: 276 us
  starting transfers between devices  144 us (52%)
  waiting for transfers between devices  96.9 us (35%)
  Pallas kernels  11 us (4%)
  other arithmetic  9.56 us (3%)
  matrix products  7.18 us (3%)
  local copies, waits for them, and re-layouts  6.97 us (2%)
    ppermute x36, starting transfers between devices, moved(): lax.ppermute(x, RING, [(i, (i + distance) % length) for i in range(length)])  104 us
    ppermute x36, waiting for transfers between devices, moved(): lax.ppermute(x, RING, [(i, (i + distance) % length) for i in range(length)])  94 us
    ppermute x2, starting transfers between devices, outward(): return lax.ppermute(x, HEAD, pairs)  23.2 us
    ppermute x6, starting transfers between devices, partner_of(): return lax.ppermute(x, CORE, [(0, 1), (1, 0)])  16.9 us
    pallas_call x1, Pallas kernels, expert_terms(): pl.pallas_call(functools.partial(experts_kernel, half), grid=(2 * half,),...  11 us
  transfers between devices with their start and end apart: 44, of which 28 were waited for; matrix products, arithmetic and copies ran while one was open for 5% of the time, Pallas kernels for 0%

profile of v2, /device:TPU:38, one launch (start us, length us, event | category | flops | bytes accessed | tf_op | source)
XLA Modules:
  0.0 276.3 jit_solution(13701760139708987335)
XLA Ops:
  2.2 1.1 broadcast_select_fusion.1
  3.5 1.1 copy-done.3
  6.1 23.1 %collective-permute-start.11 = (bf16[192,3072]{1,0:T(8,128)(2,1)S(1)}, bf16[192,3072]{1,0:T(8,128)(2,1)}, u32[]{:S(2)}, u32[]{:S(2)}) collective-permute-start(bf16[192,3072]{1,0:T(8,128)(2,1)S(1)} %pad_maximum_fusion), channel_id=1, source_target_pairs={{0,62},{2,0},{4,2},{6,4},{8,6},{10,8},{12,10},{14,12},{16,14},{18,... | collective-permute-start | bytes 3538952 | tf_op jit(solution)/shard_map/ppermute | solution.py:29
  30.2 11.3 %collective-permute-done.5 = bf16[24,960]{1,0:T(8,128)(2,1)S(1)} collective-permute-done((bf16[24,960]{1,0:T(8,128)(2,1)S(1)}, bf16[24,960]{1,0:T(8,128)(2,1)S(1)}, u32[]{:S(2)}, u32[]{:S(2)}) %collective-permute-start.5) | collective-permute-done | bytes 46112 | tf_op jit(solution)/shard_map/ppermute | solution.py:115
  41.5 8.1 %collective-permute-start.8 = (bf16[24,960]{1,0:T(8,128)(2,1)S(1)}, bf16[24,960]{1,0:T(8,128)(2,1)S(1)}, u32[]{:S(2)}, u32[]{:S(2)}) collective-permute-start(bf16[24,960]{1,0:T(8,128)(2,1)S(1)} %pad_maximum_fusion.2), channel_id=1, source_target_pairs={{0,54},{2,56},{4,58},{6,60},{8,62},{10,0},{12,2},{14,4},{16,6},{18... | collective-permute-start | bytes 138248 | tf_op jit(solution)/shard_map/ppermute | solution.py:115
  49.7 3.0 %collective-permute-done.6 = bf16[16,960]{1,0:T(8,128)(2,1)S(1)} collective-permute-done((bf16[16,960]{1,0:T(8,128)(2,1)S(1)}, bf16[16,960]{1,0:T(8,128)(2,1)S(1)}, u32[]{:S(2)}, u32[]{:S(2)}) %collective-permute-start.6) | collective-permute-done | bytes 30752 | tf_op jit(solution)/shard_map/ppermute | solution.py:115
  52.8 8.2 %collective-permute-start.9 = (bf16[16,960]{1,0:T(8,128)(2,1)S(1)}, bf16[16,960]{1,0:T(8,128)(2,1)S(1)}, u32[]{:S(2)}, u32[]{:S(2)}) collective-permute-start(bf16[16,960]{1,0:T(8,128)(2,1)S(1)} %slice.288), channel_id=1, source_target_pairs={{0,54},{2,56},{4,58},{6,60},{8,62},{10,0},{12,2},{14,4},{16,6},{18... | collective-permute-start | bytes 92168 | tf_op jit(solution)/shard_map/ppermute | solution.py:115
  60.9 1.5 collective-permute-done.7
  62.5 7.7 %collective-permute-start.12 = (bf16[192,3072]{1,0:T(8,128)(2,1)}, bf16[192,3072]{1,0:T(8,128)(2,1)}, u32[]{:S(2)}, u32[]{:S(2)}) collective-permute-start(bf16[192,3072]{1,0:T(8,128)(2,1)} %collective-permute-done.11), channel_id=1, source_target_pairs={{0,1},{1,0},{2,3},{3,2},{4,5},{5,4},{6,7},{7,6},{8,9},{9,8},{10,11... | collective-permute-start | bytes 3538952 | tf_op jit(solution)/shard_map/ppermute | solution.py:119
  70.2 5.0 %collective-permute-start.10 = (bf16[8,960]{1,0:T(8,128)(2,1)S(1)}, bf16[8,960]{1,0:T(8,128)(2,1)S(1)}, u32[]{:S(2)}, u32[]{:S(2)}) collective-permute-start(bf16[8,960]{1,0:T(8,128)(2,1)S(1)} %get-tuple-element.281), channel_id=1, source_target_pairs={{0,54},{2,56},{4,58},{6,60},{8,62},{10,0},{12,2},{14,4},{16,6},{18... | collective-permute-start | bytes 46088 | tf_op jit(solution)/shard_map/ppermute | solution.py:115
  75.4 4.1 %collective-permute-start.28 = (bf16[3072,512]{1,0:T(8,128)(2,1)}, bf16[3072,512]{1,0:T(8,128)(2,1)}, u32[]{:S(2)}, u32[]{:S(2)}) collective-permute-start(bf16[3072,512]{1,0:T(8,128)(2,1)} %up.1), channel_id=1, source_target_pairs={{0,1},{1,0},{2,3},{3,2},{4,5},{5,4},{6,7},{7,6},{8,9},{9,8},{10,11... | collective-permute-start | bytes 9437192 | tf_op jit(solution)/shard_map/ppermute | solution.py:119
  79.4 2.7 collective-permute-done.13
  82.2 4.4 %collective-permute-start.14 = (bf16[192,3072]{1,0:T(8,128)(2,1)}, bf16[192,3072]{1,0:T(8,128)(2,1)S(1)}, u32[]{:S(2)}, u32[]{:S(2)}) collective-permute-start(bf16[192,3072]{1,0:T(8,128)(2,1)} %collective-permute-done.13), channel_id=1, source_target_pairs={{0,1},{1,0},{2,3},{3,2},{4,5},{5,4},{6,7},{7,6},{8,9},{9,8},{10,11... | collective-permute-start | bytes 3538952 | tf_op jit(solution)/shard_map/ppermute | solution.py:119
  86.6 1.6 fusion.20
  88.3 1.6 fusion.16
  89.9 1.6 fusion.18
  92.2 38.5 %while.34 = (s32[]{:T(128)}, f32[8,3072]{1,0:T(8,128)S(1)}, f32[8,3072]{1,0:T(8,128)S(1)}, f32[56,3072]{1,0:T(8,128)S(1)}, s32[]{:T(128)}, /*index=5*/s32[]{:T(1...) while((s32[]{:T(128)}, f32[8,3072]{1,0:T(8,128)S(1)}, f32[8,3072]{1,0:T(8,128)S(1)}, ...), condition=%wide.region_3.4_spmd, body=%wide.region_2.3_spmd.sunk | while | flops 196624 | bytes 1179999 | solution.py:93
  92.3 1.9 collective-permute-start
  94.2 5.0 %collective-permute-start.1 = (bf16[8,3072]{1,0:T(8,128)(2,1)S(1)}, bf16[8,3072]{1,0:T(8,128)(2,1)S(1)}, u32[]{:S(2)}, u32[]{:S(2)}) collective-permute-start(bf16[8,3072]{1,0:T(8,128)(2,1)S(1)} %convert_element_type.169), channel_id=1, source_target_pairs={{0,10},{2,12},{4,14},{6,16},{8,18},{10,20},{12,22},{14,24},{16,26}... | collective-permute-start | bytes 147464 | tf_op jit(solution)/shard_map/while/body/eval_jaxpr/ppermute | solution.py:115
  99.2 4.1 %collective-permute-done = bf16[8,3072]{1,0:T(8,128)(2,1)S(1)} collective-permute-done((bf16[8,3072]{1,0:T(8,128)(2,1)S(1)}, bf16[8,3072]{1,0:T(8,128)(2,1)S(1)}, u32[]{:S(2)}, u32[]{:S(2)}) %collective-permute-start) | collective-permute-done | bytes 49184 | tf_op jit(solution)/shard_map/while/body/eval_jaxpr/ppermute | solution.py:115
  103.3 1.7 collective-permute-done.1
  105.1 1.3 collective-permute-start
  106.4 5.6 %collective-permute-start.1 = (bf16[8,3072]{1,0:T(8,128)(2,1)S(1)}, bf16[8,3072]{1,0:T(8,128)(2,1)S(1)}, u32[]{:S(2)}, u32[]{:S(2)}) collective-permute-start(bf16[8,3072]{1,0:T(8,128)(2,1)S(1)} %convert_element_type.169), channel_id=1, source_target_pairs={{0,10},{2,12},{4,14},{6,16},{8,18},{10,20},{12,22},{14,24},{16,26}... | collective-permute-start | bytes 147464 | tf_op jit(solution)/shard_map/while/body/eval_jaxpr/ppermute | solution.py:115
  112.1 3.6 %collective-permute-done = bf16[8,3072]{1,0:T(8,128)(2,1)S(1)} collective-permute-done((bf16[8,3072]{1,0:T(8,128)(2,1)S(1)}, bf16[8,3072]{1,0:T(8,128)(2,1)S(1)}, u32[]{:S(2)}, u32[]{:S(2)}) %collective-permute-start) | collective-permute-done | bytes 49184 | tf_op jit(solution)/shard_map/while/body/eval_jaxpr/ppermute | solution.py:115
  115.7 2.0 collective-permute-done.1
  117.8 1.2 collective-permute-start
  118.9 5.8 %collective-permute-start.1 = (bf16[8,3072]{1,0:T(8,128)(2,1)S(1)}, bf16[8,3072]{1,0:T(8,128)(2,1)S(1)}, u32[]{:S(2)}, u32[]{:S(2)}) collective-permute-start(bf16[8,3072]{1,0:T(8,128)(2,1)S(1)} %convert_element_type.169), channel_id=1, source_target_pairs={{0,10},{2,12},{4,14},{6,16},{8,18},{10,20},{12,22},{14,24},{16,26}... | collective-permute-start | bytes 147464 | tf_op jit(solution)/shard_map/while/body/eval_jaxpr/ppermute | solution.py:115
  124.7 2.1 collective-permute-done
  126.8 3.9 %collective-permute-done.1 = bf16[8,3072]{1,0:T(8,128)(2,1)S(1)} collective-permute-done((bf16[8,3072]{1,0:T(8,128)(2,1)S(1)}, bf16[8,3072]{1,0:T(8,128)(2,1)S(1)}, u32[]{:S(2)}, u32[]{:S(2)}) %collective-permute-start.1) | collective-permute-done | bytes 49184 | tf_op jit(solution)/shard_map/while/body/eval_jaxpr/ppermute | solution.py:115
  131.0 7.9 %collective-permute-start.15 = (bf16[8,3072]{1,0:T(8,128)(2,1)S(1)}, bf16[8,3072]{1,0:T(8,128)(2,1)S(1)}, u32[]{:S(2)}, u32[]{:S(2)}) collective-permute-start(bf16[8,3072]{1,0:T(8,128)(2,1)S(1)} %get-tuple-element.259), channel_id=1, source_target_pairs={{0,22},{2,24},{4,26},{6,28},{8,30},{10,32},{12,34},{14,36},{16,38}... | collective-permute-start | bytes 147464 | tf_op jit(solution)/shard_map/ppermute | solution.py:115
  138.9 6.9 %collective-permute-start.16 = (bf16[8,3072]{1,0:T(8,128)(2,1)S(1)}, bf16[8,3072]{1,0:T(8,128)(2,1)S(1)}, u32[]{:S(2)}, u32[]{:S(2)}) collective-permute-start(bf16[8,3072]{1,0:T(8,128)(2,1)S(1)} %get-tuple-element.259), channel_id=1, source_target_pairs={{0,42},{2,44},{4,46},{6,48},{8,50},{10,52},{12,54},{14,56},{16,58}... | collective-permute-start | bytes 147464 | tf_op jit(solution)/shard_map/ppermute | solution.py:115
  146.4 6.2 %collective-permute-done.15 = bf16[8,3072]{1,0:T(8,128)(2,1)S(1)} collective-permute-done((bf16[8,3072]{1,0:T(8,128)(2,1)S(1)}, bf16[8,3072]{1,0:T(8,128)(2,1)S(1)}, u32[]{:S(2)}, u32[]{:S(2)}) %collective-permute-start.15) | collective-permute-done | bytes 49184 | tf_op jit(solution)/shard_map/ppermute | solution.py:115
  152.6 2.6 collective-permute-done.16
  155.3 1.9 collective-permute-start.17
  157.2 3.6 %collective-permute-start.18 = (bf16[24,3072]{1,0:T(8,128)(2,1)S(1)}, bf16[24,3072]{1,0:T(8,128)(2,1)S(1)}, u32[]{:S(2)}, u32[]{:S(2)}) collective-permute-start(bf16[24,3072]{1,0:T(8,128)(2,1)S(1)} %pad_maximum_fusion.1), channel_id=1, source_target_pairs={{0,62},{2,0},{4,2},{6,4},{8,6},{10,8},{12,10},{14,12},{16,14},{18,... | collective-permute-start | bytes 442376 | tf_op jit(solution)/shard_map/ppermute | solution.py:115
  160.8 3.0 %collective-permute-done.17 = bf16[24,3072]{1,0:T(8,128)(2,1)S(1)} collective-permute-done((bf16[24,3072]{1,0:T(8,128)(2,1)S(1)}, bf16[24,3072]{1,0:T(8,128)(2,1)S(1)}, u32[]{:S(2)}, u32[]{:S(2)}) %collective-permute-start.17) | collective-permute-done | bytes 147488 | tf_op jit(solution)/shard_map/ppermute | solution.py:115
  163.9 3.3 %collective-permute-start.20 = (bf16[24,3072]{1,0:T(8,128)(2,1)S(1)}, bf16[24,3072]{1,0:T(8,128)(2,1)S(1)}, u32[]{:S(2)}, u32[]{:S(2)}) collective-permute-start(bf16[24,3072]{1,0:T(8,128)(2,1)S(1)} %collective-permute-done.18), channel_id=1, source_target_pairs={{0,62},{2,0},{4,2},{6,4},{8,6},{10,8},{12,10},{14,12},{16,14},{18,... | collective-permute-start | bytes 442376 | tf_op jit(solution)/shard_map/ppermute | solution.py:115
  167.2 3.8 %collective-permute-done.19 = bf16[24,3072]{1,0:T(8,128)(2,1)S(1)} collective-permute-done((bf16[24,3072]{1,0:T(8,128)(2,1)S(1)}, bf16[24,3072]{1,0:T(8,128)(2,1)S(1)}, u32[]{:S(2)}, u32[]{:S(2)}) %collective-permute-start.19) | collective-permute-done | bytes 147488 | tf_op jit(solution)/shard_map/ppermute | solution.py:115
  171.2 3.6 %collective-permute-start.22 = (bf16[24,3072]{1,0:T(8,128)(2,1)S(1)}, bf16[24,3072]{1,0:T(8,128)(2,1)S(1)}, u32[]{:S(2)}, u32[]{:S(2)}) collective-permute-start(bf16[24,3072]{1,0:T(8,128)(2,1)S(1)} %collective-permute-done.20), channel_id=1, source_target_pairs={{0,62},{2,0},{4,2},{6,4},{8,6},{10,8},{12,10},{14,12},{16,14},{18,... | collective-permute-start | bytes 442376 | tf_op jit(solution)/shard_map/ppermute | solution.py:115
  174.8 3.9 %collective-permute-done.21 = bf16[24,3072]{1,0:T(8,128)(2,1)S(1)} collective-permute-done((bf16[24,3072]{1,0:T(8,128)(2,1)S(1)}, bf16[24,3072]{1,0:T(8,128)(2,1)S(1)}, u32[]{:S(2)}, u32[]{:S(2)}) %collective-permute-start.21) | collective-permute-done | bytes 147488 | tf_op jit(solution)/shard_map/ppermute | solution.py:115
  178.9 3.3 %collective-permute-start.24 = (bf16[24,3072]{1,0:T(8,128)(2,1)S(1)}, bf16[24,3072]{1,0:T(8,128)(2,1)S(1)}, u32[]{:S(2)}, u32[]{:S(2)}) collective-permute-start(bf16[24,3072]{1,0:T(8,128)(2,1)S(1)} %collective-permute-done.22), channel_id=1, source_target_pairs={{0,62},{2,0},{4,2},{6,4},{8,6},{10,8},{12,10},{14,12},{16,14},{18,... | collective-permute-start | bytes 442376 | tf_op jit(solution)/shard_map/ppermute | solution.py:115
  182.2 3.6 %collective-permute-done.23 = bf16[24,3072]{1,0:T(8,128)(2,1)S(1)} collective-permute-done((bf16[24,3072]{1,0:T(8,128)(2,1)S(1)}, bf16[24,3072]{1,0:T(8,128)(2,1)S(1)}, u32[]{:S(2)}, u32[]{:S(2)}) %collective-permute-start.23) | collective-permute-done | bytes 147488 | tf_op jit(solution)/shard_map/ppermute | solution.py:115
  186.2 3.3 %collective-permute-start.26 = (bf16[24,3072]{1,0:T(8,128)(2,1)S(1)}, bf16[24,3072]{1,0:T(8,128)(2,1)S(1)}, u32[]{:S(2)}, u32[]{:S(2)}) collective-permute-start(bf16[24,3072]{1,0:T(8,128)(2,1)S(1)} %collective-permute-done.24), channel_id=1, source_target_pairs={{0,62},{2,0},{4,2},{6,4},{8,6},{10,8},{12,10},{14,12},{16,14},{18,... | collective-permute-start | bytes 442376 | tf_op jit(solution)/shard_map/ppermute | solution.py:115
  189.5 3.0 %collective-permute-done.25 = bf16[24,3072]{1,0:T(8,128)(2,1)S(1)} collective-permute-done((bf16[24,3072]{1,0:T(8,128)(2,1)S(1)}, bf16[24,3072]{1,0:T(8,128)(2,1)S(1)}, u32[]{:S(2)}, u32[]{:S(2)}) %collective-permute-start.25) | collective-permute-done | bytes 147488 | tf_op jit(solution)/shard_map/ppermute | solution.py:115
  193.8 1.9 copy-done.1
  195.6 11.0 %experts.1 = f32[264,3072]{1,0:T(8,128)S(1)} custom-call(bf16[264,3072]{1,0:T(8,128)(2,1)S(1)} %constant_dynamic-update-slice_fusion.7.x, f32[264,1]{1,0:T(8,128)S(1)} %mul.147.factor, bf16[3072,512]{1,0:T(8,128)(2,1)S(1)} %copy-done.1, bf16[3072,512]{1,0:T(8,128)(2,1)} %up.1, bf16[512,3072]{1,0:T(8,128)(2,1)} %down.1, ...), custom_call_target="tpu_custom_call" | custom-call | flops 4982833152 | bytes 18874368 | tf_op jit(solution)/shard_map/experts/pallas_call | solution.py:220
  206.9 1.4 copy-done.2
  208.4 37.8 %while.35 = (s32[]{:T(128)}, bf16[24,3072]{1,0:T(8,128)(2,1)S(1)}, bf16[24,3072]{1,0:T(8,128)(2,1)S(1)}, f32[264,3072]{1,0:T(8,128)}, s32[]{:T(128)}, /*index=5*...) while((s32[]{:T(128)}, bf16[24,3072]{1,0:T(8,128)(2,1)S(1)}, ...), condition=%wide.region_8.9_spmd, body=%wide.region_7.8_spmd.sunk | while | flops 442381 | bytes 2359629 | solution.py:170
  208.4 3.4 %collective-permute-start.2 = (bf16[24,3072]{1,0:T(8,128)(2,1)S(1)}, bf16[24,3072]{1,0:T(8,128)(2,1)S(1)}, u32[]{:S(2)}, u32[]{:S(2)}) collective-permute-start(bf16[24,3072]{1,0:T(8,128)(2,1)S(1)} %get-tuple-element.420), channel_id=1, source_target_pairs={{0,62},{2,0},{4,2},{6,4},{8,6},{10,8},{12,10},{14,12},{16,14},{18,... | collective-permute-start | bytes 442376 | tf_op jit(solution)/shard_map/while/body/eval_jaxpr/ppermute | solution.py:115
  211.9 3.0 %collective-permute-done.2 = bf16[24,3072]{1,0:T(8,128)(2,1)S(1)} collective-permute-done((bf16[24,3072]{1,0:T(8,128)(2,1)S(1)}, bf16[24,3072]{1,0:T(8,128)(2,1)S(1)}, u32[]{:S(2)}, u32[]{:S(2)}) %collective-permute-start.2) | collective-permute-done | bytes 147488 | tf_op jit(solution)/shard_map/while/body/eval_jaxpr/ppermute | solution.py:115
  214.9 3.3 %collective-permute-done.3 = bf16[24,3072]{1,0:T(8,128)(2,1)S(1)} collective-permute-done((bf16[24,3072]{1,0:T(8,128)(2,1)S(1)}, bf16[24,3072]{1,0:T(8,128)(2,1)S(1)}, u32[]{:S(2)}, u32[]{:S(2)}) %collective-permute-start.3) | collective-permute-done | bytes 147488 | tf_op jit(solution)/shard_map/while/body/eval_jaxpr/ppermute | solution.py:115
  219.5 2.0 collective-permute-start.3
  221.5 3.1 %collective-permute-done.2 = bf16[24,3072]{1,0:T(8,128)(2,1)S(1)} collective-permute-done((bf16[24,3072]{1,0:T(8,128)(2,1)S(1)}, bf16[24,3072]{1,0:T(8,128)(2,1)S(1)}, u32[]{:S(2)}, u32[]{:S(2)}) %collective-permute-start.2) | collective-permute-done | bytes 147488 | tf_op jit(solution)/shard_map/while/body/eval_jaxpr/ppermute | solution.py:115
  224.6 1.3 collective-permute-done.3
  227.1 2.4 collective-permute-start.2
  229.5 2.9 %collective-permute-done.2 = bf16[24,3072]{1,0:T(8,128)(2,1)S(1)} collective-permute-done((bf16[24,3072]{1,0:T(8,128)(2,1)S(1)}, bf16[24,3072]{1,0:T(8,128)(2,1)S(1)}, u32[]{:S(2)}, u32[]{:S(2)}) %collective-permute-start.2) | collective-permute-done | bytes 147488 | tf_op jit(solution)/shard_map/while/body/eval_jaxpr/ppermute | solution.py:115
  232.3 4.2 %collective-permute-done.3 = bf16[24,3072]{1,0:T(8,128)(2,1)S(1)} collective-permute-done((bf16[24,3072]{1,0:T(8,128)(2,1)S(1)}, bf16[24,3072]{1,0:T(8,128)(2,1)S(1)}, u32[]{:S(2)}, u32[]{:S(2)}) %collective-permute-start.3) | collective-permute-done | bytes 147488 | tf_op jit(solution)/shard_map/while/body/eval_jaxpr/ppermute | solution.py:115
  238.1 1.7 collective-permute-start.3
  239.8 5.2 %collective-permute-done.2 = bf16[24,3072]{1,0:T(8,128)(2,1)S(1)} collective-permute-done((bf16[24,3072]{1,0:T(8,128)(2,1)S(1)}, bf16[24,3072]{1,0:T(8,128)(2,1)S(1)}, u32[]{:S(2)}, u32[]{:S(2)}) %collective-permute-start.2) | collective-permute-done | bytes 147488 | tf_op jit(solution)/shard_map/while/body/eval_jaxpr/ppermute | solution.py:115
  245.1 1.1 add_convert_fusion.3
  246.3 3.2 %collective-permute-start.31 = (bf16[24,3072]{1,0:T(8,128)(2,1)S(1)}, bf16[24,3072]{1,0:T(8,128)(2,1)S(1)}, u32[]{:S(2)}, u32[]{:S(2)}) collective-permute-start(bf16[24,3072]{1,0:T(8,128)(2,1)S(1)} %get-tuple-element.237), channel_id=1, source_target_pairs={{0,62},{2,0},{4,2},{6,4},{8,6},{10,8},{12,10},{14,12},{16,14},{18,... | collective-permute-start | bytes 442376 | tf_op jit(solution)/shard_map/ppermute | solution.py:115
  249.5 7.7 %collective-permute-done.30 = bf16[24,3072]{1,0:T(8,128)(2,1)S(1)} collective-permute-done((bf16[24,3072]{1,0:T(8,128)(2,1)S(1)}, bf16[24,3072]{1,0:T(8,128)(2,1)S(1)}, u32[]{:S(2)}, u32[]{:S(2)}) %collective-permute-start.30) | collective-permute-done | bytes 147488 | tf_op jit(solution)/shard_map/ppermute | solution.py:115
  258.4 13.4 %collective-permute-start.33 = (bf16[8,3072]{1,0:T(8,128)(2,1)S(1)}, bf16[8,3072]{1,0:T(8,128)(2,1)S(1)}, u32[]{:S(2)}, u32[]{:S(2)}) collective-permute-start(bf16[8,3072]{1,0:T(8,128)(2,1)S(1)} %get-tuple-element.273), channel_id=1, source_target_pairs={{0,22},{2,24},{4,26},{6,28},{8,30},{10,32},{12,34},{14,36},{16,38}... | collective-permute-start | bytes 147464 | tf_op jit(solution)/shard_map/ppermute | solution.py:115
  271.8 3.1 %collective-permute-done.32 = bf16[8,3072]{1,0:T(8,128)(2,1)S(1)} collective-permute-done((bf16[8,3072]{1,0:T(8,128)(2,1)S(1)}, bf16[8,3072]{1,0:T(8,128)(2,1)S(1)}, u32[]{:S(2)}, u32[]{:S(2)}) %collective-permute-start.32) | collective-permute-done | bytes 49184 | tf_op jit(solution)/shard_map/ppermute | solution.py:115
  (131 shorter events, 15.3 us)
Async XLA Ops:
  0.0 5.5 %copy-start = (bf16[8,512,128]{2,1,0:T(8,128)(2,1)S(1)}, bf16[8,512,128]{2,1,0:T(8,128)(2,1)}, u32[]{:S(2)}) copy-start(bf16[8,512,128]{2,1,0:T(8,128)(2,1)} %param.20) | copy-start | bytes 3145732
  0.0 2.2 collective-permute-start.4
  0.0 193.7 %collective-permute-start.27 = (bf16[3072,512]{1,0:T(8,128)(2,1)}, bf16[3072,512]{1,0:T(8,128)(2,1)}, u32[]{:S(2)}, u32[]{:S(2)}) collective-permute-start(bf16[3072,512]{1,0:T(8,128)(2,1)} %gate.1), channel_id=1, source_target_pairs={{0,1},{1,0},{2,3},{3,2},{4,5},{5,4},{6,7},{7,6},{8,9},{9,8},{10,11... | collective-permute-start | bytes 9437192 | tf_op jit(solution)/shard_map/ppermute | solution.py:119
  3.4 1.2 copy-start.3
  3.4 1.2 copy-start.4
  5.5 69.9 %copy-start.7 = (bf16[3072]{0:T(1024)(128)(2,1)S(1)}, bf16[3072]{0:T(1024)(128)(2,1)}, u32[]{:S(2)}) copy-start(bf16[3072]{0:T(1024)(128)(2,1)} %param.24) | copy-start | bytes 18436
  6.1 56.3 %collective-permute-start.11 = (bf16[192,3072]{1,0:T(8,128)(2,1)S(1)}, bf16[192,3072]{1,0:T(8,128)(2,1)}, u32[]{:S(2)}, u32[]{:S(2)}) collective-permute-start(bf16[192,3072]{1,0:T(8,128)(2,1)S(1)} %pad_maximum_fusion), channel_id=1, source_target_pairs={{0,62},{2,0},{4,2},{6,4},{8,6},{10,8},{12,10},{14,12},{16,14},{18,... | collective-permute-start | bytes 3538952 | tf_op jit(solution)/shard_map/ppermute | solution.py:29
  30.0 11.6 %collective-permute-start.5 = (bf16[24,960]{1,0:T(8,128)(2,1)S(1)}, bf16[24,960]{1,0:T(8,128)(2,1)S(1)}, u32[]{:S(2)}, u32[]{:S(2)}) collective-permute-start(bf16[24,960]{1,0:T(8,128)(2,1)S(1)} %maximum_maximum_fusion), channel_id=1, source_target_pairs={{0,10},{2,12},{4,14},{6,16},{8,18},{10,20},{12,22},{14,24},{16,26}... | collective-permute-start | bytes 138248 | tf_op jit(solution)/shard_map/ppermute | solution.py:115
  41.5 11.1 %collective-permute-start.6 = (bf16[16,960]{1,0:T(8,128)(2,1)S(1)}, bf16[16,960]{1,0:T(8,128)(2,1)S(1)}, u32[]{:S(2)}, u32[]{:S(2)}) collective-permute-start(bf16[16,960]{1,0:T(8,128)(2,1)S(1)} %slice.278), channel_id=1, source_target_pairs={{0,10},{2,12},{4,14},{6,16},{8,18},{10,20},{12,22},{14,24},{16,26}... | collective-permute-start | bytes 92168 | tf_op jit(solution)/shard_map/ppermute | solution.py:115
  41.5 11.2 %collective-permute-start.8 = (bf16[24,960]{1,0:T(8,128)(2,1)S(1)}, bf16[24,960]{1,0:T(8,128)(2,1)S(1)}, u32[]{:S(2)}, u32[]{:S(2)}) collective-permute-start(bf16[24,960]{1,0:T(8,128)(2,1)S(1)} %pad_maximum_fusion.2), channel_id=1, source_target_pairs={{0,54},{2,56},{4,58},{6,60},{8,62},{10,0},{12,2},{14,4},{16,6},{18... | collective-permute-start | bytes 138248 | tf_op jit(solution)/shard_map/ppermute | solution.py:115
  52.7 9.8 %collective-permute-start.7 = (bf16[8,960]{1,0:T(8,128)(2,1)S(1)}, bf16[8,960]{1,0:T(8,128)(2,1)S(1)}, u32[]{:S(2)}, u32[]{:S(2)}) collective-permute-start(bf16[8,960]{1,0:T(8,128)(2,1)S(1)} %slice.279), channel_id=1, source_target_pairs={{0,10},{2,12},{4,14},{6,16},{8,18},{10,20},{12,22},{14,24},{16,26}... | collective-permute-start | bytes 46088 | tf_op jit(solution)/shard_map/ppermute | solution.py:115
  52.8 17.5 %collective-permute-start.9 = (bf16[16,960]{1,0:T(8,128)(2,1)S(1)}, bf16[16,960]{1,0:T(8,128)(2,1)S(1)}, u32[]{:S(2)}, u32[]{:S(2)}) collective-permute-start(bf16[16,960]{1,0:T(8,128)(2,1)S(1)} %slice.288), channel_id=1, source_target_pairs={{0,54},{2,56},{4,58},{6,60},{8,62},{10,0},{12,2},{14,4},{16,6},{18... | collective-permute-start | bytes 92168 | tf_op jit(solution)/shard_map/ppermute | solution.py:115
  62.4 19.8 %collective-permute-start.13 = (bf16[192,3072]{1,0:T(8,128)(2,1)}, bf16[192,3072]{1,0:T(8,128)(2,1)}, u32[]{:S(2)}, u32[]{:S(2)}) collective-permute-start(bf16[192,3072]{1,0:T(8,128)(2,1)} %collective-permute-done.11), channel_id=1, source_target_pairs={{0,62},{2,0},{4,2},{6,4},{8,6},{10,8},{12,10},{14,12},{16,14},{18,... | collective-permute-start | bytes 3538952 | tf_op jit(solution)/shard_map/ppermute | solution.py:29
  62.5 27.4 %collective-permute-start.12 = (bf16[192,3072]{1,0:T(8,128)(2,1)}, bf16[192,3072]{1,0:T(8,128)(2,1)}, u32[]{:S(2)}, u32[]{:S(2)}) collective-permute-start(bf16[192,3072]{1,0:T(8,128)(2,1)} %collective-permute-done.11), channel_id=1, source_target_pairs={{0,1},{1,0},{2,3},{3,2},{4,5},{5,4},{6,7},{7,6},{8,9},{9,8},{10,11... | collective-permute-start | bytes 3538952 | tf_op jit(solution)/shard_map/ppermute | solution.py:119
  70.2 16.4 %collective-permute-start.10 = (bf16[8,960]{1,0:T(8,128)(2,1)S(1)}, bf16[8,960]{1,0:T(8,128)(2,1)S(1)}, u32[]{:S(2)}, u32[]{:S(2)}) collective-permute-start(bf16[8,960]{1,0:T(8,128)(2,1)S(1)} %get-tuple-element.281), channel_id=1, source_target_pairs={{0,54},{2,56},{4,58},{6,60},{8,62},{10,0},{12,2},{14,4},{16,6},{18... | collective-permute-start | bytes 46088 | tf_op jit(solution)/shard_map/ppermute | solution.py:115
  75.4 118.4 %collective-permute-start.28 = (bf16[3072,512]{1,0:T(8,128)(2,1)}, bf16[3072,512]{1,0:T(8,128)(2,1)}, u32[]{:S(2)}, u32[]{:S(2)}) collective-permute-start(bf16[3072,512]{1,0:T(8,128)(2,1)} %up.1), channel_id=1, source_target_pairs={{0,1},{1,0},{2,3},{3,2},{4,5},{5,4},{6,7},{7,6},{8,9},{9,8},{10,11... | collective-permute-start | bytes 9437192 | tf_op jit(solution)/shard_map/ppermute | solution.py:119
  82.2 9.7 %collective-permute-start.14 = (bf16[192,3072]{1,0:T(8,128)(2,1)}, bf16[192,3072]{1,0:T(8,128)(2,1)S(1)}, u32[]{:S(2)}, u32[]{:S(2)}) collective-permute-start(bf16[192,3072]{1,0:T(8,128)(2,1)} %collective-permute-done.13), channel_id=1, source_target_pairs={{0,1},{1,0},{2,3},{3,2},{4,5},{5,4},{6,7},{7,6},{8,9},{9,8},{10,11... | collective-permute-start | bytes 3538952 | tf_op jit(solution)/shard_map/ppermute | solution.py:119
  92.2 38.6 %copy-start.5 = (bf16[8,3072]{1,0:T(8,128)(2,1)S(1)}, bf16[8,3072]{1,0:T(8,128)(2,1)}, u32[]{:S(2)}) copy-start(bf16[8,3072]{1,0:T(8,128)(2,1)} %param.17) | copy-start | bytes 147460
  92.3 11.1 %collective-permute-start = (bf16[8,3072]{1,0:T(8,128)(2,1)S(1)}, bf16[8,3072]{1,0:T(8,128)(2,1)S(1)}, u32[]{:S(2)}, u32[]{:S(2)}) collective-permute-start(bf16[8,3072]{1,0:T(8,128)(2,1)S(1)} %convert_element_type.167), channel_id=1, source_target_pairs={{0,54},{2,56},{4,58},{6,60},{8,62},{10,0},{12,2},{14,4},{16,6},{18... | collective-permute-start | bytes 147464 | tf_op jit(solution)/shard_map/while/body/eval_jaxpr/ppermute | solution.py:115
  94.2 10.8 %collective-permute-start.1 = (bf16[8,3072]{1,0:T(8,128)(2,1)S(1)}, bf16[8,3072]{1,0:T(8,128)(2,1)S(1)}, u32[]{:S(2)}, u32[]{:S(2)}) collective-permute-start(bf16[8,3072]{1,0:T(8,128)(2,1)S(1)} %convert_element_type.169), channel_id=1, source_target_pairs={{0,10},{2,12},{4,14},{6,16},{8,18},{10,20},{12,22},{14,24},{16,26}... | collective-permute-start | bytes 147464 | tf_op jit(solution)/shard_map/while/body/eval_jaxpr/ppermute | solution.py:115
  105.1 10.6 %collective-permute-start = (bf16[8,3072]{1,0:T(8,128)(2,1)S(1)}, bf16[8,3072]{1,0:T(8,128)(2,1)S(1)}, u32[]{:S(2)}, u32[]{:S(2)}) collective-permute-start(bf16[8,3072]{1,0:T(8,128)(2,1)S(1)} %convert_element_type.167), channel_id=1, source_target_pairs={{0,54},{2,56},{4,58},{6,60},{8,62},{10,0},{12,2},{14,4},{16,6},{18... | collective-permute-start | bytes 147464 | tf_op jit(solution)/shard_map/while/body/eval_jaxpr/ppermute | solution.py:115
  106.4 11.3 %collective-permute-start.1 = (bf16[8,3072]{1,0:T(8,128)(2,1)S(1)}, bf16[8,3072]{1,0:T(8,128)(2,1)S(1)}, u32[]{:S(2)}, u32[]{:S(2)}) collective-permute-start(bf16[8,3072]{1,0:T(8,128)(2,1)S(1)} %convert_element_type.169), channel_id=1, source_target_pairs={{0,10},{2,12},{4,14},{6,16},{8,18},{10,20},{12,22},{14,24},{16,26}... | collective-permute-start | bytes 147464 | tf_op jit(solution)/shard_map/while/body/eval_jaxpr/ppermute | solution.py:115
  117.8 9.0 %collective-permute-start = (bf16[8,3072]{1,0:T(8,128)(2,1)S(1)}, bf16[8,3072]{1,0:T(8,128)(2,1)S(1)}, u32[]{:S(2)}, u32[]{:S(2)}) collective-permute-start(bf16[8,3072]{1,0:T(8,128)(2,1)S(1)} %convert_element_type.167), channel_id=1, source_target_pairs={{0,54},{2,56},{4,58},{6,60},{8,62},{10,0},{12,2},{14,4},{16,6},{18... | collective-permute-start | bytes 147464 | tf_op jit(solution)/shard_map/while/body/eval_jaxpr/ppermute | solution.py:115
  118.9 11.8 %collective-permute-start.1 = (bf16[8,3072]{1,0:T(8,128)(2,1)S(1)}, bf16[8,3072]{1,0:T(8,128)(2,1)S(1)}, u32[]{:S(2)}, u32[]{:S(2)}) collective-permute-start(bf16[8,3072]{1,0:T(8,128)(2,1)S(1)} %convert_element_type.169), channel_id=1, source_target_pairs={{0,10},{2,12},{4,14},{6,16},{8,18},{10,20},{12,22},{14,24},{16,26}... | collective-permute-start | bytes 147464 | tf_op jit(solution)/shard_map/while/body/eval_jaxpr/ppermute | solution.py:115
  131.0 21.6 %collective-permute-start.15 = (bf16[8,3072]{1,0:T(8,128)(2,1)S(1)}, bf16[8,3072]{1,0:T(8,128)(2,1)S(1)}, u32[]{:S(2)}, u32[]{:S(2)}) collective-permute-start(bf16[8,3072]{1,0:T(8,128)(2,1)S(1)} %get-tuple-element.259), channel_id=1, source_target_pairs={{0,22},{2,24},{4,26},{6,28},{8,30},{10,32},{12,34},{14,36},{16,38}... | collective-permute-start | bytes 147464 | tf_op jit(solution)/shard_map/ppermute | solution.py:115
  138.9 16.3 %collective-permute-start.16 = (bf16[8,3072]{1,0:T(8,128)(2,1)S(1)}, bf16[8,3072]{1,0:T(8,128)(2,1)S(1)}, u32[]{:S(2)}, u32[]{:S(2)}) collective-permute-start(bf16[8,3072]{1,0:T(8,128)(2,1)S(1)} %get-tuple-element.259), channel_id=1, source_target_pairs={{0,42},{2,44},{4,46},{6,48},{8,50},{10,52},{12,54},{14,56},{16,58}... | collective-permute-start | bytes 147464 | tf_op jit(solution)/shard_map/ppermute | solution.py:115
  146.3 47.5 %collective-permute-start.29 = (bf16[512,3072]{1,0:T(8,128)(2,1)}, bf16[512,3072]{1,0:T(8,128)(2,1)}, u32[]{:S(2)}, u32[]{:S(2)}) collective-permute-start(bf16[512,3072]{1,0:T(8,128)(2,1)} %down.1), channel_id=1, source_target_pairs={{0,1},{1,0},{2,3},{3,2},{4,5},{5,4},{6,7},{7,6},{8,9},{9,8},{10,11... | collective-permute-start | bytes 9437192 | tf_op jit(solution)/shard_map/ppermute | solution.py:119
  155.2 37.3 %copy-start.6 = (bf16[3072,4]{0,1:T(4,128)(2,1)S(1)}, bf16[3072,4]{0,1:T(4,128)(2,1)}, u32[]{:S(2)}) copy-start(bf16[3072,4]{0,1:T(4,128)(2,1)} %param.25) | copy-start | bytes 73732
  155.3 8.5 %collective-permute-start.17 = (bf16[24,3072]{1,0:T(8,128)(2,1)S(1)}, bf16[24,3072]{1,0:T(8,128)(2,1)S(1)}, u32[]{:S(2)}, u32[]{:S(2)}) collective-permute-start(bf16[24,3072]{1,0:T(8,128)(2,1)S(1)} %pad_maximum_fusion.1), channel_id=1, source_target_pairs={{0,2},{2,4},{4,6},{6,8},{8,10},{10,12},{12,14},{14,16},{16,18},{18... | collective-permute-start | bytes 442376 | tf_op jit(solution)/shard_map/ppermute | solution.py:115
  157.2 6.7 %collective-permute-start.18 = (bf16[24,3072]{1,0:T(8,128)(2,1)S(1)}, bf16[24,3072]{1,0:T(8,128)(2,1)S(1)}, u32[]{:S(2)}, u32[]{:S(2)}) collective-permute-start(bf16[24,3072]{1,0:T(8,128)(2,1)S(1)} %pad_maximum_fusion.1), channel_id=1, source_target_pairs={{0,62},{2,0},{4,2},{6,4},{8,6},{10,8},{12,10},{14,12},{16,14},{18,... | collective-permute-start | bytes 442376 | tf_op jit(solution)/shard_map/ppermute | solution.py:115
  163.7 7.3 %collective-permute-start.19 = (bf16[24,3072]{1,0:T(8,128)(2,1)S(1)}, bf16[24,3072]{1,0:T(8,128)(2,1)S(1)}, u32[]{:S(2)}, u32[]{:S(2)}) collective-permute-start(bf16[24,3072]{1,0:T(8,128)(2,1)S(1)} %collective-permute-done.17), channel_id=1, source_target_pairs={{0,2},{2,4},{4,6},{6,8},{8,10},{10,12},{12,14},{14,16},{16,18},{18... | collective-permute-start | bytes 442376 | tf_op jit(solution)/shard_map/ppermute | solution.py:115
  163.9 7.2 %collective-permute-start.20 = (bf16[24,3072]{1,0:T(8,128)(2,1)S(1)}, bf16[24,3072]{1,0:T(8,128)(2,1)S(1)}, u32[]{:S(2)}, u32[]{:S(2)}) collective-permute-start(bf16[24,3072]{1,0:T(8,128)(2,1)S(1)} %collective-permute-done.18), channel_id=1, source_target_pairs={{0,62},{2,0},{4,2},{6,4},{8,6},{10,8},{12,10},{14,12},{16,14},{18,... | collective-permute-start | bytes 442376 | tf_op jit(solution)/shard_map/ppermute | solution.py:115
  171.0 7.7 %collective-permute-start.21 = (bf16[24,3072]{1,0:T(8,128)(2,1)S(1)}, bf16[24,3072]{1,0:T(8,128)(2,1)S(1)}, u32[]{:S(2)}, u32[]{:S(2)}) collective-permute-start(bf16[24,3072]{1,0:T(8,128)(2,1)S(1)} %collective-permute-done.19), channel_id=1, source_target_pairs={{0,2},{2,4},{4,6},{6,8},{8,10},{10,12},{12,14},{14,16},{16,18},{18... | collective-permute-start | bytes 442376 | tf_op jit(solution)/shard_map/ppermute | solution.py:115
  171.2 7.7 %collective-permute-start.22 = (bf16[24,3072]{1,0:T(8,128)(2,1)S(1)}, bf16[24,3072]{1,0:T(8,128)(2,1)S(1)}, u32[]{:S(2)}, u32[]{:S(2)}) collective-permute-start(bf16[24,3072]{1,0:T(8,128)(2,1)S(1)} %collective-permute-done.20), channel_id=1, source_target_pairs={{0,62},{2,0},{4,2},{6,4},{8,6},{10,8},{12,10},{14,12},{16,14},{18,... | collective-permute-start | bytes 442376 | tf_op jit(solution)/shard_map/ppermute | solution.py:115
  178.7 14.8 %copy-start.8 = (f32[33]{0:T(128)S(1)}, f32[33]{0:T(128)}, u32[]{:S(2)}) copy-start(f32[33]{0:T(128)} %constant.206.clone) | copy-start | bytes 400
  178.7 7.0 %collective-permute-start.23 = (bf16[24,3072]{1,0:T(8,128)(2,1)S(1)}, bf16[24,3072]{1,0:T(8,128)(2,1)S(1)}, u32[]{:S(2)}, u32[]{:S(2)}) collective-permute-start(bf16[24,3072]{1,0:T(8,128)(2,1)S(1)} %collective-permute-done.21), channel_id=1, source_target_pairs={{0,2},{2,4},{4,6},{6,8},{8,10},{10,12},{12,14},{14,16},{16,18},{18... | collective-permute-start | bytes 442376 | tf_op jit(solution)/shard_map/ppermute | solution.py:115
  178.9 7.3 %collective-permute-start.24 = (bf16[24,3072]{1,0:T(8,128)(2,1)S(1)}, bf16[24,3072]{1,0:T(8,128)(2,1)S(1)}, u32[]{:S(2)}, u32[]{:S(2)}) collective-permute-start(bf16[24,3072]{1,0:T(8,128)(2,1)S(1)} %collective-permute-done.22), channel_id=1, source_target_pairs={{0,62},{2,0},{4,2},{6,4},{8,6},{10,8},{12,10},{14,12},{16,14},{18,... | collective-permute-start | bytes 442376 | tf_op jit(solution)/shard_map/ppermute | solution.py:115
  185.8 6.7 %collective-permute-start.25 = (bf16[24,3072]{1,0:T(8,128)(2,1)S(1)}, bf16[24,3072]{1,0:T(8,128)(2,1)S(1)}, u32[]{:S(2)}, u32[]{:S(2)}) collective-permute-start(bf16[24,3072]{1,0:T(8,128)(2,1)S(1)} %collective-permute-done.23), channel_id=1, source_target_pairs={{0,2},{2,4},{4,6},{6,8},{8,10},{10,12},{12,14},{14,16},{16,18},{18... | collective-permute-start | bytes 442376 | tf_op jit(solution)/shard_map/ppermute | solution.py:115
  186.2 6.3 %collective-permute-start.26 = (bf16[24,3072]{1,0:T(8,128)(2,1)S(1)}, bf16[24,3072]{1,0:T(8,128)(2,1)S(1)}, u32[]{:S(2)}, u32[]{:S(2)}) collective-permute-start(bf16[24,3072]{1,0:T(8,128)(2,1)S(1)} %collective-permute-done.24), channel_id=1, source_target_pairs={{0,62},{2,0},{4,2},{6,4},{8,6},{10,8},{12,10},{14,12},{16,14},{18,... | collective-permute-start | bytes 442376 | tf_op jit(solution)/shard_map/ppermute | solution.py:115
  193.8 1.9 copy-start.1
  206.7 1.7 copy-start.2
  208.4 6.5 %collective-permute-start.2 = (bf16[24,3072]{1,0:T(8,128)(2,1)S(1)}, bf16[24,3072]{1,0:T(8,128)(2,1)S(1)}, u32[]{:S(2)}, u32[]{:S(2)}) collective-permute-start(bf16[24,3072]{1,0:T(8,128)(2,1)S(1)} %get-tuple-element.420), channel_id=1, source_target_pairs={{0,62},{2,0},{4,2},{6,4},{8,6},{10,8},{12,10},{14,12},{16,14},{18,... | collective-permute-start | bytes 442376 | tf_op jit(solution)/shard_map/while/body/eval_jaxpr/ppermute | solution.py:115
  211.9 6.4 %collective-permute-start.3 = (bf16[24,3072]{1,0:T(8,128)(2,1)S(1)}, bf16[24,3072]{1,0:T(8,128)(2,1)S(1)}, u32[]{:S(2)}, u32[]{:S(2)}) collective-permute-start(bf16[24,3072]{1,0:T(8,128)(2,1)S(1)} %get-tuple-element.419), channel_id=1, source_target_pairs={{0,2},{2,4},{4,6},{6,8},{8,10},{10,12},{12,14},{14,16},{16,18},{18... | collective-permute-start | bytes 442376 | tf_op jit(solution)/shard_map/while/body/eval_jaxpr/ppermute | solution.py:115
  219.3 5.3 %collective-permute-start.2 = (bf16[24,3072]{1,0:T(8,128)(2,1)S(1)}, bf16[24,3072]{1,0:T(8,128)(2,1)S(1)}, u32[]{:S(2)}, u32[]{:S(2)}) collective-permute-start(bf16[24,3072]{1,0:T(8,128)(2,1)S(1)} %get-tuple-element.420), channel_id=1, source_target_pairs={{0,62},{2,0},{4,2},{6,4},{8,6},{10,8},{12,10},{14,12},{16,14},{18,... | collective-permute-start | bytes 442376 | tf_op jit(solution)/shard_map/while/body/eval_jaxpr/ppermute | solution.py:115
  219.5 6.5 %collective-permute-start.3 = (bf16[24,3072]{1,0:T(8,128)(2,1)S(1)}, bf16[24,3072]{1,0:T(8,128)(2,1)S(1)}, u32[]{:S(2)}, u32[]{:S(2)}) collective-permute-start(bf16[24,3072]{1,0:T(8,128)(2,1)S(1)} %get-tuple-element.419), channel_id=1, source_target_pairs={{0,2},{2,4},{4,6},{6,8},{8,10},{10,12},{12,14},{14,16},{16,18},{18... | collective-permute-start | bytes 442376 | tf_op jit(solution)/shard_map/while/body/eval_jaxpr/ppermute | solution.py:115
  227.1 5.3 %collective-permute-start.2 = (bf16[24,3072]{1,0:T(8,128)(2,1)S(1)}, bf16[24,3072]{1,0:T(8,128)(2,1)S(1)}, u32[]{:S(2)}, u32[]{:S(2)}) collective-permute-start(bf16[24,3072]{1,0:T(8,128)(2,1)S(1)} %get-tuple-element.420), channel_id=1, source_target_pairs={{0,62},{2,0},{4,2},{6,4},{8,6},{10,8},{12,10},{14,12},{16,14},{18,... | collective-permute-start | bytes 442376 | tf_op jit(solution)/shard_map/while/body/eval_jaxpr/ppermute | solution.py:115
  229.5 7.1 %collective-permute-start.3 = (bf16[24,3072]{1,0:T(8,128)(2,1)S(1)}, bf16[24,3072]{1,0:T(8,128)(2,1)S(1)}, u32[]{:S(2)}, u32[]{:S(2)}) collective-permute-start(bf16[24,3072]{1,0:T(8,128)(2,1)S(1)} %get-tuple-element.419), channel_id=1, source_target_pairs={{0,2},{2,4},{4,6},{6,8},{8,10},{10,12},{12,14},{14,16},{16,18},{18... | collective-permute-start | bytes 442376 | tf_op jit(solution)/shard_map/while/body/eval_jaxpr/ppermute | solution.py:115
  237.7 7.4 %collective-permute-start.2 = (bf16[24,3072]{1,0:T(8,128)(2,1)S(1)}, bf16[24,3072]{1,0:T(8,128)(2,1)S(1)}, u32[]{:S(2)}, u32[]{:S(2)}) collective-permute-start(bf16[24,3072]{1,0:T(8,128)(2,1)S(1)} %get-tuple-element.420), channel_id=1, source_target_pairs={{0,62},{2,0},{4,2},{6,4},{8,6},{10,8},{12,10},{14,12},{16,14},{18,... | collective-permute-start | bytes 442376 | tf_op jit(solution)/shard_map/while/body/eval_jaxpr/ppermute | solution.py:115
  238.1 7.0 %collective-permute-start.3 = (bf16[24,3072]{1,0:T(8,128)(2,1)S(1)}, bf16[24,3072]{1,0:T(8,128)(2,1)S(1)}, u32[]{:S(2)}, u32[]{:S(2)}) collective-permute-start(bf16[24,3072]{1,0:T(8,128)(2,1)S(1)} %get-tuple-element.419), channel_id=1, source_target_pairs={{0,2},{2,4},{4,6},{6,8},{8,10},{10,12},{12,14},{14,16},{16,18},{18... | collective-permute-start | bytes 442376 | tf_op jit(solution)/shard_map/while/body/eval_jaxpr/ppermute | solution.py:115
  246.2 11.0 %collective-permute-start.30 = (bf16[24,3072]{1,0:T(8,128)(2,1)S(1)}, bf16[24,3072]{1,0:T(8,128)(2,1)S(1)}, u32[]{:S(2)}, u32[]{:S(2)}) collective-permute-start(bf16[24,3072]{1,0:T(8,128)(2,1)S(1)} %get-tuple-element.236), channel_id=1, source_target_pairs={{0,2},{2,4},{4,6},{6,8},{8,10},{10,12},{12,14},{14,16},{16,18},{18... | collective-permute-start | bytes 442376 | tf_op jit(solution)/shard_map/ppermute | solution.py:115
  246.3 10.9 %collective-permute-start.31 = (bf16[24,3072]{1,0:T(8,128)(2,1)S(1)}, bf16[24,3072]{1,0:T(8,128)(2,1)S(1)}, u32[]{:S(2)}, u32[]{:S(2)}) collective-permute-start(bf16[24,3072]{1,0:T(8,128)(2,1)S(1)} %get-tuple-element.237), channel_id=1, source_target_pairs={{0,62},{2,0},{4,2},{6,4},{8,6},{10,8},{12,10},{14,12},{16,14},{18,... | collective-permute-start | bytes 442376 | tf_op jit(solution)/shard_map/ppermute | solution.py:115
  258.3 16.7 %collective-permute-start.32 = (bf16[8,3072]{1,0:T(8,128)(2,1)S(1)}, bf16[8,3072]{1,0:T(8,128)(2,1)S(1)}, u32[]{:S(2)}, u32[]{:S(2)}) collective-permute-start(bf16[8,3072]{1,0:T(8,128)(2,1)S(1)} %get-tuple-element.272), channel_id=1, source_target_pairs={{0,42},{2,44},{4,46},{6,48},{8,50},{10,52},{12,54},{14,56},{16,58}... | collective-permute-start | bytes 147464 | tf_op jit(solution)/shard_map/ppermute | solution.py:115
  258.4 17.2 %collective-permute-start.33 = (bf16[8,3072]{1,0:T(8,128)(2,1)S(1)}, bf16[8,3072]{1,0:T(8,128)(2,1)S(1)}, u32[]{:S(2)}, u32[]{:S(2)}) collective-permute-start(bf16[8,3072]{1,0:T(8,128)(2,1)S(1)} %get-tuple-element.273), channel_id=1, source_target_pairs={{0,22},{2,24},{4,26},{6,28},{8,30},{10,32},{12,34},{14,36},{16,38}... | collective-permute-start | bytes 147464 | tf_op jit(solution)/shard_map/ppermute | solution.py:115

commit v3 on v2

--- a/solution.py
+++ b/solution.py
@@ -59,7 +59,7 @@
         right, left = moved(right, stride), moved(left, -stride)
         found[-k], found[k] = right[:rows], left[:rows]
         if k < WEIGHT_REACH:
-            ready, _, _ = lax.optimization_barrier((mine[-1], right, left))
+            ready = mine[-1]
             mine.append(outward(ready))
             theirs.append(partner_of(ready))
         elif k == WEIGHT_REACH:
@@ -80,8 +80,10 @@
         terms += product(jnp.where(first, columns(n), columns(-n)), mine[n - 1])
         terms += product(jnp.where(first, columns(-n), columns(n)), theirs[n - 1])
 
+    blocks = terms.reshape(-1, rows, terms.shape[1])
+
     def term(k):
-        return lax.dynamic_slice_in_dim(terms, (k + steps) * rows, rows, axis=0)
+        return lax.dynamic_index_in_dim(blocks, k + steps, axis=0, keepdims=False)
 
     def step(i, carry):
         k = steps - 1 - i
@@ -153,9 +155,10 @@
 def scattered(terms, rows):
     reach, window, _ = plan()
     many = 3 * rows
+    bundled = terms.reshape(-1, many, terms.shape[1])
 
     def term(at):
-        return lax.dynamic_slice_in_dim(terms, at * many, many, axis=0)
+        return lax.dynamic_index_in_dim(bundled, at, axis=0, keepdims=False)
 
     right, left = term(2 * reach), term(2 * reach - 1)
     right, left = right.astype(jnp.bfloat16), left.astype(jnp.bfloat16)

time: 279 us -> 278 us (level)
  no operation moved by 1% of the time
where the time goes in v3:
time: 278 us; the launch traced here: 276 us
  starting transfers between devices  144 us (52%)
  waiting for transfers between devices  97 us (35%)
  Pallas kernels  11 us (4%)
  other arithmetic  9.56 us (3%)
  matrix products  7.19 us (3%)
  local copies, waits for them, and re-layouts  6.97 us (3%)
    ppermute x36, starting transfers between devices, moved(): lax.ppermute(x, RING, [(i, (i + distance) % length) for i in range(length)])  104 us
    ppermute x36, waiting for transfers between devices, moved(): lax.ppermute(x, RING, [(i, (i + distance) % length) for i in range(length)])  94.1 us
    ppermute x2, starting transfers between devices, outward(): return lax.ppermute(x, HEAD, pairs)  23.2 us
    ppermute x6, starting transfers between devices, partner_of(): return lax.ppermute(x, CORE, [(0, 1), (1, 0)])  17 us
    pallas_call x1, Pallas kernels, expert_terms(): pl.pallas_call(functools.partial(experts_kernel, half), grid=(2 * half,),...  11 us
  transfers between devices with their start and end apart: 44, of which 28 were waited for; matrix products, arithmetic and copies ran while one was open for 5% of the time, Pallas kernels for 0%

profile of v3, /device:TPU:38, one launch (start us, length us, event | category | flops | bytes accessed | tf_op | source)
XLA Modules:
  0.0 276.3 jit_solution(7674915822653797146)
XLA Ops:
  2.2 1.1 broadcast_select_fusion.1
  3.5 1.1 copy-done.3
  6.1 23.1 %collective-permute-start.11 = (bf16[192,3072]{1,0:T(8,128)(2,1)S(1)}, bf16[192,3072]{1,0:T(8,128)(2,1)}, u32[]{:S(2)}, u32[]{:S(2)}) collective-permute-start(bf16[192,3072]{1,0:T(8,128)(2,1)S(1)} %pad_maximum_fusion), channel_id=1, source_target_pairs={{0,62},{2,0},{4,2},{6,4},{8,6},{10,8},{12,10},{14,12},{16,14},{18,... | collective-permute-start | bytes 3538952 | tf_op jit(solution)/shard_map/ppermute | solution.py:29
  30.2 11.3 %collective-permute-done.5 = bf16[24,960]{1,0:T(8,128)(2,1)S(1)} collective-permute-done((bf16[24,960]{1,0:T(8,128)(2,1)S(1)}, bf16[24,960]{1,0:T(8,128)(2,1)S(1)}, u32[]{:S(2)}, u32[]{:S(2)}) %collective-permute-start.5) | collective-permute-done | bytes 46112 | tf_op jit(solution)/shard_map/ppermute | solution.py:117
  41.5 8.1 %collective-permute-start.8 = (bf16[24,960]{1,0:T(8,128)(2,1)S(1)}, bf16[24,960]{1,0:T(8,128)(2,1)S(1)}, u32[]{:S(2)}, u32[]{:S(2)}) collective-permute-start(bf16[24,960]{1,0:T(8,128)(2,1)S(1)} %pad_maximum_fusion.2), channel_id=1, source_target_pairs={{0,54},{2,56},{4,58},{6,60},{8,62},{10,0},{12,2},{14,4},{16,6},{18... | collective-permute-start | bytes 138248 | tf_op jit(solution)/shard_map/ppermute | solution.py:117
  49.7 3.0 %collective-permute-done.6 = bf16[16,960]{1,0:T(8,128)(2,1)S(1)} collective-permute-done((bf16[16,960]{1,0:T(8,128)(2,1)S(1)}, bf16[16,960]{1,0:T(8,128)(2,1)S(1)}, u32[]{:S(2)}, u32[]{:S(2)}) %collective-permute-start.6) | collective-permute-done | bytes 30752 | tf_op jit(solution)/shard_map/ppermute | solution.py:117
  52.8 8.2 %collective-permute-start.9 = (bf16[16,960]{1,0:T(8,128)(2,1)S(1)}, bf16[16,960]{1,0:T(8,128)(2,1)S(1)}, u32[]{:S(2)}, u32[]{:S(2)}) collective-permute-start(bf16[16,960]{1,0:T(8,128)(2,1)S(1)} %slice.300), channel_id=1, source_target_pairs={{0,54},{2,56},{4,58},{6,60},{8,62},{10,0},{12,2},{14,4},{16,6},{18... | collective-permute-start | bytes 92168 | tf_op jit(solution)/shard_map/ppermute | solution.py:117
  60.9 1.5 collective-permute-done.7
  62.5 7.7 %collective-permute-start.12 = (bf16[192,3072]{1,0:T(8,128)(2,1)}, bf16[192,3072]{1,0:T(8,128)(2,1)}, u32[]{:S(2)}, u32[]{:S(2)}) collective-permute-start(bf16[192,3072]{1,0:T(8,128)(2,1)} %collective-permute-done.11), channel_id=1, source_target_pairs={{0,1},{1,0},{2,3},{3,2},{4,5},{5,4},{6,7},{7,6},{8,9},{9,8},{10,11... | collective-permute-start | bytes 3538952 | tf_op jit(solution)/shard_map/ppermute | solution.py:121
  70.2 4.9 %collective-permute-start.10 = (bf16[8,960]{1,0:T(8,128)(2,1)S(1)}, bf16[8,960]{1,0:T(8,128)(2,1)S(1)}, u32[]{:S(2)}, u32[]{:S(2)}) collective-permute-start(bf16[8,960]{1,0:T(8,128)(2,1)S(1)} %get-tuple-element.341), channel_id=1, source_target_pairs={{0,54},{2,56},{4,58},{6,60},{8,62},{10,0},{12,2},{14,4},{16,6},{18... | collective-permute-start | bytes 46088 | tf_op jit(solution)/shard_map/ppermute | solution.py:117
  75.3 4.2 %collective-permute-start.28 = (bf16[3072,512]{1,0:T(8,128)(2,1)}, bf16[3072,512]{1,0:T(8,128)(2,1)}, u32[]{:S(2)}, u32[]{:S(2)}) collective-permute-start(bf16[3072,512]{1,0:T(8,128)(2,1)} %up.1), channel_id=1, source_target_pairs={{0,1},{1,0},{2,3},{3,2},{4,5},{5,4},{6,7},{7,6},{8,9},{9,8},{10,11... | collective-permute-start | bytes 9437192 | tf_op jit(solution)/shard_map/ppermute | solution.py:121
  79.4 2.7 collective-permute-done.13
  82.2 4.4 %collective-permute-start.14 = (bf16[192,3072]{1,0:T(8,128)(2,1)}, bf16[192,3072]{1,0:T(8,128)(2,1)S(1)}, u32[]{:S(2)}, u32[]{:S(2)}) collective-permute-start(bf16[192,3072]{1,0:T(8,128)(2,1)} %collective-permute-done.13), channel_id=1, source_target_pairs={{0,1},{1,0},{2,3},{3,2},{4,5},{5,4},{6,7},{7,6},{8,9},{9,8},{10,11... | collective-permute-start | bytes 3538952 | tf_op jit(solution)/shard_map/ppermute | solution.py:121
  86.6 1.6 fusion.20
  88.6 1.6 fusion.17
  90.2 1.7 fusion.3
  92.3 38.5 %while.38 = (s32[]{:T(128)}, f32[8,3072]{1,0:T(8,128)S(1)}, f32[8,3072]{1,0:T(8,128)S(1)}, f32[7,8,3072]{2,1,0:T(8,128)S(1)}, s32[]{:T(128)}, /*index=5*/s32[]{:...) while((s32[]{:T(128)}, f32[8,3072]{1,0:T(8,128)S(1)}, f32[8,3072]{1,0:T(8,128)S(1)}, ...), condition=%wide.region_3.4_spmd, body=%wide.region_2.3_spmd.sunk | while | flops 196622 | bytes 1179975 | solution.py:95
  92.3 1.9 collective-permute-start
  94.2 5.0 %collective-permute-start.1 = (bf16[8,3072]{1,0:T(8,128)(2,1)S(1)}, bf16[8,3072]{1,0:T(8,128)(2,1)S(1)}, u32[]{:S(2)}, u32[]{:S(2)}) collective-permute-start(bf16[8,3072]{1,0:T(8,128)(2,1)S(1)} %convert_element_type.196), channel_id=1, source_target_pairs={{0,10},{2,12},{4,14},{6,16},{8,18},{10,20},{12,22},{14,24},{16,26}... | collective-permute-start | bytes 147464 | tf_op jit(solution)/shard_map/while/body/eval_jaxpr/ppermute | solution.py:117
  99.2 4.1 %collective-permute-done = bf16[8,3072]{1,0:T(8,128)(2,1)S(1)} collective-permute-done((bf16[8,3072]{1,0:T(8,128)(2,1)S(1)}, bf16[8,3072]{1,0:T(8,128)(2,1)S(1)}, u32[]{:S(2)}, u32[]{:S(2)}) %collective-permute-start) | collective-permute-done | bytes 49184 | tf_op jit(solution)/shard_map/while/body/eval_jaxpr/ppermute | solution.py:117
  103.3 1.7 collective-permute-done.1
  105.1 1.3 collective-permute-start
  106.4 5.6 %collective-permute-start.1 = (bf16[8,3072]{1,0:T(8,128)(2,1)S(1)}, bf16[8,3072]{1,0:T(8,128)(2,1)S(1)}, u32[]{:S(2)}, u32[]{:S(2)}) collective-permute-start(bf16[8,3072]{1,0:T(8,128)(2,1)S(1)} %convert_element_type.196), channel_id=1, source_target_pairs={{0,10},{2,12},{4,14},{6,16},{8,18},{10,20},{12,22},{14,24},{16,26}... | collective-permute-start | bytes 147464 | tf_op jit(solution)/shard_map/while/body/eval_jaxpr/ppermute | solution.py:117
  112.1 3.6 %collective-permute-done = bf16[8,3072]{1,0:T(8,128)(2,1)S(1)} collective-permute-done((bf16[8,3072]{1,0:T(8,128)(2,1)S(1)}, bf16[8,3072]{1,0:T(8,128)(2,1)S(1)}, u32[]{:S(2)}, u32[]{:S(2)}) %collective-permute-start) | collective-permute-done | bytes 49184 | tf_op jit(solution)/shard_map/while/body/eval_jaxpr/ppermute | solution.py:117
  115.7 2.0 collective-permute-done.1
  117.8 1.2 collective-permute-start
  119.0 5.8 %collective-permute-start.1 = (bf16[8,3072]{1,0:T(8,128)(2,1)S(1)}, bf16[8,3072]{1,0:T(8,128)(2,1)S(1)}, u32[]{:S(2)}, u32[]{:S(2)}) collective-permute-start(bf16[8,3072]{1,0:T(8,128)(2,1)S(1)} %convert_element_type.196), channel_id=1, source_target_pairs={{0,10},{2,12},{4,14},{6,16},{8,18},{10,20},{12,22},{14,24},{16,26}... | collective-permute-start | bytes 147464 | tf_op jit(solution)/shard_map/while/body/eval_jaxpr/ppermute | solution.py:117
  124.7 2.1 collective-permute-done
  126.8 3.9 %collective-permute-done.1 = bf16[8,3072]{1,0:T(8,128)(2,1)S(1)} collective-permute-done((bf16[8,3072]{1,0:T(8,128)(2,1)S(1)}, bf16[8,3072]{1,0:T(8,128)(2,1)S(1)}, u32[]{:S(2)}, u32[]{:S(2)}) %collective-permute-start.1) | collective-permute-done | bytes 49184 | tf_op jit(solution)/shard_map/while/body/eval_jaxpr/ppermute | solution.py:117
  131.1 7.9 %collective-permute-start.15 = (bf16[8,3072]{1,0:T(8,128)(2,1)S(1)}, bf16[8,3072]{1,0:T(8,128)(2,1)S(1)}, u32[]{:S(2)}, u32[]{:S(2)}) collective-permute-start(bf16[8,3072]{1,0:T(8,128)(2,1)S(1)} %get-tuple-element.319), channel_id=1, source_target_pairs={{0,22},{2,24},{4,26},{6,28},{8,30},{10,32},{12,34},{14,36},{16,38}... | collective-permute-start | bytes 147464 | tf_op jit(solution)/shard_map/ppermute | solution.py:117
  139.0 6.9 %collective-permute-start.16 = (bf16[8,3072]{1,0:T(8,128)(2,1)S(1)}, bf16[8,3072]{1,0:T(8,128)(2,1)S(1)}, u32[]{:S(2)}, u32[]{:S(2)}) collective-permute-start(bf16[8,3072]{1,0:T(8,128)(2,1)S(1)} %get-tuple-element.319), channel_id=1, source_target_pairs={{0,42},{2,44},{4,46},{6,48},{8,50},{10,52},{12,54},{14,56},{16,58}... | collective-permute-start | bytes 147464 | tf_op jit(solution)/shard_map/ppermute | solution.py:117
  146.4 6.2 %collective-permute-done.15 = bf16[8,3072]{1,0:T(8,128)(2,1)S(1)} collective-permute-done((bf16[8,3072]{1,0:T(8,128)(2,1)S(1)}, bf16[8,3072]{1,0:T(8,128)(2,1)S(1)}, u32[]{:S(2)}, u32[]{:S(2)}) %collective-permute-start.15) | collective-permute-done | bytes 49184 | tf_op jit(solution)/shard_map/ppermute | solution.py:117
  152.6 2.6 collective-permute-done.16
  155.3 1.9 collective-permute-start.17
  157.2 3.6 %collective-permute-start.18 = (bf16[24,3072]{1,0:T(8,128)(2,1)S(1)}, bf16[24,3072]{1,0:T(8,128)(2,1)S(1)}, u32[]{:S(2)}, u32[]{:S(2)}) collective-permute-start(bf16[24,3072]{1,0:T(8,128)(2,1)S(1)} %pad_maximum_fusion.1), channel_id=1, source_target_pairs={{0,62},{2,0},{4,2},{6,4},{8,6},{10,8},{12,10},{14,12},{16,14},{18,... | collective-permute-start | bytes 442376 | tf_op jit(solution)/shard_map/ppermute | solution.py:117
  160.8 3.0 %collective-permute-done.17 = bf16[24,3072]{1,0:T(8,128)(2,1)S(1)} collective-permute-done((bf16[24,3072]{1,0:T(8,128)(2,1)S(1)}, bf16[24,3072]{1,0:T(8,128)(2,1)S(1)}, u32[]{:S(2)}, u32[]{:S(2)}) %collective-permute-start.17) | collective-permute-done | bytes 147488 | tf_op jit(solution)/shard_map/ppermute | solution.py:117
  163.9 3.3 %collective-permute-start.20 = (bf16[24,3072]{1,0:T(8,128)(2,1)S(1)}, bf16[24,3072]{1,0:T(8,128)(2,1)S(1)}, u32[]{:S(2)}, u32[]{:S(2)}) collective-permute-start(bf16[24,3072]{1,0:T(8,128)(2,1)S(1)} %collective-permute-done.18), channel_id=1, source_target_pairs={{0,62},{2,0},{4,2},{6,4},{8,6},{10,8},{12,10},{14,12},{16,14},{18,... | collective-permute-start | bytes 442376 | tf_op jit(solution)/shard_map/ppermute | solution.py:117
  167.2 3.8 %collective-permute-done.19 = bf16[24,3072]{1,0:T(8,128)(2,1)S(1)} collective-permute-done((bf16[24,3072]{1,0:T(8,128)(2,1)S(1)}, bf16[24,3072]{1,0:T(8,128)(2,1)S(1)}, u32[]{:S(2)}, u32[]{:S(2)}) %collective-permute-start.19) | collective-permute-done | bytes 147488 | tf_op jit(solution)/shard_map/ppermute | solution.py:117
  171.2 3.6 %collective-permute-start.22 = (bf16[24,3072]{1,0:T(8,128)(2,1)S(1)}, bf16[24,3072]{1,0:T(8,128)(2,1)S(1)}, u32[]{:S(2)}, u32[]{:S(2)}) collective-permute-start(bf16[24,3072]{1,0:T(8,128)(2,1)S(1)} %collective-permute-done.20), channel_id=1, source_target_pairs={{0,62},{2,0},{4,2},{6,4},{8,6},{10,8},{12,10},{14,12},{16,14},{18,... | collective-permute-start | bytes 442376 | tf_op jit(solution)/shard_map/ppermute | solution.py:117
  174.8 3.9 %collective-permute-done.21 = bf16[24,3072]{1,0:T(8,128)(2,1)S(1)} collective-permute-done((bf16[24,3072]{1,0:T(8,128)(2,1)S(1)}, bf16[24,3072]{1,0:T(8,128)(2,1)S(1)}, u32[]{:S(2)}, u32[]{:S(2)}) %collective-permute-start.21) | collective-permute-done | bytes 147488 | tf_op jit(solution)/shard_map/ppermute | solution.py:117
  178.9 3.3 %collective-permute-start.24 = (bf16[24,3072]{1,0:T(8,128)(2,1)S(1)}, bf16[24,3072]{1,0:T(8,128)(2,1)S(1)}, u32[]{:S(2)}, u32[]{:S(2)}) collective-permute-start(bf16[24,3072]{1,0:T(8,128)(2,1)S(1)} %collective-permute-done.22), channel_id=1, source_target_pairs={{0,62},{2,0},{4,2},{6,4},{8,6},{10,8},{12,10},{14,12},{16,14},{18,... | collective-permute-start | bytes 442376 | tf_op jit(solution)/shard_map/ppermute | solution.py:117
  182.2 3.6 %collective-permute-done.23 = bf16[24,3072]{1,0:T(8,128)(2,1)S(1)} collective-permute-done((bf16[24,3072]{1,0:T(8,128)(2,1)S(1)}, bf16[24,3072]{1,0:T(8,128)(2,1)S(1)}, u32[]{:S(2)}, u32[]{:S(2)}) %collective-permute-start.23) | collective-permute-done | bytes 147488 | tf_op jit(solution)/shard_map/ppermute | solution.py:117
  186.2 3.3 %collective-permute-start.26 = (bf16[24,3072]{1,0:T(8,128)(2,1)S(1)}, bf16[24,3072]{1,0:T(8,128)(2,1)S(1)}, u32[]{:S(2)}, u32[]{:S(2)}) collective-permute-start(bf16[24,3072]{1,0:T(8,128)(2,1)S(1)} %collective-permute-done.24), channel_id=1, source_target_pairs={{0,62},{2,0},{4,2},{6,4},{8,6},{10,8},{12,10},{14,12},{16,14},{18,... | collective-permute-start | bytes 442376 | tf_op jit(solution)/shard_map/ppermute | solution.py:117
  189.5 3.0 %collective-permute-done.25 = bf16[24,3072]{1,0:T(8,128)(2,1)S(1)} collective-permute-done((bf16[24,3072]{1,0:T(8,128)(2,1)S(1)}, bf16[24,3072]{1,0:T(8,128)(2,1)S(1)}, u32[]{:S(2)}, u32[]{:S(2)}) %collective-permute-start.25) | collective-permute-done | bytes 147488 | tf_op jit(solution)/shard_map/ppermute | solution.py:117
  193.8 1.9 copy-done.1
  195.7 11.0 %experts.1 = f32[264,3072]{1,0:T(8,128)S(1)} custom-call(bf16[264,3072]{1,0:T(8,128)(2,1)S(1)} %constant_dynamic-update-slice_fusion.7.x, f32[264,1]{1,0:T(8,128)S(1)} %mul.125.factor, bf16[3072,512]{1,0:T(8,128)(2,1)S(1)} %copy-done.1, bf16[3072,512]{1,0:T(8,128)(2,1)} %up.1, bf16[512,3072]{1,0:T(8,128)(2,1)} %down.1, ...), custom_call_target="tpu_custom_call" | custom-call | flops 4982833152 | bytes 18874368 | tf_op jit(solution)/shard_map/experts/pallas_call | solution.py:223
  206.9 1.4 copy-done.2
  208.4 37.8 %while.39 = (s32[]{:T(128)}, bf16[24,3072]{1,0:T(8,128)(2,1)S(1)}, bf16[24,3072]{1,0:T(8,128)(2,1)S(1)}, f32[11,24,3072]{2,1,0:T(8,128)}, s32[]{:T(128)}, /*inde...) while((s32[]{:T(128)}, bf16[24,3072]{1,0:T(8,128)(2,1)S(1)}, ...), condition=%wide.region_8.9_spmd, body=%wide.region_7.8_spmd.sunk | while | flops 442379 | bytes 2359597 | solution.py:173
  208.4 3.4 %collective-permute-start.2 = (bf16[24,3072]{1,0:T(8,128)(2,1)S(1)}, bf16[24,3072]{1,0:T(8,128)(2,1)S(1)}, u32[]{:S(2)}, u32[]{:S(2)}) collective-permute-start(bf16[24,3072]{1,0:T(8,128)(2,1)S(1)} %get-tuple-element.479), channel_id=1, source_target_pairs={{0,62},{2,0},{4,2},{6,4},{8,6},{10,8},{12,10},{14,12},{16,14},{18,... | collective-permute-start | bytes 442376 | tf_op jit(solution)/shard_map/while/body/eval_jaxpr/ppermute | solution.py:117
  211.9 3.0 %collective-permute-done.2 = bf16[24,3072]{1,0:T(8,128)(2,1)S(1)} collective-permute-done((bf16[24,3072]{1,0:T(8,128)(2,1)S(1)}, bf16[24,3072]{1,0:T(8,128)(2,1)S(1)}, u32[]{:S(2)}, u32[]{:S(2)}) %collective-permute-start.2) | collective-permute-done | bytes 147488 | tf_op jit(solution)/shard_map/while/body/eval_jaxpr/ppermute | solution.py:117
  214.9 3.4 %collective-permute-done.3 = bf16[24,3072]{1,0:T(8,128)(2,1)S(1)} collective-permute-done((bf16[24,3072]{1,0:T(8,128)(2,1)S(1)}, bf16[24,3072]{1,0:T(8,128)(2,1)S(1)}, u32[]{:S(2)}, u32[]{:S(2)}) %collective-permute-start.3) | collective-permute-done | bytes 147488 | tf_op jit(solution)/shard_map/while/body/eval_jaxpr/ppermute | solution.py:117
  219.5 2.0 collective-permute-start.3
  221.5 3.1 %collective-permute-done.2 = bf16[24,3072]{1,0:T(8,128)(2,1)S(1)} collective-permute-done((bf16[24,3072]{1,0:T(8,128)(2,1)S(1)}, bf16[24,3072]{1,0:T(8,128)(2,1)S(1)}, u32[]{:S(2)}, u32[]{:S(2)}) %collective-permute-start.2) | collective-permute-done | bytes 147488 | tf_op jit(solution)/shard_map/while/body/eval_jaxpr/ppermute | solution.py:117
  224.6 1.3 collective-permute-done.3
  227.1 2.4 collective-permute-start.2
  229.4 2.9 %collective-permute-done.2 = bf16[24,3072]{1,0:T(8,128)(2,1)S(1)} collective-permute-done((bf16[24,3072]{1,0:T(8,128)(2,1)S(1)}, bf16[24,3072]{1,0:T(8,128)(2,1)S(1)}, u32[]{:S(2)}, u32[]{:S(2)}) %collective-permute-start.2) | collective-permute-done | bytes 147488 | tf_op jit(solution)/shard_map/while/body/eval_jaxpr/ppermute | solution.py:117
  232.3 4.3 %collective-permute-done.3 = bf16[24,3072]{1,0:T(8,128)(2,1)S(1)} collective-permute-done((bf16[24,3072]{1,0:T(8,128)(2,1)S(1)}, bf16[24,3072]{1,0:T(8,128)(2,1)S(1)}, u32[]{:S(2)}, u32[]{:S(2)}) %collective-permute-start.3) | collective-permute-done | bytes 147488 | tf_op jit(solution)/shard_map/while/body/eval_jaxpr/ppermute | solution.py:117
  238.1 1.8 collective-permute-start.3
  239.8 5.2 %collective-permute-done.2 = bf16[24,3072]{1,0:T(8,128)(2,1)S(1)} collective-permute-done((bf16[24,3072]{1,0:T(8,128)(2,1)S(1)}, bf16[24,3072]{1,0:T(8,128)(2,1)S(1)}, u32[]{:S(2)}, u32[]{:S(2)}) %collective-permute-start.2) | collective-permute-done | bytes 147488 | tf_op jit(solution)/shard_map/while/body/eval_jaxpr/ppermute | solution.py:117
  245.1 1.1 fusion.61
  246.3 3.2 %collective-permute-start.31 = (bf16[24,3072]{1,0:T(8,128)(2,1)S(1)}, bf16[24,3072]{1,0:T(8,128)(2,1)S(1)}, u32[]{:S(2)}, u32[]{:S(2)}) collective-permute-start(bf16[24,3072]{1,0:T(8,128)(2,1)S(1)} %get-tuple-element.297), channel_id=1, source_target_pairs={{0,62},{2,0},{4,2},{6,4},{8,6},{10,8},{12,10},{14,12},{16,14},{18,... | collective-permute-start | bytes 442376 | tf_op jit(solution)/shard_map/ppermute | solution.py:117
  249.5 7.7 %collective-permute-done.30 = bf16[24,3072]{1,0:T(8,128)(2,1)S(1)} collective-permute-done((bf16[24,3072]{1,0:T(8,128)(2,1)S(1)}, bf16[24,3072]{1,0:T(8,128)(2,1)S(1)}, u32[]{:S(2)}, u32[]{:S(2)}) %collective-permute-start.30) | collective-permute-done | bytes 147488 | tf_op jit(solution)/shard_map/ppermute | solution.py:117
  258.4 13.4 %collective-permute-start.33 = (bf16[8,3072]{1,0:T(8,128)(2,1)S(1)}, bf16[8,3072]{1,0:T(8,128)(2,1)S(1)}, u32[]{:S(2)}, u32[]{:S(2)}) collective-permute-start(bf16[8,3072]{1,0:T(8,128)(2,1)S(1)} %get-tuple-element.333), channel_id=1, source_target_pairs={{0,22},{2,24},{4,26},{6,28},{8,30},{10,32},{12,34},{14,36},{16,38}... | collective-permute-start | bytes 147464 | tf_op jit(solution)/shard_map/ppermute | solution.py:117
  271.8 3.1 %collective-permute-done.32 = bf16[8,3072]{1,0:T(8,128)(2,1)S(1)} collective-permute-done((bf16[8,3072]{1,0:T(8,128)(2,1)S(1)}, bf16[8,3072]{1,0:T(8,128)(2,1)S(1)}, u32[]{:S(2)}, u32[]{:S(2)}) %collective-permute-start.32) | collective-permute-done | bytes 49184 | tf_op jit(solution)/shard_map/ppermute | solution.py:117
  (131 shorter events, 15.3 us)
Async XLA Ops:
  0.0 5.5 %copy-start = (bf16[8,512,128]{2,1,0:T(8,128)(2,1)S(1)}, bf16[8,512,128]{2,1,0:T(8,128)(2,1)}, u32[]{:S(2)}) copy-start(bf16[8,512,128]{2,1,0:T(8,128)(2,1)} %param.20) | copy-start | bytes 3145732
  0.0 2.2 collective-permute-start.4
  0.0 193.7 %collective-permute-start.27 = (bf16[3072,512]{1,0:T(8,128)(2,1)}, bf16[3072,512]{1,0:T(8,128)(2,1)}, u32[]{:S(2)}, u32[]{:S(2)}) collective-permute-start(bf16[3072,512]{1,0:T(8,128)(2,1)} %gate.1), channel_id=1, source_target_pairs={{0,1},{1,0},{2,3},{3,2},{4,5},{5,4},{6,7},{7,6},{8,9},{9,8},{10,11... | collective-permute-start | bytes 9437192 | tf_op jit(solution)/shard_map/ppermute | solution.py:121
  3.4 1.2 copy-start.3
  3.4 1.2 copy-start.4
  5.5 69.8 %copy-start.7 = (bf16[3072]{0:T(1024)(128)(2,1)S(1)}, bf16[3072]{0:T(1024)(128)(2,1)}, u32[]{:S(2)}) copy-start(bf16[3072]{0:T(1024)(128)(2,1)} %param.24) | copy-start | bytes 18436
  6.1 56.3 %collective-permute-start.11 = (bf16[192,3072]{1,0:T(8,128)(2,1)S(1)}, bf16[192,3072]{1,0:T(8,128)(2,1)}, u32[]{:S(2)}, u32[]{:S(2)}) collective-permute-start(bf16[192,3072]{1,0:T(8,128)(2,1)S(1)} %pad_maximum_fusion), channel_id=1, source_target_pairs={{0,62},{2,0},{4,2},{6,4},{8,6},{10,8},{12,10},{14,12},{16,14},{18,... | collective-permute-start | bytes 3538952 | tf_op jit(solution)/shard_map/ppermute | solution.py:29
  30.0 11.6 %collective-permute-start.5 = (bf16[24,960]{1,0:T(8,128)(2,1)S(1)}, bf16[24,960]{1,0:T(8,128)(2,1)S(1)}, u32[]{:S(2)}, u32[]{:S(2)}) collective-permute-start(bf16[24,960]{1,0:T(8,128)(2,1)S(1)} %maximum_maximum_fusion), channel_id=1, source_target_pairs={{0,10},{2,12},{4,14},{6,16},{8,18},{10,20},{12,22},{14,24},{16,26}... | collective-permute-start | bytes 138248 | tf_op jit(solution)/shard_map/ppermute | solution.py:117
  41.5 11.1 %collective-permute-start.6 = (bf16[16,960]{1,0:T(8,128)(2,1)S(1)}, bf16[16,960]{1,0:T(8,128)(2,1)S(1)}, u32[]{:S(2)}, u32[]{:S(2)}) collective-permute-start(bf16[16,960]{1,0:T(8,128)(2,1)S(1)} %slice.290), channel_id=1, source_target_pairs={{0,10},{2,12},{4,14},{6,16},{8,18},{10,20},{12,22},{14,24},{16,26}... | collective-permute-start | bytes 92168 | tf_op jit(solution)/shard_map/ppermute | solution.py:117
  41.5 11.2 %collective-permute-start.8 = (bf16[24,960]{1,0:T(8,128)(2,1)S(1)}, bf16[24,960]{1,0:T(8,128)(2,1)S(1)}, u32[]{:S(2)}, u32[]{:S(2)}) collective-permute-start(bf16[24,960]{1,0:T(8,128)(2,1)S(1)} %pad_maximum_fusion.2), channel_id=1, source_target_pairs={{0,54},{2,56},{4,58},{6,60},{8,62},{10,0},{12,2},{14,4},{16,6},{18... | collective-permute-start | bytes 138248 | tf_op jit(solution)/shard_map/ppermute | solution.py:117
  52.7 9.8 %collective-permute-start.7 = (bf16[8,960]{1,0:T(8,128)(2,1)S(1)}, bf16[8,960]{1,0:T(8,128)(2,1)S(1)}, u32[]{:S(2)}, u32[]{:S(2)}) collective-permute-start(bf16[8,960]{1,0:T(8,128)(2,1)S(1)} %slice.291), channel_id=1, source_target_pairs={{0,10},{2,12},{4,14},{6,16},{8,18},{10,20},{12,22},{14,24},{16,26}... | collective-permute-start | bytes 46088 | tf_op jit(solution)/shard_map/ppermute | solution.py:117
  52.8 17.5 %collective-permute-start.9 = (bf16[16,960]{1,0:T(8,128)(2,1)S(1)}, bf16[16,960]{1,0:T(8,128)(2,1)S(1)}, u32[]{:S(2)}, u32[]{:S(2)}) collective-permute-start(bf16[16,960]{1,0:T(8,128)(2,1)S(1)} %slice.300), channel_id=1, source_target_pairs={{0,54},{2,56},{4,58},{6,60},{8,62},{10,0},{12,2},{14,4},{16,6},{18... | collective-permute-start | bytes 92168 | tf_op jit(solution)/shard_map/ppermute | solution.py:117
  62.4 19.8 %collective-permute-start.13 = (bf16[192,3072]{1,0:T(8,128)(2,1)}, bf16[192,3072]{1,0:T(8,128)(2,1)}, u32[]{:S(2)}, u32[]{:S(2)}) collective-permute-start(bf16[192,3072]{1,0:T(8,128)(2,1)} %collective-permute-done.11), channel_id=1, source_target_pairs={{0,62},{2,0},{4,2},{6,4},{8,6},{10,8},{12,10},{14,12},{16,14},{18,... | collective-permute-start | bytes 3538952 | tf_op jit(solution)/shard_map/ppermute | solution.py:29
  62.5 27.7 %collective-permute-start.12 = (bf16[192,3072]{1,0:T(8,128)(2,1)}, bf16[192,3072]{1,0:T(8,128)(2,1)}, u32[]{:S(2)}, u32[]{:S(2)}) collective-permute-start(bf16[192,3072]{1,0:T(8,128)(2,1)} %collective-permute-done.11), channel_id=1, source_target_pairs={{0,1},{1,0},{2,3},{3,2},{4,5},{5,4},{6,7},{7,6},{8,9},{9,8},{10,11... | collective-permute-start | bytes 3538952 | tf_op jit(solution)/shard_map/ppermute | solution.py:121
  70.2 16.4 %collective-permute-start.10 = (bf16[8,960]{1,0:T(8,128)(2,1)S(1)}, bf16[8,960]{1,0:T(8,128)(2,1)S(1)}, u32[]{:S(2)}, u32[]{:S(2)}) collective-permute-start(bf16[8,960]{1,0:T(8,128)(2,1)S(1)} %get-tuple-element.341), channel_id=1, source_target_pairs={{0,54},{2,56},{4,58},{6,60},{8,62},{10,0},{12,2},{14,4},{16,6},{18... | collective-permute-start | bytes 46088 | tf_op jit(solution)/shard_map/ppermute | solution.py:117
  75.3 118.5 %collective-permute-start.28 = (bf16[3072,512]{1,0:T(8,128)(2,1)}, bf16[3072,512]{1,0:T(8,128)(2,1)}, u32[]{:S(2)}, u32[]{:S(2)}) collective-permute-start(bf16[3072,512]{1,0:T(8,128)(2,1)} %up.1), channel_id=1, source_target_pairs={{0,1},{1,0},{2,3},{3,2},{4,5},{5,4},{6,7},{7,6},{8,9},{9,8},{10,11... | collective-permute-start | bytes 9437192 | tf_op jit(solution)/shard_map/ppermute | solution.py:121
  82.2 9.7 %collective-permute-start.14 = (bf16[192,3072]{1,0:T(8,128)(2,1)}, bf16[192,3072]{1,0:T(8,128)(2,1)S(1)}, u32[]{:S(2)}, u32[]{:S(2)}) collective-permute-start(bf16[192,3072]{1,0:T(8,128)(2,1)} %collective-permute-done.13), channel_id=1, source_target_pairs={{0,1},{1,0},{2,3},{3,2},{4,5},{5,4},{6,7},{7,6},{8,9},{9,8},{10,11... | collective-permute-start | bytes 3538952 | tf_op jit(solution)/shard_map/ppermute | solution.py:121
  92.2 38.6 %copy-start.5 = (bf16[8,3072]{1,0:T(8,128)(2,1)S(1)}, bf16[8,3072]{1,0:T(8,128)(2,1)}, u32[]{:S(2)}) copy-start(bf16[8,3072]{1,0:T(8,128)(2,1)} %param.17) | copy-start | bytes 147460
  92.3 11.1 %collective-permute-start = (bf16[8,3072]{1,0:T(8,128)(2,1)S(1)}, bf16[8,3072]{1,0:T(8,128)(2,1)S(1)}, u32[]{:S(2)}, u32[]{:S(2)}) collective-permute-start(bf16[8,3072]{1,0:T(8,128)(2,1)S(1)} %convert_element_type.194), channel_id=1, source_target_pairs={{0,54},{2,56},{4,58},{6,60},{8,62},{10,0},{12,2},{14,4},{16,6},{18... | collective-permute-start | bytes 147464 | tf_op jit(solution)/shard_map/while/body/eval_jaxpr/ppermute | solution.py:117
  94.2 10.8 %collective-permute-start.1 = (bf16[8,3072]{1,0:T(8,128)(2,1)S(1)}, bf16[8,3072]{1,0:T(8,128)(2,1)S(1)}, u32[]{:S(2)}, u32[]{:S(2)}) collective-permute-start(bf16[8,3072]{1,0:T(8,128)(2,1)S(1)} %convert_element_type.196), channel_id=1, source_target_pairs={{0,10},{2,12},{4,14},{6,16},{8,18},{10,20},{12,22},{14,24},{16,26}... | collective-permute-start | bytes 147464 | tf_op jit(solution)/shard_map/while/body/eval_jaxpr/ppermute | solution.py:117
  105.1 10.6 %collective-permute-start = (bf16[8,3072]{1,0:T(8,128)(2,1)S(1)}, bf16[8,3072]{1,0:T(8,128)(2,1)S(1)}, u32[]{:S(2)}, u32[]{:S(2)}) collective-permute-start(bf16[8,3072]{1,0:T(8,128)(2,1)S(1)} %convert_element_type.194), channel_id=1, source_target_pairs={{0,54},{2,56},{4,58},{6,60},{8,62},{10,0},{12,2},{14,4},{16,6},{18... | collective-permute-start | bytes 147464 | tf_op jit(solution)/shard_map/while/body/eval_jaxpr/ppermute | solution.py:117
  106.4 11.3 %collective-permute-start.1 = (bf16[8,3072]{1,0:T(8,128)(2,1)S(1)}, bf16[8,3072]{1,0:T(8,128)(2,1)S(1)}, u32[]{:S(2)}, u32[]{:S(2)}) collective-permute-start(bf16[8,3072]{1,0:T(8,128)(2,1)S(1)} %convert_element_type.196), channel_id=1, source_target_pairs={{0,10},{2,12},{4,14},{6,16},{8,18},{10,20},{12,22},{14,24},{16,26}... | collective-permute-start | bytes 147464 | tf_op jit(solution)/shard_map/while/body/eval_jaxpr/ppermute | solution.py:117
  117.8 9.0 %collective-permute-start = (bf16[8,3072]{1,0:T(8,128)(2,1)S(1)}, bf16[8,3072]{1,0:T(8,128)(2,1)S(1)}, u32[]{:S(2)}, u32[]{:S(2)}) collective-permute-start(bf16[8,3072]{1,0:T(8,128)(2,1)S(1)} %convert_element_type.194), channel_id=1, source_target_pairs={{0,54},{2,56},{4,58},{6,60},{8,62},{10,0},{12,2},{14,4},{16,6},{18... | collective-permute-start | bytes 147464 | tf_op jit(solution)/shard_map/while/body/eval_jaxpr/ppermute | solution.py:117
  119.0 11.8 %collective-permute-start.1 = (bf16[8,3072]{1,0:T(8,128)(2,1)S(1)}, bf16[8,3072]{1,0:T(8,128)(2,1)S(1)}, u32[]{:S(2)}, u32[]{:S(2)}) collective-permute-start(bf16[8,3072]{1,0:T(8,128)(2,1)S(1)} %convert_element_type.196), channel_id=1, source_target_pairs={{0,10},{2,12},{4,14},{6,16},{8,18},{10,20},{12,22},{14,24},{16,26}... | collective-permute-start | bytes 147464 | tf_op jit(solution)/shard_map/while/body/eval_jaxpr/ppermute | solution.py:117
  131.1 21.6 %collective-permute-start.15 = (bf16[8,3072]{1,0:T(8,128)(2,1)S(1)}, bf16[8,3072]{1,0:T(8,128)(2,1)S(1)}, u32[]{:S(2)}, u32[]{:S(2)}) collective-permute-start(bf16[8,3072]{1,0:T(8,128)(2,1)S(1)} %get-tuple-element.319), channel_id=1, source_target_pairs={{0,22},{2,24},{4,26},{6,28},{8,30},{10,32},{12,34},{14,36},{16,38}... | collective-permute-start | bytes 147464 | tf_op jit(solution)/shard_map/ppermute | solution.py:117
  139.0 16.3 %collective-permute-start.16 = (bf16[8,3072]{1,0:T(8,128)(2,1)S(1)}, bf16[8,3072]{1,0:T(8,128)(2,1)S(1)}, u32[]{:S(2)}, u32[]{:S(2)}) collective-permute-start(bf16[8,3072]{1,0:T(8,128)(2,1)S(1)} %get-tuple-element.319), channel_id=1, source_target_pairs={{0,42},{2,44},{4,46},{6,48},{8,50},{10,52},{12,54},{14,56},{16,58}... | collective-permute-start | bytes 147464 | tf_op jit(solution)/shard_map/ppermute | solution.py:117
  146.3 47.5 %collective-permute-start.29 = (bf16[512,3072]{1,0:T(8,128)(2,1)}, bf16[512,3072]{1,0:T(8,128)(2,1)}, u32[]{:S(2)}, u32[]{:S(2)}) collective-permute-start(bf16[512,3072]{1,0:T(8,128)(2,1)} %down.1), channel_id=1, source_target_pairs={{0,1},{1,0},{2,3},{3,2},{4,5},{5,4},{6,7},{7,6},{8,9},{9,8},{10,11... | collective-permute-start | bytes 9437192 | tf_op jit(solution)/shard_map/ppermute | solution.py:121
  155.3 37.3 %copy-start.6 = (bf16[3072,4]{0,1:T(4,128)(2,1)S(1)}, bf16[3072,4]{0,1:T(4,128)(2,1)}, u32[]{:S(2)}) copy-start(bf16[3072,4]{0,1:T(4,128)(2,1)} %param.25) | copy-start | bytes 73732
  155.3 8.5 %collective-permute-start.17 = (bf16[24,3072]{1,0:T(8,128)(2,1)S(1)}, bf16[24,3072]{1,0:T(8,128)(2,1)S(1)}, u32[]{:S(2)}, u32[]{:S(2)}) collective-permute-start(bf16[24,3072]{1,0:T(8,128)(2,1)S(1)} %pad_maximum_fusion.1), channel_id=1, source_target_pairs={{0,2},{2,4},{4,6},{6,8},{8,10},{10,12},{12,14},{14,16},{16,18},{18... | collective-permute-start | bytes 442376 | tf_op jit(solution)/shard_map/ppermute | solution.py:117
  157.2 6.7 %collective-permute-start.18 = (bf16[24,3072]{1,0:T(8,128)(2,1)S(1)}, bf16[24,3072]{1,0:T(8,128)(2,1)S(1)}, u32[]{:S(2)}, u32[]{:S(2)}) collective-permute-start(bf16[24,3072]{1,0:T(8,128)(2,1)S(1)} %pad_maximum_fusion.1), channel_id=1, source_target_pairs={{0,62},{2,0},{4,2},{6,4},{8,6},{10,8},{12,10},{14,12},{16,14},{18,... | collective-permute-start | bytes 442376 | tf_op jit(solution)/shard_map/ppermute | solution.py:117
  163.7 7.3 %collective-permute-start.19 = (bf16[24,3072]{1,0:T(8,128)(2,1)S(1)}, bf16[24,3072]{1,0:T(8,128)(2,1)S(1)}, u32[]{:S(2)}, u32[]{:S(2)}) collective-permute-start(bf16[24,3072]{1,0:T(8,128)(2,1)S(1)} %collective-permute-done.17), channel_id=1, source_target_pairs={{0,2},{2,4},{4,6},{6,8},{8,10},{10,12},{12,14},{14,16},{16,18},{18... | collective-permute-start | bytes 442376 | tf_op jit(solution)/shard_map/ppermute | solution.py:117
  163.9 7.2 %collective-permute-start.20 = (bf16[24,3072]{1,0:T(8,128)(2,1)S(1)}, bf16[24,3072]{1,0:T(8,128)(2,1)S(1)}, u32[]{:S(2)}, u32[]{:S(2)}) collective-permute-start(bf16[24,3072]{1,0:T(8,128)(2,1)S(1)} %collective-permute-done.18), channel_id=1, source_target_pairs={{0,62},{2,0},{4,2},{6,4},{8,6},{10,8},{12,10},{14,12},{16,14},{18,... | collective-permute-start | bytes 442376 | tf_op jit(solution)/shard_map/ppermute | solution.py:117
  171.0 7.7 %collective-permute-start.21 = (bf16[24,3072]{1,0:T(8,128)(2,1)S(1)}, bf16[24,3072]{1,0:T(8,128)(2,1)S(1)}, u32[]{:S(2)}, u32[]{:S(2)}) collective-permute-start(bf16[24,3072]{1,0:T(8,128)(2,1)S(1)} %collective-permute-done.19), channel_id=1, source_target_pairs={{0,2},{2,4},{4,6},{6,8},{8,10},{10,12},{12,14},{14,16},{16,18},{18... | collective-permute-start | bytes 442376 | tf_op jit(solution)/shard_map/ppermute | solution.py:117
  171.2 7.7 %collective-permute-start.22 = (bf16[24,3072]{1,0:T(8,128)(2,1)S(1)}, bf16[24,3072]{1,0:T(8,128)(2,1)S(1)}, u32[]{:S(2)}, u32[]{:S(2)}) collective-permute-start(bf16[24,3072]{1,0:T(8,128)(2,1)S(1)} %collective-permute-done.20), channel_id=1, source_target_pairs={{0,62},{2,0},{4,2},{6,4},{8,6},{10,8},{12,10},{14,12},{16,14},{18,... | collective-permute-start | bytes 442376 | tf_op jit(solution)/shard_map/ppermute | solution.py:117
  178.7 14.8 %copy-start.8 = (f32[33]{0:T(128)S(1)}, f32[33]{0:T(128)}, u32[]{:S(2)}) copy-start(f32[33]{0:T(128)} %constant.252.clone) | copy-start | bytes 400
  178.7 7.1 %collective-permute-start.23 = (bf16[24,3072]{1,0:T(8,128)(2,1)S(1)}, bf16[24,3072]{1,0:T(8,128)(2,1)S(1)}, u32[]{:S(2)}, u32[]{:S(2)}) collective-permute-start(bf16[24,3072]{1,0:T(8,128)(2,1)S(1)} %collective-permute-done.21), channel_id=1, source_target_pairs={{0,2},{2,4},{4,6},{6,8},{8,10},{10,12},{12,14},{14,16},{16,18},{18... | collective-permute-start | bytes 442376 | tf_op jit(solution)/shard_map/ppermute | solution.py:117
  178.9 7.3 %collective-permute-start.24 = (bf16[24,3072]{1,0:T(8,128)(2,1)S(1)}, bf16[24,3072]{1,0:T(8,128)(2,1)S(1)}, u32[]{:S(2)}, u32[]{:S(2)}) collective-permute-start(bf16[24,3072]{1,0:T(8,128)(2,1)S(1)} %collective-permute-done.22), channel_id=1, source_target_pairs={{0,62},{2,0},{4,2},{6,4},{8,6},{10,8},{12,10},{14,12},{16,14},{18,... | collective-permute-start | bytes 442376 | tf_op jit(solution)/shard_map/ppermute | solution.py:117
  185.8 6.7 %collective-permute-start.25 = (bf16[24,3072]{1,0:T(8,128)(2,1)S(1)}, bf16[24,3072]{1,0:T(8,128)(2,1)S(1)}, u32[]{:S(2)}, u32[]{:S(2)}) collective-permute-start(bf16[24,3072]{1,0:T(8,128)(2,1)S(1)} %collective-permute-done.23), channel_id=1, source_target_pairs={{0,2},{2,4},{4,6},{6,8},{8,10},{10,12},{12,14},{14,16},{16,18},{18... | collective-permute-start | bytes 442376 | tf_op jit(solution)/shard_map/ppermute | solution.py:117
  186.2 6.3 %collective-permute-start.26 = (bf16[24,3072]{1,0:T(8,128)(2,1)S(1)}, bf16[24,3072]{1,0:T(8,128)(2,1)S(1)}, u32[]{:S(2)}, u32[]{:S(2)}) collective-permute-start(bf16[24,3072]{1,0:T(8,128)(2,1)S(1)} %collective-permute-done.24), channel_id=1, source_target_pairs={{0,62},{2,0},{4,2},{6,4},{8,6},{10,8},{12,10},{14,12},{16,14},{18,... | collective-permute-start | bytes 442376 | tf_op jit(solution)/shard_map/ppermute | solution.py:117
  193.8 1.9 copy-start.1
  206.7 1.7 copy-start.2
  208.4 6.4 %collective-permute-start.2 = (bf16[24,3072]{1,0:T(8,128)(2,1)S(1)}, bf16[24,3072]{1,0:T(8,128)(2,1)S(1)}, u32[]{:S(2)}, u32[]{:S(2)}) collective-permute-start(bf16[24,3072]{1,0:T(8,128)(2,1)S(1)} %get-tuple-element.479), channel_id=1, source_target_pairs={{0,62},{2,0},{4,2},{6,4},{8,6},{10,8},{12,10},{14,12},{16,14},{18,... | collective-permute-start | bytes 442376 | tf_op jit(solution)/shard_map/while/body/eval_jaxpr/ppermute | solution.py:117
  211.9 6.4 %collective-permute-start.3 = (bf16[24,3072]{1,0:T(8,128)(2,1)S(1)}, bf16[24,3072]{1,0:T(8,128)(2,1)S(1)}, u32[]{:S(2)}, u32[]{:S(2)}) collective-permute-start(bf16[24,3072]{1,0:T(8,128)(2,1)S(1)} %get-tuple-element.478), channel_id=1, source_target_pairs={{0,2},{2,4},{4,6},{6,8},{8,10},{10,12},{12,14},{14,16},{16,18},{18... | collective-permute-start | bytes 442376 | tf_op jit(solution)/shard_map/while/body/eval_jaxpr/ppermute | solution.py:117
  219.3 5.3 %collective-permute-start.2 = (bf16[24,3072]{1,0:T(8,128)(2,1)S(1)}, bf16[24,3072]{1,0:T(8,128)(2,1)S(1)}, u32[]{:S(2)}, u32[]{:S(2)}) collective-permute-start(bf16[24,3072]{1,0:T(8,128)(2,1)S(1)} %get-tuple-element.479), channel_id=1, source_target_pairs={{0,62},{2,0},{4,2},{6,4},{8,6},{10,8},{12,10},{14,12},{16,14},{18,... | collective-permute-start | bytes 442376 | tf_op jit(solution)/shard_map/while/body/eval_jaxpr/ppermute | solution.py:117
  219.5 6.5 %collective-permute-start.3 = (bf16[24,3072]{1,0:T(8,128)(2,1)S(1)}, bf16[24,3072]{1,0:T(8,128)(2,1)S(1)}, u32[]{:S(2)}, u32[]{:S(2)}) collective-permute-start(bf16[24,3072]{1,0:T(8,128)(2,1)S(1)} %get-tuple-element.478), channel_id=1, source_target_pairs={{0,2},{2,4},{4,6},{6,8},{8,10},{10,12},{12,14},{14,16},{16,18},{18... | collective-permute-start | bytes 442376 | tf_op jit(solution)/shard_map/while/body/eval_jaxpr/ppermute | solution.py:117
  227.1 5.3 %collective-permute-start.2 = (bf16[24,3072]{1,0:T(8,128)(2,1)S(1)}, bf16[24,3072]{1,0:T(8,128)(2,1)S(1)}, u32[]{:S(2)}, u32[]{:S(2)}) collective-permute-start(bf16[24,3072]{1,0:T(8,128)(2,1)S(1)} %get-tuple-element.479), channel_id=1, source_target_pairs={{0,62},{2,0},{4,2},{6,4},{8,6},{10,8},{12,10},{14,12},{16,14},{18,... | collective-permute-start | bytes 442376 | tf_op jit(solution)/shard_map/while/body/eval_jaxpr/ppermute | solution.py:117
  229.4 7.1 %collective-permute-start.3 = (bf16[24,3072]{1,0:T(8,128)(2,1)S(1)}, bf16[24,3072]{1,0:T(8,128)(2,1)S(1)}, u32[]{:S(2)}, u32[]{:S(2)}) collective-permute-start(bf16[24,3072]{1,0:T(8,128)(2,1)S(1)} %get-tuple-element.478), channel_id=1, source_target_pairs={{0,2},{2,4},{4,6},{6,8},{8,10},{10,12},{12,14},{14,16},{16,18},{18... | collective-permute-start | bytes 442376 | tf_op jit(solution)/shard_map/while/body/eval_jaxpr/ppermute | solution.py:117
  237.7 7.4 %collective-permute-start.2 = (bf16[24,3072]{1,0:T(8,128)(2,1)S(1)}, bf16[24,3072]{1,0:T(8,128)(2,1)S(1)}, u32[]{:S(2)}, u32[]{:S(2)}) collective-permute-start(bf16[24,3072]{1,0:T(8,128)(2,1)S(1)} %get-tuple-element.479), channel_id=1, source_target_pairs={{0,62},{2,0},{4,2},{6,4},{8,6},{10,8},{12,10},{14,12},{16,14},{18,... | collective-permute-start | bytes 442376 | tf_op jit(solution)/shard_map/while/body/eval_jaxpr/ppermute | solution.py:117
  238.1 7.0 %collective-permute-start.3 = (bf16[24,3072]{1,0:T(8,128)(2,1)S(1)}, bf16[24,3072]{1,0:T(8,128)(2,1)S(1)}, u32[]{:S(2)}, u32[]{:S(2)}) collective-permute-start(bf16[24,3072]{1,0:T(8,128)(2,1)S(1)} %get-tuple-element.478), channel_id=1, source_target_pairs={{0,2},{2,4},{4,6},{6,8},{8,10},{10,12},{12,14},{14,16},{16,18},{18... | collective-permute-start | bytes 442376 | tf_op jit(solution)/shard_map/while/body/eval_jaxpr/ppermute | solution.py:117
  246.2 11.1 %collective-permute-start.30 = (bf16[24,3072]{1,0:T(8,128)(2,1)S(1)}, bf16[24,3072]{1,0:T(8,128)(2,1)S(1)}, u32[]{:S(2)}, u32[]{:S(2)}) collective-permute-start(bf16[24,3072]{1,0:T(8,128)(2,1)S(1)} %get-tuple-element.296), channel_id=1, source_target_pairs={{0,2},{2,4},{4,6},{6,8},{8,10},{10,12},{12,14},{14,16},{16,18},{18... | collective-permute-start | bytes 442376 | tf_op jit(solution)/shard_map/ppermute | solution.py:117
  246.3 10.9 %collective-permute-start.31 = (bf16[24,3072]{1,0:T(8,128)(2,1)S(1)}, bf16[24,3072]{1,0:T(8,128)(2,1)S(1)}, u32[]{:S(2)}, u32[]{:S(2)}) collective-permute-start(bf16[24,3072]{1,0:T(8,128)(2,1)S(1)} %get-tuple-element.297), channel_id=1, source_target_pairs={{0,62},{2,0},{4,2},{6,4},{8,6},{10,8},{12,10},{14,12},{16,14},{18,... | collective-permute-start | bytes 442376 | tf_op jit(solution)/shard_map/ppermute | solution.py:117
  258.3 16.6 %collective-permute-start.32 = (bf16[8,3072]{1,0:T(8,128)(2,1)S(1)}, bf16[8,3072]{1,0:T(8,128)(2,1)S(1)}, u32[]{:S(2)}, u32[]{:S(2)}) collective-permute-start(bf16[8,3072]{1,0:T(8,128)(2,1)S(1)} %get-tuple-element.332), channel_id=1, source_target_pairs={{0,42},{2,44},{4,46},{6,48},{8,50},{10,52},{12,54},{14,56},{16,58}... | collective-permute-start | bytes 147464 | tf_op jit(solution)/shard_map/ppermute | solution.py:117
  258.4 17.2 %collective-permute-start.33 = (bf16[8,3072]{1,0:T(8,128)(2,1)S(1)}, bf16[8,3072]{1,0:T(8,128)(2,1)S(1)}, u32[]{:S(2)}, u32[]{:S(2)}) collective-permute-start(bf16[8,3072]{1,0:T(8,128)(2,1)S(1)} %get-tuple-element.333), channel_id=1, source_target_pairs={{0,22},{2,24},{4,26},{6,28},{8,30},{10,32},{12,34},{14,36},{16,38}... | collective-permute-start | bytes 147464 | tf_op jit(solution)/shard_map/ppermute | solution.py:117
